TPU v7x, 256 devices: a whole 4x4x8 slice. The times are simulated.
256 devices in a mesh: seq: 32 (over z, x), head: 8 (over y, core).
Axes of the slice: x: 4, y: 4, z: 8, core: 2. Of those that a mesh axis runs over, the one named last changes fastest.
Arguments:
- token_values: bfloat16 [8192, 5120], P('seq', 'head'), may hold values from -6 to 6
- gate_values: bfloat16 [8192, 5120], P('seq', 'head'), may hold values from -30 to 30
- state_in: bfloat16 [8192, 128], P('seq'), may hold values from -0.5 to 0.5
- state_out: bfloat16 [8192, 128], P('seq'), may hold values from -6 to 6
- step_size: float32 [8192, 80], P('seq', 'head'), may hold values from 0.02 to 0.2
- log_decay: float32 [8192, 80], P('seq', 'head'), may hold values from -1 to 0
- level_weight: bfloat16 [8192, 80, 14], P('seq', 'head'), may hold values from 0.25 to 2
- skip_weight: float32 [80], P('head'), may hold values from 0.5 to 1.5
- norm_gain: float32 [5120], P('head'), may hold values from 0.1 to 1.9
- out_weight: bfloat16 [5120, 2560], P('head'), may hold values from -0.078125 to 0.078125
Outputs:
- layer_out: bfloat16 [8192, 2560], P(('seq', 'head'))
All inputs are finite; a program needn't handle non-finite values.
Results may differ from a plain program's by a relative error of at most 0.014.
Values may be sent and summed in bfloat16 or wider, within the bound.
No kernel may reach another device: no remote copies, remote signals or barrier semaphores. Data moves between devices by JAX's collectives and lax.ppermute only.
A program may use at most 64 MiB of HBM per device.

v0:
```python
import jax
import jax.numpy as jnp
from jax import lax
from jax.sharding import PartitionSpec as P

H = 80
P_SIZE = 64
N = 128
STRETCH_BITS = 6
STRETCH = 64


EPSILON = 1e-05


def partner_2(value, axis, distance):
    mask = 2**distance
    pairs = [(source, source ^ mask) for source in range(lax.axis_size(axis))]
    return lax.ppermute(value, axis, pairs)


def copy_for_each(value, axis):
    size = lax.axis_size(axis)
    return lax.all_to_all(
        jnp.broadcast_to(value[None], (size, *value.shape)), axis, 0, 0, tiled=True
    )


def of_everyone(value, axis):
    return copy_for_each(value, axis).sum(axis=0)


def cut_along(value, dim, size):
    before, after = (value.shape[:dim], value.shape[dim + 1 :])
    return jnp.moveaxis(value.reshape(*before, size, -1, *after), dim, 0)


def sum_at_owner(value, axis, dim):
    size = lax.axis_size(axis)
    tiles = lax.all_to_all(cut_along(value, dim, size), axis, 0, 0, tiled=True)
    return jnp.sum(tiles.astype(jnp.float32), axis=0)


def bit_count(values, bit_width):
    counted = jnp.zeros(values.shape, jnp.int32)
    for shift in range(bit_width):
        counted = counted + (values >= 1 << shift).astype(jnp.int32)
    return counted


def stretch_levels():
    inside = jnp.arange(STRETCH, dtype=jnp.int32)
    later = inside[:, None]
    earlier = inside[None, :]
    causal = earlier <= later
    levels = bit_count(jnp.bitwise_xor(later, earlier), STRETCH_BITS)
    onehot = (
        levels[:, :, None] == jnp.arange(STRETCH_BITS + 1, dtype=jnp.int32)[None, None, :]
    ) & causal[:, :, None]
    return (causal, onehot.astype(jnp.float32))


def on_device(
    token_values,
    gate_values,
    state_in,
    state_out,
    step_size,
    log_decay,
    level_weight,
    skip_weight,
    norm_gain,
    out_weight,
):
    rows = token_values.shape[0]
    heads = step_size.shape[1]
    blocks_here = rows // STRETCH
    local_bits = blocks_here.bit_length() - 1
    seq_bits = lax.axis_size("seq").bit_length() - 1
    causal, onehot = stretch_levels()
    values = token_values.astype(jnp.float32).reshape(blocks_here, STRETCH, heads, P_SIZE)
    inputs = values * step_size.reshape(blocks_here, STRETCH, heads)[:, :, :, None]
    within = jnp.cumsum(log_decay.reshape(blocks_here, STRETCH, heads), axis=1)
    totals = within[:, -1]
    weights = level_weight.astype(jnp.float32).reshape(blocks_here, STRETCH, heads, -1)
    query_narrow = state_out.reshape(blocks_here, STRETCH, N)
    key_narrow = state_in.reshape(blocks_here, STRETCH, N)
    scores = jnp.einsum(
        "ctn,csn->cts", query_narrow, key_narrow, preferred_element_type=jnp.float32
    )
    within_heads = jnp.transpose(within, (0, 2, 1))
    gaps = jnp.where(
        causal[None, None], within_heads[:, :, :, None] - within_heads[:, :, None, :], -jnp.inf
    )
    mixing = (
        jnp.einsum("cthl,tsl->chts", weights[:, :, :, : STRETCH_BITS + 1], onehot)
        * jnp.exp(gaps)
        * scores[:, None]
    )
    output = jnp.einsum("chts,cshp->cthp", mixing, inputs)
    to_end = jnp.exp(totals[:, None, :] - within)
    key_rows = state_in.astype(jnp.float32).reshape(blocks_here, STRETCH, N)
    query_rows = state_out.astype(jnp.float32).reshape(blocks_here, STRETCH, N)
    states = jnp.einsum("csn,cshp->chnp", key_rows, inputs * to_end[:, :, :, None])
    lift = jnp.exp(within)
    block_ids = jnp.arange(blocks_here, dtype=jnp.int32)
    blocks = states
    block_totals = totals
    for depth in range(1, local_bits + 1):
        size = 2 ** (depth - 1)
        grouped = totals.reshape(blocks_here // size, size, heads)
        before = (jnp.cumsum(grouped, axis=1) - grouped).reshape(blocks_here, heads)
        upper = (block_ids >> depth - 1 & 1).astype(jnp.float32)
        sibling = jnp.bitwise_xor(block_ids >> depth - 1, 1)
        carried = blocks[sibling] * (upper[:, None] * jnp.exp(before))[:, :, None, None]
        reached = jnp.einsum("ctn,chnp->cthp", query_rows, carried)
        output = (
            output + weights[:, :, :, STRETCH_BITS + depth, None] * lift[:, :, :, None] * reached
        )
        paired = blocks.reshape(-1, 2, heads, N, P_SIZE)
        pair_totals = block_totals.reshape(-1, 2, heads)
        blocks = jnp.exp(pair_totals[:, 1])[:, :, None, None] * paired[:, 0] + paired[:, 1]
        block_totals = pair_totals[:, 0] + pair_totals[:, 1]
    ahead = jnp.cumsum(totals, axis=0) - totals
    device_state = blocks[0]
    device_total = block_totals[0]
    element_index = lax.axis_index("seq")
    spanned = jnp.zeros((heads,), jnp.float32)
    level_states = []
    for depth in range(seq_bits):
        partner, partner_total = (
            partner_2(device_state.astype(jnp.bfloat16), "seq", depth).astype(device_state.dtype),
            partner_2(device_total.astype(jnp.bfloat16), "seq", depth).astype(device_total.dtype),
        )
        upper = (element_index >> depth & 1).astype(jnp.float32)
        level_states.append(upper * jnp.exp(spanned)[:, None, None] * partner)
        device_state = jnp.where(
            upper > 0,
            jnp.exp(device_total)[:, None, None] * partner + device_state,
            jnp.exp(partner_total)[:, None, None] * device_state + partner,
        )
        spanned = spanned + upper * partner_total
        device_total = device_total + partner_total
    remote_states = jnp.stack(level_states)
    remote = jnp.einsum("ctn,mhnp->cthmp", query_rows, remote_states)
    remote_lift = jnp.exp(within + ahead[:, None, :])
    far_weights = weights[:, :, :, STRETCH_BITS + local_bits + 1 :]
    output = output + remote_lift[:, :, :, None] * jnp.einsum(
        "cthmp,cthm->cthp", remote, far_weights
    )
    mixed = (output + skip_weight[:, None] * values).reshape(rows, heads * P_SIZE)
    gated = mixed * jax.nn.silu(gate_values.astype(jnp.float32))
    square = of_everyone(jnp.sum(gated * gated, axis=1), "head")
    features = (gated * lax.rsqrt(square / (H * P_SIZE) + EPSILON)[:, None] * norm_gain).astype(
        jnp.bfloat16
    )
    product = jnp.dot(features, out_weight, preferred_element_type=jnp.float32)
    rounded = lax.optimization_barrier(product.astype(jnp.bfloat16))
    summed = sum_at_owner(rounded.astype(jnp.float32).astype(jnp.bfloat16), "head", 0)
    return summed.astype(jnp.bfloat16)


def solution(mesh):
    placed = (
        P("seq", "head"),
        P("seq", "head"),
        P("seq", None),
        P("seq", None),
        P("seq", "head"),
        P("seq", "head"),
        P("seq", "head", None),
        P("head"),
        P("head"),
        P("head", None),
    )
    return jax.shard_map(
        on_device, mesh=mesh, in_specs=placed, out_specs=P(("seq", "head"), None), check_vma=False
    )
```

profile of v0, /device:TPU:1, one launch (start us, length us, event | category | flops | bytes accessed | tf_op | source)
XLA Modules:
  0.0 152.5 jit_solution(5111827308806731194)
XLA Ops:
  2.8 2.0 %collective-permute-start.1 = (bf16[10]{0:T(256)(128)(2,1)}, bf16[10]{0:T(256)(128)(2,1)}, u32[]{:S(2)}, u32[]{:S(2)}) collective-permute-start(bf16[10]{0:T(256)(128)(2,1)} %bitcast_convert_fusion), channel_id=1, source_target_pairs={{0,8},{8,0},{16,24},{24,16},{32,40},{40,32},{48,56},{56,48},{64,72... | collective-permute-start | bytes 68 | tf_op jit(solution)/shard_map/ppermute | solution.py:19
  8.3 2.0 %copy.75 = f32[256,640]{0,1:T(8,128)} copy(bf16[256,640]{1,0:T(8,128)(2,1)} %param.10) | data formatting | bytes 983040 | tf_op jit(solution)/shard_map/reshape | solution.py:81
  10.3 2.7 %reshape.326 = f32[4,64,10,64]{1,0,3,2:T(4,128)} reshape(f32[256,640]{0,1:T(8,128)} %copy.75) | data formatting | bytes 1310720 | tf_op jit(solution)/shard_map/reshape | solution.py:81
  13.0 2.6 %broadcast_multiply_fusion = (bf16[4,64,10,64]{1,0,3,2:T(4,128)(2,1)S(1)}, bf16[4,64,10,64]{1,0,3,2:T(4,128)(2,1)}) fusion(f32[4,64,10]{1,0,2:T(4,128)S(1)} %copy-done.12, f32[4,64,10,64]{1,0,3,2:T(4,128)} %reshape.326, f32[4,64,10]{1,0,2:T(4,128)S(1)} %copy-done.13), kind=kLoop, calls=%fused_computation.40 | loop fusion | flops 655360 | bytes 1331200 | tf_op jit(solution)/shard_map/mul | solution.py:104
  25.4 2.3 %bitcast_add_fusion.1 = f32[2,10,128,64]{2,3,1,0:T(8,128)} fusion(f32[2,2,10,128,64]{3,4,2,1,0:T(8,128)} %bitcast.157, f32[2,10]{1,0:T(2,128)} %bitcast.174), kind=kLoop, calls=%fused_computation.34 | loop fusion | flops 327680 | bytes 1966160 | tf_op jit(solution)/shard_map/add | solution.py:122
  42.7 2.2 %fusion.1 = bf16[4,10,64,64]{3,1,0,2:T(8,128)(2,1)S(1)} fusion(bf16[4,64,10,7]{2,3,0,1:T(8,128)(2,1)} %copy.111, f32[4,64,64]{2,0,1:T(4,128)} %copy.81, f32[4,10,64]{2,1,0:T(8,128)} %copy.80, f32[4,10,64]{1,0,2:T(4,128)} %copy.79, pred[64,64]{1,0:T(8,128)(4,1)S(1)} %copy-done.14, pred[64,64,7,1]{1,0,2,3:T(32,128)(4,1)S(1)} %fusion.44), kind=kOutput, calls=%fused_computation.6 | convolution fusion | flops 3112960 | bytes 482304 | tf_op jit(solution)/shard_map/cthl,tsl->chts/dot_general | solution.py:96
  46.6 2.9 %gather_fusion.1 = f32[4,10,128,64]{2,3,1,0:T(8,128)} fusion(f32[2,10,128,64]{2,3,1,0:T(8,128)} %bitcast_add_fusion.1, s32[1024]{0:T(1024)} %pad_clamp_fusion), kind=kCustom, calls=%fused_computation.1 | custom fusion | bytes 2621456 | tf_op jit(solution)/shard_map/gather | solution.py:115
  49.5 3.2 %gather_fusion = f32[4,10,128,64]{2,3,1,0:T(8,128)} fusion(f32[4,10,128,64]{2,3,1,0:T(8,128)} %bitcast.158, s32[1024]{0:T(1024)} %pad_clamp_fusion.1), kind=kCustom, calls=%fused_computation | custom fusion | bytes 2621456 | tf_op jit(solution)/shard_map/gather | solution.py:115
  52.7 2.2 %fusion.6 = f32[4,64,10,64]{1,3,2,0:T(8,128)S(1)} fusion(f32[4,64,10,64]{1,3,2,0:T(8,128)} %convolution_bitcast_fusion.2, bf16[4,64,128,1]{2,1,3,0:T(8,128)(2,1)S(1)} %bitcast.163, f32[4,10,128,64]{2,3,1,0:T(8,128)} %gather_fusion, f32[4,10]{1,0:T(4,128)S(1)} %broadcast_multiply_fusion.2, f32[4,64,10]{1,2,0:T(8,128)S(1)} %copy.85), kind=kOutput, calls=%fused_computation.13 | convolution fusion | flops 42598400 | bytes 2697376 | tf_op jit(solution)/shard_map/ctn,chnp->cthp/dot_general | solution.py:116
  55.5 3.0 %collective-permute-start.3 = (bf16[10]{0:T(256)(128)(2,1)S(1)}, bf16[10]{0:T(256)(128)(2,1)S(1)}, u32[]{:S(2)}, u32[]{:S(2)}) collective-permute-start(bf16[10]{0:T(256)(128)(2,1)S(1)} %fusion.59), channel_id=1, source_target_pairs={{0,16},{8,24},{16,0},{24,8},{32,48},{40,56},{48,32},{56,40},{64,80... | collective-permute-start | bytes 68 | tf_op jit(solution)/shard_map/ppermute | solution.py:19
  60.0 1.9 %collective-permute-start.5 = (bf16[10]{0:T(256)(128)(2,1)S(1)}, bf16[10]{0:T(256)(128)(2,1)S(1)}, u32[]{:S(2)}, u32[]{:S(2)}) collective-permute-start(bf16[10]{0:T(256)(128)(2,1)S(1)} %convert_element_type.165), channel_id=1, source_target_pairs={{0,32},{8,40},{16,48},{24,56},{32,0},{40,8},{48,16},{56,24},{64,96... | collective-permute-start | bytes 68 | tf_op jit(solution)/shard_map/ppermute | solution.py:19
  62.9 3.0 %collective-permute-start.7 = (bf16[10]{0:T(256)(128)(2,1)S(1)}, bf16[10]{0:T(256)(128)(2,1)S(1)}, u32[]{:S(2)}, u32[]{:S(2)}) collective-permute-start(bf16[10]{0:T(256)(128)(2,1)S(1)} %get-tuple-element.24), channel_id=1, source_target_pairs={{0,64},{8,72},{16,80},{24,88},{32,96},{40,104},{48,112},{56,120},{... | collective-permute-start | bytes 68 | tf_op jit(solution)/shard_map/ppermute | solution.py:19
  68.7 2.8 %collective-permute-start.2 = (bf16[10,128,64]{1,2,0:T(8,128)(2,1)S(1)}, bf16[10,128,64]{1,2,0:T(8,128)(2,1)S(1)}, u32[]{:S(2)}, u32[]{:S(2)}) collective-permute-start(bf16[10,128,64]{1,2,0:T(8,128)(2,1)S(1)} %get-tuple-element.9), channel_id=1, source_target_pairs={{0,16},{8,24},{16,0},{24,8},{32,48},{40,56},{48,32},{56,40},{64,80... | collective-permute-start | bytes 491528 | tf_op jit(solution)/shard_map/ppermute | solution.py:19
  72.4 2.0 %collective-permute-done.2 = bf16[10,128,64]{1,2,0:T(8,128)(2,1)S(1)} collective-permute-done((bf16[10,128,64]{1,2,0:T(8,128)(2,1)S(1)}, bf16[10,128,64]{1,2,0:T(8,128)(2,1)S(1)}, u32[]{:S(2)}, u32[]{:S(2)}) %collective-permute-start.2) | collective-permute-done | bytes 163872 | tf_op jit(solution)/shard_map/ppermute | solution.py:19
  76.2 2.9 %collective-permute-done.4 = bf16[10,128,64]{1,2,0:T(8,128)(2,1)S(1)} collective-permute-done((bf16[10,128,64]{1,2,0:T(8,128)(2,1)S(1)}, bf16[10,128,64]{1,2,0:T(8,128)(2,1)S(1)}, u32[]{:S(2)}, u32[]{:S(2)}) %collective-permute-start.4) | collective-permute-done | bytes 163872 | tf_op jit(solution)/shard_map/ppermute | solution.py:19
  79.4 2.4 %collective-permute-start.6 = (bf16[10,128,64]{1,2,0:T(8,128)(2,1)S(1)}, bf16[10,128,64]{1,2,0:T(8,128)(2,1)S(1)}, u32[]{:S(2)}, u32[]{:S(2)}) collective-permute-start(bf16[10,128,64]{1,2,0:T(8,128)(2,1)S(1)} %fusion.61), channel_id=1, source_target_pairs={{0,64},{8,72},{16,80},{24,88},{32,96},{40,104},{48,112},{56,120},{... | collective-permute-start | bytes 491528 | tf_op jit(solution)/shard_map/ppermute | solution.py:19
  82.0 4.4 %collective-permute-done.6 = bf16[10,128,64]{1,2,0:T(8,128)(2,1)S(1)} collective-permute-done((bf16[10,128,64]{1,2,0:T(8,128)(2,1)S(1)}, bf16[10,128,64]{1,2,0:T(8,128)(2,1)S(1)}, u32[]{:S(2)}, u32[]{:S(2)}) %collective-permute-start.6) | collective-permute-done | bytes 163872 | tf_op jit(solution)/shard_map/ppermute | solution.py:19
  86.7 6.3 %collective-permute-start.8 = (bf16[10,128,64]{1,2,0:T(8,128)(2,1)S(1)}, bf16[10,128,64]{1,2,0:T(8,128)(2,1)S(1)}, u32[]{:S(2)}, u32[]{:S(2)}) collective-permute-start(bf16[10,128,64]{1,2,0:T(8,128)(2,1)S(1)} %fusion.37), channel_id=1, source_target_pairs={{0,128},{8,136},{16,144},{24,152},{32,160},{40,168},{48,176},{56,1... | collective-permute-start | bytes 491528 | tf_op jit(solution)/shard_map/ppermute | solution.py:19
  93.1 2.8 %collective-permute-done.8 = bf16[10,128,64]{1,2,0:T(8,128)(2,1)S(1)} collective-permute-done((bf16[10,128,64]{1,2,0:T(8,128)(2,1)S(1)}, bf16[10,128,64]{1,2,0:T(8,128)(2,1)S(1)}, u32[]{:S(2)}, u32[]{:S(2)}) %collective-permute-start.8) | collective-permute-done | bytes 163872 | tf_op jit(solution)/shard_map/ppermute | solution.py:19
  100.3 2.9 %reshape.323 = f32[256,640]{0,1:T(8,128)} reshape(f32[4,64,10,64]{1,0,3,2:T(4,128)} %copy.93) | data formatting | bytes 1310720 | tf_op jit(solution)/shard_map/reshape | solution.py:151
  104.6 21.6 %all_to_all.11 = f32[8,1,256]{2,1,0:T(1,128)S(1)} all-to-all(f32[8,1,256]{2,1,0:T(1,128)S(1)} %broadcast_in_dim.16), channel_id=1, replica_groups=mesh['seq'=32,'head'=8] {'head'}, dimensions={0} | all-to-all | bytes 16384 | tf_op jit(solution)/shard_map/all_to_all | solution.py:24
  126.2 2.5 %convolution_convert_fusion = bf16[256,2560]{1,0:T(8,128)(2,1)S(1)} fusion(bf16[640,2560]{1,0:T(8,128)(2,1)S(1)} %copy-done, f32[640]{0:T(1024)S(1)} %copy-done.23, f32[256]{0:T(256)S(1)} %add_rsqrt_fusion, f32[256,640]{0,1:T(8,128)} %reshape.323, bf16[256,640]{0,1:T(8,128)(2,1)} %copy.94), kind=kOutput, calls=%fused_computation.4 | convolution fusion | flops 840990720 | bytes 5574144 | tf_op jit(solution)/shard_map/dot_general | solution.py:157
  128.7 21.6 %all_to_all.12 = bf16[8,32,2560]{2,1,0:T(8,128)(2,1)} all-to-all(bf16[8,32,2560]{2,1,0:T(8,128)(2,1)S(1)} %bitcast.161), channel_id=1, replica_groups=mesh['seq'=32,'head'=8] {'head'}, dimensions={0} | all-to-all | bytes 2621440 | tf_op jit(solution)/shard_map/all_to_all | solution.py:40
  150.3 2.2 %reduce_sum.32 = bf16[32,2560]{1,0:T(8,128)(2,1)} reduce(bf16[8,32,2560]{2,1,0:T(8,128)(2,1)} %all_to_all.12, bf16[]{:T(256)} %constant.54.clone.1), dimensions={0}, to_apply=%region_5.6 | reduce | flops 573440 | bytes 1474562 | tf_op jit(solution)/shard_map/reduce_sum | solution.py:41
  (119 shorter events, 47.7 us)
Async XLA Ops:
  0.0 126.2 %copy-start = (bf16[640,2560]{1,0:T(8,128)(2,1)S(1)}, bf16[640,2560]{1,0:T(8,128)(2,1)}, u32[]{:S(2)}) copy-start(bf16[640,2560]{1,0:T(8,128)(2,1)} %param.19) | copy-start | bytes 9830404
  1.7 14.2 %copy-start.15 = (f32[2,1,10]{2,1,0:T(1,128)}, f32[2,1,10]{2,1,0:T(1,128)S(1)}, u32[]{:S(2)}) copy-start(f32[2,1,10]{2,1,0:T(1,128)S(1)} %get-tuple-element.22) | copy-start | bytes 244
  2.8 52.1 %collective-permute-start.1 = (bf16[10]{0:T(256)(128)(2,1)}, bf16[10]{0:T(256)(128)(2,1)}, u32[]{:S(2)}, u32[]{:S(2)}) collective-permute-start(bf16[10]{0:T(256)(128)(2,1)} %bitcast_convert_fusion), channel_id=1, source_target_pairs={{0,8},{8,0},{16,24},{24,16},{32,40},{40,32},{48,56},{56,48},{64,72... | collective-permute-start | bytes 68 | tf_op jit(solution)/shard_map/ppermute | solution.py:19
  8.3 4.7 %copy-start.12 = (f32[4,64,10]{1,0,2:T(4,128)S(1)}, f32[4,64,10]{1,0,2:T(4,128)}, u32[]{:S(2)}) copy-start(f32[4,64,10]{1,0,2:T(4,128)} %copy.86) | copy-start | bytes 30724
  8.3 4.7 %copy-start.13 = (f32[4,64,10]{1,0,2:T(4,128)S(1)}, f32[4,64,10]{1,0,2:T(4,128)}, u32[]{:S(2)}) copy-start(f32[4,64,10]{1,0,2:T(4,128)} %mul.312) | copy-start | bytes 30724
  13.0 2.6 %copy-start.10 = (bf16[256,128]{1,0:T(8,128)(2,1)S(1)}, bf16[256,128]{1,0:T(8,128)(2,1)}, u32[]{:S(2)}) copy-start(bf16[256,128]{1,0:T(8,128)(2,1)} %param.12) | copy-start | bytes 196612
  17.5 50.0 %collective-permute-start = (bf16[10,128,64]{1,2,0:T(8,128)(2,1)}, bf16[10,128,64]{1,2,0:T(8,128)(2,1)}, u32[]{:S(2)}, u32[]{:S(2)}) collective-permute-start(bf16[10,128,64]{1,2,0:T(8,128)(2,1)} %fusion.53), channel_id=1, source_target_pairs={{0,8},{8,0},{16,24},{24,16},{32,40},{40,32},{48,56},{56,48},{64,72... | collective-permute-start | bytes 491528 | tf_op jit(solution)/shard_map/ppermute | solution.py:19
  24.0 3.6 %copy-start.7 = (bf16[4,64,10,14]{1,0,3,2:T(4,128)(2,1)}, bf16[4,64,10,14]{1,0,3,2:T(4,128)(2,1)S(1)}, u32[]{:S(2)}) copy-start(bf16[4,64,10,14]{1,0,3,2:T(4,128)(2,1)S(1)} %reshape.317) | copy-start | bytes 215044
  27.7 7.8 %slice-start = ((bf16[4,64,10,14]{1,0,3,2:T(4,128)(2,1)}), bf16[4,64,10,7]{1,0,3,2:T(4,128)(2,1)S(1)}, s32[]{:S(2)}) async-start(bf16[4,64,10,14]{1,0,3,2:T(4,128)(2,1)} %copy-done.7), calls=%async_computation.2 | async-start | bytes 143360 | tf_op jit(solution)/shard_map/slice | solution.py:96
  37.1 3.2 %copy-start.14 = (pred[64,64]{1,0:T(8,128)(4,1)S(1)}, pred[64,64]{1,0:T(8,128)(4,1)}, u32[]{:S(2)}) copy-start(pred[64,64]{1,0:T(8,128)(4,1)} %iota_compare_fusion.1) | copy-start | bytes 12292
  37.1 4.0 %copy-start.16 = (f32[4,1,10]{2,1,0:T(1,128)S(1)}, f32[4,1,10]{2,1,0:T(1,128)}, u32[]{:S(2)}) copy-start(f32[4,1,10]{2,1,0:T(1,128)} %get-tuple-element.19) | copy-start | bytes 484
  49.5 3.2 %copy-start.9 = (bf16[256,128]{1,0:T(8,128)(2,1)S(1)}, bf16[256,128]{1,0:T(8,128)(2,1)}, u32[]{:S(2)}) copy-start(bf16[256,128]{1,0:T(8,128)(2,1)} %param.13) | copy-start | bytes 196612
  52.7 14.8 %copy-start.5 = (f32[1,2,10,128,64]{3,4,2,1,0:T(8,128)S(1)}, f32[1,2,10,128,64]{3,4,2,1,0:T(8,128)}, u32[]{:S(2)}) copy-start(f32[1,2,10,128,64]{3,4,2,1,0:T(8,128)} %copy-done.4) | copy-start | bytes 1966084
  52.7 14.8 %copy-start.17 = (f32[10]{0:T(128)S(1)}, f32[10]{0:T(128)}, u32[]{:S(2)}) copy-start(f32[10]{0:T(128)} %get-tuple-element.11) | copy-start | bytes 124
  52.7 14.8 %copy-start.19 = (f32[10]{0:T(128)S(1)}, f32[10]{0:T(128)}, u32[]{:S(2)}) copy-start(f32[10]{0:T(128)} %exponential_bitcast_fusion) | copy-start | bytes 124
  55.5 3.9 %collective-permute-start.3 = (bf16[10]{0:T(256)(128)(2,1)S(1)}, bf16[10]{0:T(256)(128)(2,1)S(1)}, u32[]{:S(2)}, u32[]{:S(2)}) collective-permute-start(bf16[10]{0:T(256)(128)(2,1)S(1)} %fusion.59), channel_id=1, source_target_pairs={{0,16},{8,24},{16,0},{24,8},{32,48},{40,56},{48,32},{56,40},{64,80... | collective-permute-start | bytes 68 | tf_op jit(solution)/shard_map/ppermute | solution.py:19
  60.0 2.9 %collective-permute-start.5 = (bf16[10]{0:T(256)(128)(2,1)S(1)}, bf16[10]{0:T(256)(128)(2,1)S(1)}, u32[]{:S(2)}, u32[]{:S(2)}) collective-permute-start(bf16[10]{0:T(256)(128)(2,1)S(1)} %convert_element_type.165), channel_id=1, source_target_pairs={{0,32},{8,40},{16,48},{24,56},{32,0},{40,8},{48,16},{56,24},{64,96... | collective-permute-start | bytes 68 | tf_op jit(solution)/shard_map/ppermute | solution.py:19
  62.9 3.9 %collective-permute-start.7 = (bf16[10]{0:T(256)(128)(2,1)S(1)}, bf16[10]{0:T(256)(128)(2,1)S(1)}, u32[]{:S(2)}, u32[]{:S(2)}) collective-permute-start(bf16[10]{0:T(256)(128)(2,1)S(1)} %get-tuple-element.24), channel_id=1, source_target_pairs={{0,64},{8,72},{16,80},{24,88},{32,96},{40,104},{48,112},{56,120},{... | collective-permute-start | bytes 68 | tf_op jit(solution)/shard_map/ppermute | solution.py:19
  68.7 5.8 %collective-permute-start.2 = (bf16[10,128,64]{1,2,0:T(8,128)(2,1)S(1)}, bf16[10,128,64]{1,2,0:T(8,128)(2,1)S(1)}, u32[]{:S(2)}, u32[]{:S(2)}) collective-permute-start(bf16[10,128,64]{1,2,0:T(8,128)(2,1)S(1)} %get-tuple-element.9), channel_id=1, source_target_pairs={{0,16},{8,24},{16,0},{24,8},{32,48},{40,56},{48,32},{56,40},{64,80... | collective-permute-start | bytes 491528 | tf_op jit(solution)/shard_map/ppermute | solution.py:19
  74.6 4.6 %collective-permute-start.4 = (bf16[10,128,64]{1,2,0:T(8,128)(2,1)S(1)}, bf16[10,128,64]{1,2,0:T(8,128)(2,1)S(1)}, u32[]{:S(2)}, u32[]{:S(2)}) collective-permute-start(bf16[10,128,64]{1,2,0:T(8,128)(2,1)S(1)} %fusion.63), channel_id=1, source_target_pairs={{0,32},{8,40},{16,48},{24,56},{32,0},{40,8},{48,16},{56,24},{64,96... | collective-permute-start | bytes 491528 | tf_op jit(solution)/shard_map/ppermute | solution.py:19
  79.4 16.7 %copy-start.8 = (bf16[4,64,10,14]{1,0,3,2:T(4,128)(2,1)S(1)}, bf16[4,64,10,14]{1,0,3,2:T(4,128)(2,1)}, u32[]{:S(2)}) copy-start(bf16[4,64,10,14]{1,0,3,2:T(4,128)(2,1)} %copy-done.7) | copy-start | bytes 215044
  79.4 7.0 %collective-permute-start.6 = (bf16[10,128,64]{1,2,0:T(8,128)(2,1)S(1)}, bf16[10,128,64]{1,2,0:T(8,128)(2,1)S(1)}, u32[]{:S(2)}, u32[]{:S(2)}) collective-permute-start(bf16[10,128,64]{1,2,0:T(8,128)(2,1)S(1)} %fusion.61), channel_id=1, source_target_pairs={{0,64},{8,72},{16,80},{24,88},{32,96},{40,104},{48,112},{56,120},{... | collective-permute-start | bytes 491528 | tf_op jit(solution)/shard_map/ppermute | solution.py:19
  86.7 9.2 %collective-permute-start.8 = (bf16[10,128,64]{1,2,0:T(8,128)(2,1)S(1)}, bf16[10,128,64]{1,2,0:T(8,128)(2,1)S(1)}, u32[]{:S(2)}, u32[]{:S(2)}) collective-permute-start(bf16[10,128,64]{1,2,0:T(8,128)(2,1)S(1)} %fusion.37), channel_id=1, source_target_pairs={{0,128},{8,136},{16,144},{24,152},{32,160},{40,168},{48,176},{56,1... | collective-permute-start | bytes 491528 | tf_op jit(solution)/shard_map/ppermute | solution.py:19
  100.3 26.0 %copy-start.23 = (f32[640]{0:T(1024)S(1)}, f32[640]{0:T(1024)}, u32[]{:S(2)}) copy-start(f32[640]{0:T(1024)} %param.18) | copy-start | bytes 7684
  (10 other events, 14.6 us)
where the time goes:
time: 153 us; the launch traced here: 152 us
  blocking collectives  43.1 us (28%)
  local copies, waits for them, and re-layouts  31.3 us (20%)
  other arithmetic  28 us (18%)
  starting transfers between devices  23.1 us (15%)
  waiting for transfers between devices  15 us (10%)
  matrix products  11.6 us (8%)
    ppermute x9, starting transfers between devices, partner_2(): return lax.ppermute(value, axis, pairs)  23.1 us
    all_to_all x1, blocking collectives, copy_for_each(): lax.all_to_all(jnp.broadcast_to(value[None], (size, *value.shape)), axis,...  21.6 us
    all_to_all x1, blocking collectives, sum_at_owner(): tiles = lax.all_to_all(cut_along(value, dim, size), axis, 0, 0, tiled=True)  21.6 us
    ppermute x9, waiting for transfers between devices, partner_2(): return lax.ppermute(value, axis, pairs)  15 us
    gather x2, local copies, waits for them, and re-layouts, on_device(): blocks[sibling] * (upper[:, None] * jnp.exp(before))[:, :, None, None]  6.1 us
    reshape x2, local copies, waits for them, and re-layouts, on_device(): token_values.astype(jnp.float32)  4.72 us
    unnamed x50, local copies, waits for them, and re-layouts  4.7 us
  transfers between devices with their start and end apart: 9, of which 7 were waited for; matrix products, arithmetic and copies ran while one was open for 34% of the time, Pallas kernels for 0%

commit v1 on v0

v1 whole, which is shorter than its diff:
```python
import jax
import jax.numpy as jnp
from jax import lax
from jax.experimental import pallas as pl
from jax.experimental.pallas import tpu as pltpu
from jax.sharding import PartitionSpec as P

H = 80
HEADS = 10
P_SIZE = 64
N = 128
TOK = 256
WIDTH = HEADS * P_SIZE
DM = 2560
WIDE = DM + 128
LOCAL_LEVELS = 9
PAY = WIDTH + 32

EPSILON = 1e-05

F32 = jnp.float32
BF16 = jnp.bfloat16


def dot(a, b):
    return jnp.dot(a, b, preferred_element_type=F32)


def split_two(value):
    high = value.astype(BF16)
    return high, (value - high.astype(F32)).astype(BF16)


def pad_heads(value):
    return jnp.concatenate([value, jnp.zeros((16 - HEADS, value.shape[1]), F32)], axis=0)


def state_kernel(x_ref, k_ref, step_ref, decay_ref, pay_ref, state_ref, xt_ref, cum_ref, tot_ref):
    decay = pad_heads(decay_ref[...])
    step = pad_heads(step_ref[...])
    high = decay.astype(BF16)
    rest = decay - high.astype(F32)
    mid, low = split_two(rest)
    earlier = lax.broadcasted_iota(jnp.int32, (TOK, TOK), 0)
    later = lax.broadcasted_iota(jnp.int32, (TOK, TOK), 1)
    upto = jnp.where(earlier <= later, 1.0, 0.0).astype(BF16)
    parts = dot(jnp.concatenate([high, mid, low], axis=0), upto)
    cum = parts[0:16] + parts[16:32] + parts[32:48]
    total = jnp.broadcast_to(cum[:, TOK - 1 : TOK], (16, 128))
    cum_ref[...] = cum
    tot_ref[...] = total
    high, low = split_two(total)
    pay_ref[WIDTH : WIDTH + 16, :] = high
    pay_ref[WIDTH + 16 : WIDTH + 32, :] = low
    coef = step * jnp.exp(cum[:, TOK - 1 : TOK] - cum)
    keys = k_ref[...]
    for j in range(WIDTH // 128):
        rows = slice(j * 128, (j + 1) * 128)
        xt = x_ref[:, rows].astype(F32).T
        xt_ref[rows, :] = xt.astype(BF16)
        scaled = jnp.concatenate(
            [xt[0:64] * coef[2 * j : 2 * j + 1], xt[64:128] * coef[2 * j + 1 : 2 * j + 2]], axis=0
        )
        state = dot(scaled.astype(BF16), keys)
        state_ref[rows, :] = state
        pay_ref[rows, :] = state.astype(BF16)


def local_kernel(xt_ref, k_ref, q_ref, step_ref, cum_ref, w_ref, skip_ref, out_ref, qt_ref):
    qt = q_ref[...].astype(F32).T.astype(BF16)
    qt_ref[...] = qt
    scores = dot(k_ref[...], qt)
    cum = cum_ref[...]
    cols = cum.T
    early = lax.broadcasted_iota(jnp.int32, (128, 128), 0)
    late = lax.broadcasted_iota(jnp.int32, (128, 128), 1)
    differ = jnp.bitwise_xor(early, late)
    level = jnp.zeros((128, 128), jnp.int32)
    for shift in range(7):
        level = level + (differ >= 1 << shift).astype(jnp.int32)
    level = jnp.where(early <= late, level, -1)
    for h in range(HEADS):
        weights = w_ref[h, 0:LOCAL_LEVELS, :].astype(F32)
        xt = xt_ref[h * 64 : (h + 1) * 64, :].astype(F32)
        inputs = (xt * step_ref[h : h + 1, :]).astype(BF16)

        def faded(i, j):
            s, t = slice(i * 128, (i + 1) * 128), slice(j * 128, (j + 1) * 128)
            gap = jnp.minimum(cum[h : h + 1, t] - cols[s, h : h + 1], 0.0)
            return jnp.exp(gap) * scores[s, t]

        def diagonal(i):
            t = slice(i * 128, (i + 1) * 128)
            picked = jnp.zeros((128, 128), F32)
            for l in range(LOCAL_LEVELS - 1):
                picked = jnp.where(level == l, weights[l : l + 1, t], picked)
            return (faded(i, i) * picked).astype(BF16)

        first = diagonal(0)
        second = jnp.concatenate(
            [(faded(0, 1) * weights[8:9, 128:256]).astype(BF16), diagonal(1)], axis=0
        )
        mixed = jnp.concatenate([dot(inputs[:, 0:128], first), dot(inputs, second)], axis=1)
        out_ref[h * 64 : (h + 1) * 64, :] = mixed + skip_ref[h] * xt


def combine_kernel(bit, state_ref, tot_ref, span_ref, recv_ref, pay_ref, new_ref, ntot_ref, nspan_ref):
    upper = ((lax.axis_index("seq") >> bit) & 1) > 0
    total = tot_ref[...]
    other = recv_ref[WIDTH : WIDTH + 16, :].astype(F32) + recv_ref[WIDTH + 16 : WIDTH + 32, :].astype(F32)
    new_total = total + other
    ntot_ref[...] = new_total
    nspan_ref[...] = span_ref[...] + jnp.where(upper, other, 0.0)
    high, low = split_two(new_total)
    pay_ref[WIDTH : WIDTH + 16, :] = high
    pay_ref[WIDTH + 16 : WIDTH + 32, :] = low
    for_other = jnp.where(upper, jnp.exp(total), 1.0)
    for_mine = jnp.where(upper, 1.0, jnp.exp(other))
    for h in range(HEADS):
        rows = slice(h * 64, (h + 1) * 64)
        new = for_other[h : h + 1] * recv_ref[rows, :].astype(F32) + for_mine[h : h + 1] * state_ref[rows, :]
        new_ref[rows, :] = new
        pay_ref[rows, :] = new.astype(BF16)


def far_term(recv_ref, qt, h, coef):
    rows = slice(h * 64, (h + 1) * 64)
    return dot(recv_ref[rows, :], qt) * coef


def far_coef(bit, cum, span_ref, w_ref, h):
    upper = ((lax.axis_index("seq") >> bit) & 1) > 0
    lift = jnp.exp(cum[h : h + 1, :] + span_ref[h : h + 1, 0:1])
    weight = w_ref[h, LOCAL_LEVELS + bit : LOCAL_LEVELS + bit + 1, :].astype(F32)
    return jnp.where(upper, lift * weight, 0.0)


def near_kernel(local_ref, r0, r1, r2, r3, s0, s1, s2, s3, qt_ref, cum_ref, w_ref, out_ref):
    qt = qt_ref[...]
    cum = cum_ref[...]
    for h in range(HEADS):
        rows = slice(h * 64, (h + 1) * 64)
        total = local_ref[rows, :]
        for bit, (recv, span) in enumerate(((r0, s0), (r1, s1), (r2, s2), (r3, s3))):
            total = total + far_term(recv, qt, h, far_coef(bit, cum, span, w_ref, h))
        out_ref[rows, :] = total


def project_kernel(
    near_ref, recv_ref, span_ref, qt_ref, cum_ref, w_ref, gate_ref, gain_ref, ow_ref,
    mine_ref, theirs_ref, feat_ref, square_ref,
):
    qt = qt_ref[...]
    cum = cum_ref[...]
    squares = jnp.zeros((TOK, 1), F32)
    for j in range(WIDTH // 128):
        cols = slice(j * 128, (j + 1) * 128)
        far = jnp.concatenate(
            [far_term(recv_ref, qt, h, far_coef(4, cum, span_ref, w_ref, h)) for h in (2 * j, 2 * j + 1)],
            axis=0,
        )
        mixed = (near_ref[cols, :] + far).T
        gate = gate_ref[:, cols].astype(F32)
        gated = mixed * (gate / (1.0 + jnp.exp(-gate)))
        squares = squares + jnp.sum(gated * gated, axis=1, keepdims=True)
        feat_ref[:, cols] = (gated * gain_ref[:, cols]).astype(BF16)
    square_ref[...] = jnp.broadcast_to(squares, (TOK, 128))
    core = lax.axis_index("head") & 1
    lane = lax.broadcasted_iota(jnp.int32, (32, 128), 1)
    for out_ref, side in ((theirs_ref, 1 - core), (mine_ref, core)):
        starts = [pl.multiple_of((2 * y + side) * 32, 32) for y in range(4)]
        rows = jnp.concatenate([feat_ref[pl.ds(s, 32), :] for s in starts], axis=0)
        out_ref[:, 0:DM] = dot(rows, ow_ref[...]).astype(BF16)
        for y, s in enumerate(starts):
            high, low = split_two(square_ref[pl.ds(s, 32), :])
            out_ref[y * 32 : (y + 1) * 32, DM:WIDE] = jnp.where(
                lane < 64, high.astype(F32), low.astype(F32)
            ).astype(BF16)


def squares_of(ref, rows):
    return ref[rows, DM : DM + 1].astype(F32) + ref[rows, DM + 64 : DM + 65].astype(F32)


def pair_kernel(mine_ref, recv_ref, own_ref, o1, o2, o3):
    y = lax.axis_index("head") >> 1
    lane = lax.broadcasted_iota(jnp.int32, (32, 128), 1)
    for k, out_ref in enumerate((own_ref, o1, o2, o3)):
        rows = pl.ds(pl.multiple_of(jnp.bitwise_xor(y, k) * 32, 32), 32)
        total = mine_ref[rows, 0:DM].astype(F32) + recv_ref[rows, 0:DM].astype(F32)
        out_ref[:, 0:DM] = total.astype(out_ref.dtype)
        square = jnp.broadcast_to(squares_of(mine_ref, rows) + squares_of(recv_ref, rows), (32, 128))
        high, low = split_two(square)
        out_ref[:, DM:WIDE] = jnp.where(lane < 64, high.astype(F32), low.astype(F32)).astype(out_ref.dtype)


def final_kernel(own_ref, r1, r2, r3, out_ref):
    every = slice(0, 32)
    square = squares_of(own_ref, every) + squares_of(r1, every) + squares_of(r2, every) + squares_of(r3, every)
    scale = lax.rsqrt(square * (1.0 / (H * P_SIZE)) + EPSILON)
    total = own_ref[:, 0:DM].astype(F32)
    for ref in (r1, r2, r3):
        total = total + ref[:, 0:DM].astype(F32)
    out_ref[...] = (total * scale).astype(BF16)


def call(kernel, outs, *args, scratch=(), flops=0, name=None, smem=()):
    specs = [
        pl.BlockSpec(memory_space=pltpu.SMEM if i in smem else pltpu.VMEM) for i in range(len(args))
    ]
    shapes = [jax.ShapeDtypeStruct(shape, dtype) for shape, dtype in outs]
    outputs = pl.pallas_call(
        kernel,
        out_shape=shapes,
        in_specs=specs,
        out_specs=[pl.BlockSpec(memory_space=pltpu.VMEM) for _ in outs],
        scratch_shapes=list(scratch),
        compiler_params=pltpu.CompilerParams(vmem_limit_bytes=48 << 20),
        cost_estimate=pl.CostEstimate(flops=flops, transcendentals=0, bytes_accessed=flops // 100),
        name=name,
    )(*args)
    return outputs


SENDS = (
    [(d, d ^ 1) for d in range(32)],
    [(d, d ^ 3) for d in range(32)],
    [(d, d ^ 4) for d in range(32)],
    [(d, d ^ 8) for d in range(32)],
    [(d, d ^ 28) for d in range(16)],
)


def on_device(token_values, gate_values, state_in, state_out, step_size, log_decay, level_weight, skip_weight, norm_gain, out_weight):
    step = jnp.transpose(step_size)
    decay = jnp.transpose(log_decay)
    weight = jnp.transpose(level_weight, (1, 2, 0))
    pay, state, xt, cum, total = call(
        state_kernel,
        [((PAY, N), BF16), ((WIDTH, N), F32), ((WIDTH, TOK), BF16), ((16, TOK), F32), ((16, 128), F32)],
        token_values, state_in, step, decay, flops=10**8, name="state",
    )
    local, qt = call(
        local_kernel,
        [((WIDTH, TOK), F32), ((N, TOK), BF16)],
        xt, state_in, state_out, step, cum, weight, skip_weight,
        flops=5 * 10**9, name="local", smem=(6,),
    )
    span = jnp.zeros((16, 128), F32)
    recvs, spans = [], []
    for bit in range(5):
        recv = lax.ppermute(pay, "seq", SENDS[bit])
        recvs.append(recv)
        spans.append(span)
        if bit < 4:
            pay, state, total, span = call(
                lambda *refs, bit=bit: combine_kernel(bit, *refs),
                [((PAY, N), BF16), ((WIDTH, N), F32), ((16, 128), F32), ((16, 128), F32)],
                state, total, span, recv, flops=10**6, name="combine",
            )
    (near,) = call(
        near_kernel, [((WIDTH, TOK), F32)], local, *recvs[:4], *spans[:4], qt, cum, weight,
        flops=2 * 10**9, name="near",
    )
    mine, theirs = call(
        project_kernel,
        [((128, WIDE), BF16), ((128, WIDE), BF16)],
        near, recvs[4], spans[4], qt, cum, weight, gate_values, norm_gain[None, :], out_weight,
        scratch=[pltpu.VMEM((TOK, WIDTH), BF16), pltpu.VMEM((TOK, 128), F32)],
        flops=10**9, name="project",
    )
    recv = lax.ppermute(theirs, "head", [(g, g ^ 1) for g in range(8)])
    own, *sends = call(
        pair_kernel,
        [((32, WIDE), F32)] + [((32, WIDE), BF16)] * 3,
        mine, recv, flops=10**6, name="pair",
    )
    got = [lax.ppermute(sends[k - 1], "head", [(g, g ^ (2 * k)) for g in range(8)]) for k in (1, 2, 3)]
    (out,) = call(final_kernel, [((32, DM), BF16)], own, *got, flops=10**6, name="final")
    return out


def solution(mesh):
    placed = (
        P("seq", "head"),
        P("seq", "head"),
        P("seq", None),
        P("seq", None),
        P("seq", "head"),
        P("seq", "head"),
        P("seq", "head", None),
        P("head"),
        P("head"),
        P("head", None),
    )
    return jax.shard_map(
        on_device, mesh=mesh, in_specs=placed, out_specs=P(("seq", "head"), None), check_vma=False
    )
```

time: 153 us -> 65.2 us (0.43)
  blocking collectives: 43.1 us -> 0 us
  other arithmetic: 28 us -> 0 us
  local copies, waits for them, and re-layouts: 31.3 us -> 7.21 us
  matrix products: 11.6 us -> 0 us
  waiting for transfers between devices: 15 us -> 24.3 us
  Pallas kernels: 0 us -> 6.94 us
  starting transfers between devices: 23.1 us -> 26.1 us
    all_to_all x2 -> x0, blocking collectives: 43.1 us -> none  [the longest x1 21.6 us: copy_for_each(): lax.all_to_all(jnp.broadcast_to(value[None], (size, *value.shape)), axis,...]
    dot_general x8 -> x0, matrix products: 11.6 us -> none  [the longest x2 2.73 us: on_device(): reached = jnp.einsum('ctn,chnp->cthp', query_rows, carried)]
    reshape x6 -> x0, local copies, waits for them, and re-layouts: 11 us -> none  [the longest x2 4.72 us: on_device(): token_values.astype(jnp.float32)]
    ppermute x9, waiting for transfers between devices: 15 us -> 24.3 us  [the longest x5 12 us: on_device(): recv = lax.ppermute(pay, 'seq', SENDS[bit])]
    pallas_call x0 -> x10, Pallas kernels: none -> 6.94 us  [call(): pl.pallas_call(kernel, out_shape=shapes, in_specs=specs, out_specs=[pl.Bl...]
    gather x2 -> x0, local copies, waits for them, and re-layouts: 6.1 us -> none  [on_device(): blocks[sibling] * (upper[:, None] * jnp.exp(before))[:, :, None, None]]
    mul x6 -> x0, other arithmetic: 5.36 us -> none  [the longest x1 2.58 us: on_device(): inputs * to_end[:, :, :, None]]
    convert_element_type x10 -> x0, other arithmetic: 4.9 us -> none  [the longest x5 2.71 us: on_device(): device_state.astype(jnp.bfloat16)]
  transfers between devices with their start and end apart: 9 -> 9, of which waited for: 7 -> 8; matrix products, arithmetic and copies ran while one was open for 34% -> 0% of each run, Pallas kernels for 0% -> 4%
where the time goes in v1:
time: 65.2 us; the launch traced here: 64.7 us
  starting transfers between devices  26.1 us (40%)
  waiting for transfers between devices  24.3 us (37%)
  local copies, waits for them, and re-layouts  7.21 us (11%)
  Pallas kernels  6.94 us (11%)
    ppermute x5, starting transfers between devices, on_device(): recv = lax.ppermute(pay, 'seq', SENDS[bit])  16.4 us
    ppermute x5, waiting for transfers between devices, on_device(): recv = lax.ppermute(pay, 'seq', SENDS[bit])  12 us
    ppermute x3, waiting for transfers between devices, on_device(): lax.ppermute(sends[k - 1], 'head', [(g, g ^ 2 * k) for g in range(8)])  10.5 us
    unnamed x26, local copies, waits for them, and re-layouts  7.2 us
    pallas_call x10, Pallas kernels, call(): pl.pallas_call(kernel, out_shape=shapes, in_specs=specs, out_specs=[pl.Bl...  6.94 us
    ppermute x1, starting transfers between devices, on_device(): recv = lax.ppermute(theirs, 'head', [(g, g ^ 1) for g in range(8)])  5.78 us
    ppermute x3, starting transfers between devices, on_device(): lax.ppermute(sends[k - 1], 'head', [(g, g ^ 2 * k) for g in range(8)])  3.97 us
    ppermute x1, waiting for transfers between devices, on_device(): recv = lax.ppermute(theirs, 'head', [(g, g ^ 1) for g in range(8)])  1.77 us
  transfers between devices with their start and end apart: 9, of which 8 were waited for; matrix products, arithmetic and copies ran while one was open for 0% of the time, Pallas kernels for 4%

profile of v1, /device:TPU:1, one launch (start us, length us, event | category | flops | bytes accessed | tf_op | source)
XLA Modules:
  0.0 64.7 jit_solution(11787474972503328287)
XLA Ops:
  0.0 1.0 %copy-done.2 = bf16[256,640]{1,0:T(8,128)(2,1)S(1)} copy-done((bf16[256,640]{1,0:T(8,128)(2,1)S(1)}, bf16[256,640]{1,0:T(8,128)(2,1)}, u32[]{:S(2)}) %copy-start.2) | copy-done | bytes 327704
  1.0 0.8 %copy-done.5 = bf16[256,128]{1,0:T(8,128)(2,1)S(1)} copy-done((bf16[256,128]{1,0:T(8,128)(2,1)S(1)}, bf16[256,128]{1,0:T(8,128)(2,1)}, u32[]{:S(2)}) %copy-start.5) | copy-done | bytes 65560
  3.7 2.1 %collective-permute-start = (bf16[672,128]{1,0:T(8,128)(2,1)S(1)}, bf16[672,128]{1,0:T(8,128)(2,1)S(1)}, u32[]{:S(2)}, u32[]{:S(2)}) collective-permute-start(bf16[672,128]{1,0:T(8,128)(2,1)S(1)} %get-tuple-element.35), channel_id=1, source_target_pairs={{0,8},{8,0},{16,24},{24,16},{32,40},{40,32},{48,56},{56,48},{64,72... | collective-permute-start | bytes 516104 | tf_op jit(solution)/shard_map/ppermute | solution.py:252
  5.9 2.8 %collective-permute-done.refs_3_.r0 = bf16[672,128]{1,0:T(8,128)(2,1)S(1)} collective-permute-done((bf16[672,128]{1,0:T(8,128)(2,1)S(1)}, bf16[672,128]{1,0:T(8,128)(2,1)S(1)}, u32[]{:S(2)}, u32[]{:S(2)}) %collective-permute-start) | collective-permute-done | bytes 172064 | tf_op jit(solution)/shard_map/ppermute | solution.py:252
  8.8 3.8 %collective-permute-start.1 = (bf16[672,128]{1,0:T(8,128)(2,1)S(1)}, bf16[672,128]{1,0:T(8,128)(2,1)S(1)}, u32[]{:S(2)}, u32[]{:S(2)}) collective-permute-start(bf16[672,128]{1,0:T(8,128)(2,1)S(1)} %get-tuple-element.38), channel_id=1, source_target_pairs={{0,24},{8,16},{16,8},{24,0},{32,56},{40,48},{48,40},{56,32},{64,88... | collective-permute-start | bytes 516104 | tf_op jit(solution)/shard_map/ppermute | solution.py:252
  12.5 2.8 %collective-permute-done.1.refs_3_.r1 = bf16[672,128]{1,0:T(8,128)(2,1)S(1)} collective-permute-done((bf16[672,128]{1,0:T(8,128)(2,1)S(1)}, bf16[672,128]{1,0:T(8,128)(2,1)S(1)}, u32[]{:S(2)}, u32[]{:S(2)}) %collective-permute-start.1) | collective-permute-done | bytes 172064 | tf_op jit(solution)/shard_map/ppermute | solution.py:252
  15.4 1.9 %collective-permute-start.2 = (bf16[672,128]{1,0:T(8,128)(2,1)S(1)}, bf16[672,128]{1,0:T(8,128)(2,1)S(1)}, u32[]{:S(2)}, u32[]{:S(2)}) collective-permute-start(bf16[672,128]{1,0:T(8,128)(2,1)S(1)} %get-tuple-element.42), channel_id=1, source_target_pairs={{0,32},{8,40},{16,48},{24,56},{32,0},{40,8},{48,16},{56,24},{64,96... | collective-permute-start | bytes 516104 | tf_op jit(solution)/shard_map/ppermute | solution.py:252
  17.3 2.8 %collective-permute-done.2.refs_3_.r2 = bf16[672,128]{1,0:T(8,128)(2,1)S(1)} collective-permute-done((bf16[672,128]{1,0:T(8,128)(2,1)S(1)}, bf16[672,128]{1,0:T(8,128)(2,1)S(1)}, u32[]{:S(2)}, u32[]{:S(2)}) %collective-permute-start.2) | collective-permute-done | bytes 172064 | tf_op jit(solution)/shard_map/ppermute | solution.py:252
  20.2 3.1 %collective-permute-start.3 = (bf16[672,128]{1,0:T(8,128)(2,1)S(1)}, bf16[672,128]{1,0:T(8,128)(2,1)S(1)}, u32[]{:S(2)}, u32[]{:S(2)}) collective-permute-start(bf16[672,128]{1,0:T(8,128)(2,1)S(1)} %get-tuple-element.46), channel_id=1, source_target_pairs={{0,64},{8,72},{16,80},{24,88},{32,96},{40,104},{48,112},{56,120},{... | collective-permute-start | bytes 516104 | tf_op jit(solution)/shard_map/ppermute | solution.py:252
  23.3 0.9 %copy-done.3 = bf16[256,10,14]{0,2,1:T(8,128)(2,1)S(1)} copy-done((bf16[256,10,14]{0,2,1:T(8,128)(2,1)S(1)}, bf16[256,10,14]{0,2,1:T(8,128)(2,1)}, u32[]{:S(2)}) %copy-start.3) | copy-done | bytes 71704
  24.2 0.8 %copy-done.6 = bf16[256,128]{1,0:T(8,128)(2,1)S(1)} copy-done((bf16[256,128]{1,0:T(8,128)(2,1)S(1)}, bf16[256,128]{1,0:T(8,128)(2,1)}, u32[]{:S(2)}) %copy-start.6) | copy-done | bytes 65560
  25.7 0.8 %copy-done.10 = bf16[256,128]{1,0:T(8,128)(2,1)S(1)} copy-done((bf16[256,128]{1,0:T(8,128)(2,1)S(1)}, bf16[256,128]{1,0:T(8,128)(2,1)}, u32[]{:S(2)}) %copy-start.10) | copy-done | bytes 65560
  27.2 2.0 %local.1 = (f32[640,256]{1,0:T(8,128)S(1)}, bf16[128,256]{1,0:T(8,128)(2,1)S(1)}) custom-call(bf16[640,256]{1,0:T(8,128)(2,1)S(1)} %get-tuple-element.32.xt_ref, bf16[256,128]{1,0:T(8,128)(2,1)S(1)} %copy-done.6, bf16[256,128]{1,0:T(8,128)(2,1)S(1)} %copy-done.10, f32[10,256]{1,0:T(8,128)S(1)} %bitcast.8, f32[16,256]{1,0:T(8,128)S(1)} %get-tuple-element.33.cum_ref, ...), custom_call_target="tpu_custom_call" | custom-call | flops 5000000000 | bytes 50000000 | tf_op jit(solution)/shard_map/local/pallas_call | solution.py:212
  30.1 5.5 %collective-permute-start.4 = (bf16[672,128]{1,0:T(8,128)(2,1)S(1)}, bf16[672,128]{1,0:T(8,128)(2,1)S(1)}, u32[]{:S(2)}, u32[]{:S(2)}) collective-permute-start(bf16[672,128]{1,0:T(8,128)(2,1)S(1)} %get-tuple-element.51), channel_id=1, source_target_pairs={{0,224},{8,232},{16,240},{24,248},{32,192},{40,200},{48,208},{56,2... | collective-permute-start | bytes 516104 | tf_op jit(solution)/shard_map/ppermute | solution.py:252
  36.1 3.6 %collective-permute-done.4.recv_ref = bf16[672,128]{1,0:T(8,128)(2,1)S(1)} collective-permute-done((bf16[672,128]{1,0:T(8,128)(2,1)S(1)}, bf16[672,128]{1,0:T(8,128)(2,1)S(1)}, u32[]{:S(2)}, u32[]{:S(2)}) %collective-permute-start.4) | collective-permute-done | bytes 172064 | tf_op jit(solution)/shard_map/ppermute | solution.py:252
  39.7 1.8 %project.1 = (bf16[128,2688]{1,0:T(8,128)(2,1)S(1)}, bf16[128,2688]{1,0:T(8,128)(2,1)S(1)}) custom-call(f32[640,256]{1,0:T(8,128)S(1)} %near.1.near_ref, bf16[672,128]{1,0:T(8,128)(2,1)S(1)} %collective-permute-done.4.recv_ref, f32[16,128]{1,0:T(8,128)S(1)} %get-tuple-element.52.span_ref, bf16[128,256]{1,0:T(8,128)(2,1)S(1)} %get-tuple-element.48.qt_ref, ...), custom_call_target="tpu_custom_call" | custom-call | flops 1000000000 | bytes 10000000 | tf_op jit(solution)/shard_map/project/pallas_call | solution.py:212
  41.5 5.8 %collective-permute-start.5 = (bf16[128,2688]{1,0:T(8,128)(2,1)S(1)}, bf16[128,2688]{1,0:T(8,128)(2,1)S(1)}, u32[]{:S(2)}, u32[]{:S(2)}) collective-permute-start(bf16[128,2688]{1,0:T(8,128)(2,1)S(1)} %get-tuple-element.54), channel_id=1, source_target_pairs={{0,1},{1,0},{2,3},{3,2},{4,5},{5,4},{6,7},{7,6},{8,9},{9,8},{10,11... | collective-permute-start | bytes 2064392 | tf_op jit(solution)/shard_map/ppermute | solution.py:272
  47.3 1.8 %collective-permute-done.5.recv_ref = bf16[128,2688]{1,0:T(8,128)(2,1)S(1)} collective-permute-done((bf16[128,2688]{1,0:T(8,128)(2,1)S(1)}, bf16[128,2688]{1,0:T(8,128)(2,1)S(1)}, u32[]{:S(2)}, u32[]{:S(2)}) %collective-permute-start.5) | collective-permute-done | bytes 688160 | tf_op jit(solution)/shard_map/ppermute | solution.py:272
  49.4 1.3 %collective-permute-start.6 = (bf16[32,2688]{1,0:T(8,128)(2,1)S(1)}, bf16[32,2688]{1,0:T(8,128)(2,1)S(1)}, u32[]{:S(2)}, u32[]{:S(2)}) collective-permute-start(bf16[32,2688]{1,0:T(8,128)(2,1)S(1)} %get-tuple-element.56), channel_id=1, source_target_pairs={{0,2},{1,3},{2,0},{3,1},{4,6},{5,7},{6,4},{7,5},{8,10},{9,11},{10,... | collective-permute-start | bytes 516104 | tf_op jit(solution)/shard_map/ppermute | solution.py:278
  50.7 2.6 %collective-permute-start.7 = (bf16[32,2688]{1,0:T(8,128)(2,1)S(1)}, bf16[32,2688]{1,0:T(8,128)(2,1)S(1)}, u32[]{:S(2)}, u32[]{:S(2)}) collective-permute-start(bf16[32,2688]{1,0:T(8,128)(2,1)S(1)} %get-tuple-element.57), channel_id=1, source_target_pairs={{0,4},{1,5},{2,6},{3,7},{4,0},{5,1},{6,2},{7,3},{8,12},{9,13},{10,... | collective-permute-start | bytes 516104 | tf_op jit(solution)/shard_map/ppermute | solution.py:278
  53.4 1.6 %collective-permute-done.6.r1 = bf16[32,2688]{1,0:T(8,128)(2,1)S(1)} collective-permute-done((bf16[32,2688]{1,0:T(8,128)(2,1)S(1)}, bf16[32,2688]{1,0:T(8,128)(2,1)S(1)}, u32[]{:S(2)}, u32[]{:S(2)}) %collective-permute-start.6) | collective-permute-done | bytes 172064 | tf_op jit(solution)/shard_map/ppermute | solution.py:278
  55.0 6.2 %collective-permute-done.7.r2 = bf16[32,2688]{1,0:T(8,128)(2,1)S(1)} collective-permute-done((bf16[32,2688]{1,0:T(8,128)(2,1)S(1)}, bf16[32,2688]{1,0:T(8,128)(2,1)S(1)}, u32[]{:S(2)}, u32[]{:S(2)}) %collective-permute-start.7) | collective-permute-done | bytes 172064 | tf_op jit(solution)/shard_map/ppermute | solution.py:278
  61.2 2.7 %collective-permute-done.8.r3 = bf16[32,2688]{1,0:T(8,128)(2,1)S(1)} collective-permute-done((bf16[32,2688]{1,0:T(8,128)(2,1)S(1)}, bf16[32,2688]{1,0:T(8,128)(2,1)S(1)}, u32[]{:S(2)}, u32[]{:S(2)}) %collective-permute-start.8) | collective-permute-done | bytes 172064 | tf_op jit(solution)/shard_map/ppermute | solution.py:278
  63.9 0.8 %final.1 = bf16[32,2560]{1,0:T(8,128)(2,1)} custom-call(f32[32,2688]{1,0:T(8,128)S(1)} %get-tuple-element.55.own_ref, bf16[32,2688]{1,0:T(8,128)(2,1)S(1)} %collective-permute-done.6.r1, bf16[32,2688]{1,0:T(8,128)(2,1)S(1)} %collective-permute-done.7.r2, bf16[32,2688]{1,0:T(8,128)(2,1)S(1)} %collective-permute-done.8.r3), custom_call_target="tpu_custom_call" | custom-call | flops 1000000 | bytes 10000 | tf_op jit(solution)/shard_map/final/pallas_call | solution.py:212
  (32 shorter events, 5.2 us)
Async XLA Ops:
  0.0 1.0 %copy-start.2 = (bf16[256,640]{1,0:T(8,128)(2,1)S(1)}, bf16[256,640]{1,0:T(8,128)(2,1)}, u32[]{:S(2)}) copy-start(bf16[256,640]{1,0:T(8,128)(2,1)} %x_ref.1) | copy-start | bytes 983044
  1.0 0.8 %copy-start.5 = (bf16[256,128]{1,0:T(8,128)(2,1)S(1)}, bf16[256,128]{1,0:T(8,128)(2,1)}, u32[]{:S(2)}) copy-start(bf16[256,128]{1,0:T(8,128)(2,1)} %k_ref.3) | copy-start | bytes 196612
  1.8 0.7 %copy-start.7 = (f32[256,10]{0,1:T(8,128)S(1)}, f32[256,10]{0,1:T(8,128)}, u32[]{:S(2)}) copy-start(f32[256,10]{0,1:T(8,128)} %param.15) | copy-start | bytes 30724
  2.5 0.7 %copy-start.8 = (f32[256,10]{0,1:T(8,128)S(1)}, f32[256,10]{0,1:T(8,128)}, u32[]{:S(2)}) copy-start(f32[256,10]{0,1:T(8,128)} %param.14) | copy-start | bytes 30724
  3.7 5.0 %collective-permute-start = (bf16[672,128]{1,0:T(8,128)(2,1)S(1)}, bf16[672,128]{1,0:T(8,128)(2,1)S(1)}, u32[]{:S(2)}, u32[]{:S(2)}) collective-permute-start(bf16[672,128]{1,0:T(8,128)(2,1)S(1)} %get-tuple-element.35), channel_id=1, source_target_pairs={{0,8},{8,0},{16,24},{24,16},{32,40},{40,32},{48,56},{56,48},{64,72... | collective-permute-start | bytes 516104 | tf_op jit(solution)/shard_map/ppermute | solution.py:252
  8.8 6.6 %collective-permute-start.1 = (bf16[672,128]{1,0:T(8,128)(2,1)S(1)}, bf16[672,128]{1,0:T(8,128)(2,1)S(1)}, u32[]{:S(2)}, u32[]{:S(2)}) collective-permute-start(bf16[672,128]{1,0:T(8,128)(2,1)S(1)} %get-tuple-element.38), channel_id=1, source_target_pairs={{0,24},{8,16},{16,8},{24,0},{32,56},{40,48},{48,40},{56,32},{64,88... | collective-permute-start | bytes 516104 | tf_op jit(solution)/shard_map/ppermute | solution.py:252
  15.4 4.7 %collective-permute-start.2 = (bf16[672,128]{1,0:T(8,128)(2,1)S(1)}, bf16[672,128]{1,0:T(8,128)(2,1)S(1)}, u32[]{:S(2)}, u32[]{:S(2)}) collective-permute-start(bf16[672,128]{1,0:T(8,128)(2,1)S(1)} %get-tuple-element.42), channel_id=1, source_target_pairs={{0,32},{8,40},{16,48},{24,56},{32,0},{40,8},{48,16},{56,24},{64,96... | collective-permute-start | bytes 516104 | tf_op jit(solution)/shard_map/ppermute | solution.py:252
  20.2 9.1 %collective-permute-start.3 = (bf16[672,128]{1,0:T(8,128)(2,1)S(1)}, bf16[672,128]{1,0:T(8,128)(2,1)S(1)}, u32[]{:S(2)}, u32[]{:S(2)}) collective-permute-start(bf16[672,128]{1,0:T(8,128)(2,1)S(1)} %get-tuple-element.46), channel_id=1, source_target_pairs={{0,64},{8,72},{16,80},{24,88},{32,96},{40,104},{48,112},{56,120},{... | collective-permute-start | bytes 516104 | tf_op jit(solution)/shard_map/ppermute | solution.py:252
  23.3 0.9 %copy-start.3 = (bf16[256,10,14]{0,2,1:T(8,128)(2,1)S(1)}, bf16[256,10,14]{0,2,1:T(8,128)(2,1)}, u32[]{:S(2)}) copy-start(bf16[256,10,14]{0,2,1:T(8,128)(2,1)} %param.16) | copy-start | bytes 215044
  24.2 0.8 %copy-start.6 = (bf16[256,128]{1,0:T(8,128)(2,1)S(1)}, bf16[256,128]{1,0:T(8,128)(2,1)}, u32[]{:S(2)}) copy-start(bf16[256,128]{1,0:T(8,128)(2,1)} %k_ref.3) | copy-start | bytes 196612
  25.0 0.7 %copy-start.9 = (f32[256,10]{0,1:T(8,128)S(1)}, f32[256,10]{0,1:T(8,128)}, u32[]{:S(2)}) copy-start(f32[256,10]{0,1:T(8,128)} %param.14) | copy-start | bytes 30724
  25.7 0.8 %copy-start.10 = (bf16[256,128]{1,0:T(8,128)(2,1)S(1)}, bf16[256,128]{1,0:T(8,128)(2,1)}, u32[]{:S(2)}) copy-start(bf16[256,128]{1,0:T(8,128)(2,1)} %q_ref.1) | copy-start | bytes 196612
  26.5 0.7 %copy-start.11 = (f32[10]{0:T(128)S(1)}, f32[10]{0:T(128)}, u32[]{:S(2)}) copy-start(f32[10]{0:T(128)} %skip_ref.1) | copy-start | bytes 124
  27.2 2.0 %copy-start.12 = (f32[640]{0:T(1024)S(1)}, f32[640]{0:T(1024)}, u32[]{:S(2)}) copy-start(f32[640]{0:T(1024)} %param.18) | copy-start | bytes 7684
  27.2 8.4 %copy-start.4 = (bf16[256,10,14]{0,2,1:T(8,128)(2,1)S(1)}, bf16[256,10,14]{0,2,1:T(8,128)(2,1)}, u32[]{:S(2)}) copy-start(bf16[256,10,14]{0,2,1:T(8,128)(2,1)} %param.16) | copy-start | bytes 215044
  30.1 9.7 %collective-permute-start.4 = (bf16[672,128]{1,0:T(8,128)(2,1)S(1)}, bf16[672,128]{1,0:T(8,128)(2,1)S(1)}, u32[]{:S(2)}, u32[]{:S(2)}) collective-permute-start(bf16[672,128]{1,0:T(8,128)(2,1)S(1)} %get-tuple-element.51), channel_id=1, source_target_pairs={{0,224},{8,232},{16,240},{24,248},{32,192},{40,200},{48,208},{56,2... | collective-permute-start | bytes 516104 | tf_op jit(solution)/shard_map/ppermute | solution.py:252
  35.6 4.2 %copy-start = (bf16[640,2560]{1,0:T(8,128)(2,1)S(1)}, bf16[640,2560]{1,0:T(8,128)(2,1)}, u32[]{:S(2)}) copy-start(bf16[640,2560]{1,0:T(8,128)(2,1)} %ow_ref.1) | copy-start | bytes 9830404
  35.6 4.2 %copy-start.1 = (bf16[256,640]{1,0:T(8,128)(2,1)S(1)}, bf16[256,640]{1,0:T(8,128)(2,1)}, u32[]{:S(2)}) copy-start(bf16[256,640]{1,0:T(8,128)(2,1)} %gate_ref.1) | copy-start | bytes 983044
  41.5 7.5 %collective-permute-start.5 = (bf16[128,2688]{1,0:T(8,128)(2,1)S(1)}, bf16[128,2688]{1,0:T(8,128)(2,1)S(1)}, u32[]{:S(2)}, u32[]{:S(2)}) collective-permute-start(bf16[128,2688]{1,0:T(8,128)(2,1)S(1)} %get-tuple-element.54), channel_id=1, source_target_pairs={{0,1},{1,0},{2,3},{3,2},{4,5},{5,4},{6,7},{7,6},{8,9},{9,8},{10,11... | collective-permute-start | bytes 2064392 | tf_op jit(solution)/shard_map/ppermute | solution.py:272
  49.4 5.6 %collective-permute-start.6 = (bf16[32,2688]{1,0:T(8,128)(2,1)S(1)}, bf16[32,2688]{1,0:T(8,128)(2,1)S(1)}, u32[]{:S(2)}, u32[]{:S(2)}) collective-permute-start(bf16[32,2688]{1,0:T(8,128)(2,1)S(1)} %get-tuple-element.56), channel_id=1, source_target_pairs={{0,2},{1,3},{2,0},{3,1},{4,6},{5,7},{6,4},{7,5},{8,10},{9,11},{10,... | collective-permute-start | bytes 516104 | tf_op jit(solution)/shard_map/ppermute | solution.py:278
  50.7 10.4 %collective-permute-start.7 = (bf16[32,2688]{1,0:T(8,128)(2,1)S(1)}, bf16[32,2688]{1,0:T(8,128)(2,1)S(1)}, u32[]{:S(2)}, u32[]{:S(2)}) collective-permute-start(bf16[32,2688]{1,0:T(8,128)(2,1)S(1)} %get-tuple-element.57), channel_id=1, source_target_pairs={{0,4},{1,5},{2,6},{3,7},{4,0},{5,1},{6,2},{7,3},{8,12},{9,13},{10,... | collective-permute-start | bytes 516104 | tf_op jit(solution)/shard_map/ppermute | solution.py:278
  53.4 10.5 %collective-permute-start.8 = (bf16[32,2688]{1,0:T(8,128)(2,1)S(1)}, bf16[32,2688]{1,0:T(8,128)(2,1)S(1)}, u32[]{:S(2)}, u32[]{:S(2)}) collective-permute-start(bf16[32,2688]{1,0:T(8,128)(2,1)S(1)} %get-tuple-element.58), channel_id=1, source_target_pairs={{0,6},{1,7},{2,4},{3,5},{4,2},{5,3},{6,0},{7,1},{8,14},{9,15},{10,... | collective-permute-start | bytes 516104 | tf_op jit(solution)/shard_map/ppermute | solution.py:278

commit v2 on v1

--- a/solution.py
+++ b/solution.py
@@ -35,7 +35,20 @@
     return jnp.concatenate([value, jnp.zeros((16 - HEADS, value.shape[1]), F32)], axis=0)
 
 
-def state_kernel(x_ref, k_ref, step_ref, decay_ref, pay_ref, state_ref, xt_ref, cum_ref, tot_ref):
+def fetch(sources, targets, sems):
+    copies = [pltpu.make_async_copy(s, t, sems.at[i]) for i, (s, t) in enumerate(zip(sources, targets))]
+    for copy in copies:
+        copy.start()
+    return copies
+
+
+def state_kernel(
+    x_in, k_in, step_in, decay_in, pay_ref, state_ref, xt_ref, cum_ref, tot_ref,
+    x_ref, k_ref, step_ref, decay_ref, sems,
+):
+    copies = fetch((decay_in, step_in, k_in, x_in), (decay_ref, step_ref, k_ref, x_ref), sems)
+    copies[0].wait()
+    copies[1].wait()
     decay = pad_heads(decay_ref[...])
     step = pad_heads(step_ref[...])
     high = decay.astype(BF16)
@@ -53,6 +66,8 @@
     pay_ref[WIDTH : WIDTH + 16, :] = high
     pay_ref[WIDTH + 16 : WIDTH + 32, :] = low
     coef = step * jnp.exp(cum[:, TOK - 1 : TOK] - cum)
+    copies[2].wait()
+    copies[3].wait()
     keys = k_ref[...]
     for j in range(WIDTH // 128):
         rows = slice(j * 128, (j + 1) * 128)
@@ -66,7 +81,13 @@
         pay_ref[rows, :] = state.astype(BF16)
 
 
-def local_kernel(xt_ref, k_ref, q_ref, step_ref, cum_ref, w_ref, skip_ref, out_ref, qt_ref):
+def local_kernel(
+    xt_ref, cum_ref, skip_ref, k_in, q_in, step_in, w_in, out_ref, qt_ref,
+    k_ref, q_ref, step_ref, w_ref, sems,
+):
+    copies = fetch((q_in, k_in, step_in, w_in), (q_ref, k_ref, step_ref, w_ref), sems)
+    copies[0].wait()
+    copies[1].wait()
     qt = q_ref[...].astype(F32).T.astype(BF16)
     qt_ref[...] = qt
     scores = dot(k_ref[...], qt)
@@ -79,6 +100,8 @@
     for shift in range(7):
         level = level + (differ >= 1 << shift).astype(jnp.int32)
     level = jnp.where(early <= late, level, -1)
+    copies[2].wait()
+    copies[3].wait()
     for h in range(HEADS):
         weights = w_ref[h, 0:LOCAL_LEVELS, :].astype(F32)
         xt = xt_ref[h * 64 : (h + 1) * 64, :].astype(F32)
@@ -123,6 +146,54 @@
         pay_ref[rows, :] = new.astype(BF16)
 
 
+def totals_of(recv_ref):
+    return recv_ref[WIDTH : WIDTH + 16, :].astype(F32) + recv_ref[WIDTH + 16 : WIDTH + 32, :].astype(F32)
+
+
+def quad_kernel(_, r3, r2, r1, state_ref, tot_ref, pay_ref, pair_ref, new_ref, ntot_ref, span1_ref, span2_ref):
+    x = lax.axis_index("seq")
+    odd, upper = (x & 1) > 0, (x & 2) > 0
+    t0 = tot_ref[...]
+    t1, t2, t3 = totals_of(r1), totals_of(r2), totals_of(r3)
+    total = t0 + t1 + t2 + t3
+    ntot_ref[...] = total
+    high, low = split_two(total)
+    pay_ref[WIDTH : WIDTH + 16, :] = high
+    pay_ref[WIDTH + 16 : WIDTH + 32, :] = low
+    span1 = jnp.where(odd, t1, 0.0)
+    span1_ref[...] = span1
+    span2_ref[...] = span1 + jnp.where(upper, t2 + t3, 0.0)
+    mine_to = jnp.where(odd, 0.0, t1)
+    next_to = jnp.where(odd, t0, 0.0)
+    across_to = jnp.where(odd, 0.0, t3)
+    far_to = jnp.where(odd, t2, 0.0)
+    lower_pair = jnp.exp(jnp.where(upper, t0 + t1, 0.0))
+    f2, f3 = jnp.exp(across_to), jnp.exp(far_to)
+    other = jnp.where(upper, 0.0, t2 + t3)
+    f0, f1 = jnp.exp(mine_to + other), jnp.exp(next_to + other)
+    for h in range(HEADS):
+        rows = slice(h * 64, (h + 1) * 64)
+        row = slice(h, h + 1)
+        pair = f2[row] * r2[rows, :].astype(F32) + f3[row] * r3[rows, :].astype(F32)
+        pair_ref[rows, :] = pair.astype(BF16)
+        new = f0[row] * state_ref[rows, :] + f1[row] * r1[rows, :].astype(F32) + lower_pair[row] * pair
+        new_ref[rows, :] = new
+        pay_ref[rows, :] = new.astype(BF16)
+
+
+def last_combine_kernel(state_ref, tot_ref, span_ref, recv_ref, pay_ref, nspan_ref):
+    upper = ((lax.axis_index("seq") >> 3) & 1) > 0
+    total = tot_ref[...]
+    other = recv_ref[WIDTH : WIDTH + 16, :].astype(F32) + recv_ref[WIDTH + 16 : WIDTH + 32, :].astype(F32)
+    nspan_ref[...] = span_ref[...] + jnp.where(upper, other, 0.0)
+    for_other = jnp.where(upper, jnp.exp(total), 1.0)
+    for_mine = jnp.where(upper, 1.0, jnp.exp(other))
+    for h in range(HEADS):
+        rows = slice(h * 64, (h + 1) * 64)
+        new = for_other[h : h + 1] * recv_ref[rows, :].astype(F32) + for_mine[h : h + 1] * state_ref[rows, :]
+        pay_ref[rows, :] = new.astype(BF16)
+
+
 def far_term(recv_ref, qt, h, coef):
     rows = slice(h * 64, (h + 1) * 64)
     return dot(recv_ref[rows, :], qt) * coef
@@ -148,7 +219,7 @@
 
 def project_kernel(
     near_ref, recv_ref, span_ref, qt_ref, cum_ref, w_ref, gate_ref, gain_ref, ow_ref,
-    mine_ref, theirs_ref, feat_ref, square_ref,
+    theirs_ref, feat_ref, square_ref,
 ):
     qt = qt_ref[...]
     cum = cum_ref[...]
@@ -165,17 +236,23 @@
         squares = squares + jnp.sum(gated * gated, axis=1, keepdims=True)
         feat_ref[:, cols] = (gated * gain_ref[:, cols]).astype(BF16)
     square_ref[...] = jnp.broadcast_to(squares, (TOK, 128))
-    core = lax.axis_index("head") & 1
+    product_rows(feat_ref, square_ref, ow_ref, theirs_ref, 1 - (lax.axis_index("head") & 1))
+
+
+def product_rows(feat_ref, square_ref, ow_ref, out_ref, side):
     lane = lax.broadcasted_iota(jnp.int32, (32, 128), 1)
-    for out_ref, side in ((theirs_ref, 1 - core), (mine_ref, core)):
-        starts = [pl.multiple_of((2 * y + side) * 32, 32) for y in range(4)]
-        rows = jnp.concatenate([feat_ref[pl.ds(s, 32), :] for s in starts], axis=0)
-        out_ref[:, 0:DM] = dot(rows, ow_ref[...]).astype(BF16)
-        for y, s in enumerate(starts):
-            high, low = split_two(square_ref[pl.ds(s, 32), :])
-            out_ref[y * 32 : (y + 1) * 32, DM:WIDE] = jnp.where(
-                lane < 64, high.astype(F32), low.astype(F32)
-            ).astype(BF16)
+    starts = [pl.multiple_of((2 * y + side) * 32, 32) for y in range(4)]
+    rows = jnp.concatenate([feat_ref[pl.ds(s, 32), :] for s in starts], axis=0)
+    out_ref[:, 0:DM] = dot(rows, ow_ref[...]).astype(BF16)
+    for y, s in enumerate(starts):
+        high, low = split_two(square_ref[pl.ds(s, 32), :])
+        out_ref[y * 32 : (y + 1) * 32, DM:WIDE] = jnp.where(
+            lane < 64, high.astype(F32), low.astype(F32)
+        ).astype(BF16)
+
+
+def own_rows_kernel(feat_ref, square_ref, ow_ref, mine_ref):
+    product_rows(feat_ref, square_ref, ow_ref, mine_ref, lax.axis_index("head") & 1)
 
 
 def squares_of(ref, rows):
@@ -204,10 +281,16 @@
     out_ref[...] = (total * scale).astype(BF16)
 
 
-def call(kernel, outs, *args, scratch=(), flops=0, name=None, smem=()):
-    specs = [
-        pl.BlockSpec(memory_space=pltpu.SMEM if i in smem else pltpu.VMEM) for i in range(len(args))
-    ]
+def call(kernel, outs, *args, scratch=(), flops=0, name=None, smem=(), hbm=(), free=()):
+    def space(i):
+        if i in smem:
+            return pltpu.SMEM
+        if i in hbm:
+            return pltpu.HBM
+        return pl.ANY if i in free else pltpu.VMEM
+
+    specs = [pl.BlockSpec(memory_space=space(i)) for i in range(len(args))]
+    args = [pltpu.with_memory_space_constraint(a, pltpu.HBM) if i in hbm else a for i, a in enumerate(args)]
     shapes = [jax.ShapeDtypeStruct(shape, dtype) for shape, dtype in outs]
     outputs = pl.pallas_call(
         kernel,
@@ -222,15 +305,6 @@
     return outputs
 
 
-SENDS = (
-    [(d, d ^ 1) for d in range(32)],
-    [(d, d ^ 3) for d in range(32)],
-    [(d, d ^ 4) for d in range(32)],
-    [(d, d ^ 8) for d in range(32)],
-    [(d, d ^ 28) for d in range(16)],
-)
-
-
 def on_device(token_values, gate_values, state_in, state_out, step_size, log_decay, level_weight, skip_weight, norm_gain, out_weight):
     step = jnp.transpose(step_size)
     decay = jnp.transpose(log_decay)
@@ -238,44 +312,61 @@
     pay, state, xt, cum, total = call(
         state_kernel,
         [((PAY, N), BF16), ((WIDTH, N), F32), ((WIDTH, TOK), BF16), ((16, TOK), F32), ((16, 128), F32)],
-        token_values, state_in, step, decay, flops=10**8, name="state",
+        token_values, state_in, step, decay, flops=10**8, name="state", hbm=(0, 1, 2, 3),
+        scratch=[
+            pltpu.VMEM((TOK, WIDTH), BF16), pltpu.VMEM((TOK, N), BF16), pltpu.VMEM((HEADS, TOK), F32),
+            pltpu.VMEM((HEADS, TOK), F32), pltpu.SemaphoreType.DMA((4,)),
+        ],
     )
     local, qt = call(
         local_kernel,
         [((WIDTH, TOK), F32), ((N, TOK), BF16)],
-        xt, state_in, state_out, step, cum, weight, skip_weight,
-        flops=5 * 10**9, name="local", smem=(6,),
-    )
-    span = jnp.zeros((16, 128), F32)
-    recvs, spans = [], []
-    for bit in range(5):
-        recv = lax.ppermute(pay, "seq", SENDS[bit])
-        recvs.append(recv)
-        spans.append(span)
-        if bit < 4:
-            pay, state, total, span = call(
-                lambda *refs, bit=bit: combine_kernel(bit, *refs),
-                [((PAY, N), BF16), ((WIDTH, N), F32), ((16, 128), F32), ((16, 128), F32)],
-                state, total, span, recv, flops=10**6, name="combine",
-            )
+        xt, cum, skip_weight, state_in, state_out, step, weight,
+        flops=5 * 10**9, name="local", smem=(2,), hbm=(3, 4, 5, 6),
+        scratch=[
+            pltpu.VMEM((TOK, N), BF16), pltpu.VMEM((TOK, N), BF16), pltpu.VMEM((HEADS, TOK), F32),
+            pltpu.VMEM((HEADS, 14, TOK), BF16), pltpu.SemaphoreType.DMA((4,)),
+        ],
+    )
+    r3, r2, r1 = [lax.ppermute(pay, "seq", [(d, d ^ k) for d in range(32)]) for k in (3, 2, 1)]
+    pay, pair, state, total, span1, span2 = call(
+        quad_kernel,
+        [((PAY, N), BF16), ((WIDTH, N), BF16), ((WIDTH, N), F32)] + [((16, 128), F32)] * 3,
+        local, r3, r2, r1, state, total, flops=10**6, name="quad", free=(0,),
+    )
+    recvs, spans = [r1, pair], [jnp.zeros((16, 128), F32), span1, span2]
+    recvs.append(lax.ppermute(pay, "seq", [(d, d ^ 4) for d in range(32)]))
+    pay, state, total, span = call(
+        lambda *refs: combine_kernel(2, *refs),
+        [((PAY, N), BF16), ((WIDTH, N), F32), ((16, 128), F32), ((16, 128), F32)],
+        state, total, span2, recvs[2], flops=10**6, name="combine",
+    )
+    spans.append(span)
+    recvs.append(lax.ppermute(pay, "seq", [(d, d ^ 12) for d in range(32)]))
+    pay, span = call(
+        last_combine_kernel, [((WIDTH, N), BF16), ((16, 128), F32)],
+        state, total, span, recvs[3], flops=10**6, name="combine",
+    )
+    spans.append(span)
+    recvs.append(lax.ppermute(pay, "seq", [(d, d ^ 28) for d in range(32)]))
     (near,) = call(
         near_kernel, [((WIDTH, TOK), F32)], local, *recvs[:4], *spans[:4], qt, cum, weight,
         flops=2 * 10**9, name="near",
     )
-    mine, theirs = call(
+    theirs, feat, square = call(
         project_kernel,
-        [((128, WIDE), BF16), ((128, WIDE), BF16)],
+        [((128, WIDE), BF16), ((TOK, WIDTH), BF16), ((TOK, 128), F32)],
         near, recvs[4], spans[4], qt, cum, weight, gate_values, norm_gain[None, :], out_weight,
-        scratch=[pltpu.VMEM((TOK, WIDTH), BF16), pltpu.VMEM((TOK, 128), F32)],
         flops=10**9, name="project",
     )
+    (mine,) = call(own_rows_kernel, [((128, WIDE), BF16)], feat, square, out_weight, flops=10**9, name="own_rows")
     recv = lax.ppermute(theirs, "head", [(g, g ^ 1) for g in range(8)])
     own, *sends = call(
         pair_kernel,
         [((32, WIDE), F32)] + [((32, WIDE), BF16)] * 3,
         mine, recv, flops=10**6, name="pair",
     )
-    got = [lax.ppermute(sends[k - 1], "head", [(g, g ^ (2 * k)) for g in range(8)]) for k in (1, 2, 3)]
+    got = [lax.ppermute(sends[k - 1], "head", [(g, g ^ (2 * k)) for g in range(8)]) for k in (3, 2, 1)]
     (out,) = call(final_kernel, [((32, DM), BF16)], own, *got, flops=10**6, name="final")
     return out
 

time: 65.2 us -> 55.1 us (0.85)
  local copies, waits for them, and re-layouts: 7.21 us -> 0.67 us
  waiting for transfers between devices: 24.3 us -> 20.5 us
  Pallas kernels: 6.94 us -> 8.27 us
  starting transfers between devices: 26.1 us -> 25.3 us
    unnamed x26 -> x10, local copies, waits for them, and re-layouts: 7.2 us -> 0.67 us
    ppermute x3, waiting for transfers between devices: 10.5 us -> 7.7 us  [on_device(): lax.ppermute(sends[k - 1], 'head', [(g, g ^ 2 * k) for g in range(8)])]
    pallas_call x10, Pallas kernels: 6.94 us -> 8.27 us  [call(): pl.pallas_call(kernel, out_shape=shapes, in_specs=specs, out_specs=[pl.Bl...]
    ppermute x5 -> x6, starting transfers between devices: 16.4 us -> 15.1 us  [the longest x3 4.57 us: on_device(): lax.ppermute(pay, 'seq', [(d, d ^ k) for d in range(32)])]
    ppermute x1, starting transfers between devices: 5.78 us -> 6.75 us  [on_device(): recv = lax.ppermute(theirs, 'head', [(g, g ^ 1) for g in range(8)])]
    ppermute x1, waiting for transfers between devices: 1.77 us -> 1.06 us  [on_device(): recv = lax.ppermute(theirs, 'head', [(g, g ^ 1) for g in range(8)])]
    ppermute x5 -> x6, waiting for transfers between devices: 12 us -> 11.7 us  [the longest x3 3.8 us: on_device(): lax.ppermute(pay, 'seq', [(d, d ^ k) for d in range(32)])]
  transfers between devices with their start and end apart: 9 -> 10, of which waited for: 8 -> 7; matrix products, arithmetic and copies ran while one was open for 0% -> 0% of each run, Pallas kernels for 4% -> 8%
where the time goes in v2:
time: 55.1 us; the launch traced here: 54.9 us
  starting transfers between devices  25.3 us (46%)
  waiting for transfers between devices  20.5 us (37%)
  Pallas kernels  8.27 us (15%)
  local copies, waits for them, and re-layouts  0.67 us (1%)
    pallas_call x10, Pallas kernels, call(): pl.pallas_call(kernel, out_shape=shapes, in_specs=specs, out_specs=[pl.Bl...  8.27 us
    ppermute x3, waiting for transfers between devices, on_device(): lax.ppermute(sends[k - 1], 'head', [(g, g ^ 2 * k) for g in range(8)])  7.7 us
    ppermute x1, starting transfers between devices, on_device(): recv = lax.ppermute(theirs, 'head', [(g, g ^ 1) for g in range(8)])  6.75 us
    ppermute x3, starting transfers between devices, on_device(): lax.ppermute(pay, 'seq', [(d, d ^ k) for d in range(32)])  4.57 us
    ppermute x1, starting transfers between devices, on_device(): recvs.append(lax.ppermute(pay, 'seq', [(d, d ^ 28) for d in range(32)]))  4.57 us
    ppermute x1, starting transfers between devices, on_device(): recvs.append(lax.ppermute(pay, 'seq', [(d, d ^ 12) for d in range(32)]))  4.26 us
    ppermute x3, waiting for transfers between devices, on_device(): lax.ppermute(pay, 'seq', [(d, d ^ k) for d in range(32)])  3.8 us
    ppermute x3, starting transfers between devices, on_device(): lax.ppermute(sends[k - 1], 'head', [(g, g ^ 2 * k) for g in range(8)])  3.47 us
  transfers between devices with their start and end apart: 10, of which 7 were waited for; matrix products, arithmetic and copies ran while one was open for 0% of the time, Pallas kernels for 8%

profile of v2, /device:TPU:1, one launch (start us, length us, event | category | flops | bytes accessed | tf_op | source)
XLA Modules:
  0.0 54.9 jit_solution(12649104215983704680)
XLA Ops:
  0.0 1.4 %state.1 = (bf16[672,128]{1,0:T(8,128)(2,1)S(1)}, f32[640,128]{1,0:T(8,128)S(1)}, bf16[640,256]{1,0:T(8,128)(2,1)S(1)}, f32[16,256]{1,0:T(8,128)S(1)}, f32[16,128]{1,0:T(8,128)S(1)}) custom-call(bf16[256,640]{1,0:T(8,128)(2,1)} %x_in.1, bf16[256,128]{1,0:T(8,128)(2,1)} %k_in.3, f32[10,256]{1,0:T(8,128)} %bitcast.7, f32[10,256]{1,0:T(8,128)} %bitcast.6), custom_call_target="tpu_custom_call" | custom-call | flops 100000000 | bytes 1000000 | tf_op jit(solution)/shard_map/state/pallas_call | solution.py:295
  1.4 2.1 %collective-permute-start = (bf16[672,128]{1,0:T(8,128)(2,1)S(1)}, bf16[672,128]{1,0:T(8,128)(2,1)S(1)}, u32[]{:S(2)}, u32[]{:S(2)}) collective-permute-start(bf16[672,128]{1,0:T(8,128)(2,1)S(1)} %get-tuple-element.34), channel_id=1, source_target_pairs={{0,8},{8,0},{16,24},{24,16},{32,40},{40,32},{48,56},{56,48},{64,72... | collective-permute-start | bytes 516104 | tf_op jit(solution)/shard_map/ppermute | solution.py:331
  3.5 1.8 %collective-permute-start.1 = (bf16[672,128]{1,0:T(8,128)(2,1)S(1)}, bf16[672,128]{1,0:T(8,128)(2,1)S(1)}, u32[]{:S(2)}, u32[]{:S(2)}) collective-permute-start(bf16[672,128]{1,0:T(8,128)(2,1)S(1)} %get-tuple-element.34), channel_id=1, source_target_pairs={{0,24},{8,16},{16,8},{24,0},{32,56},{40,48},{48,40},{56,32},{64,88... | collective-permute-start | bytes 516104 | tf_op jit(solution)/shard_map/ppermute | solution.py:331
  5.3 0.6 %collective-permute-start.2 = (bf16[672,128]{1,0:T(8,128)(2,1)S(1)}, bf16[672,128]{1,0:T(8,128)(2,1)S(1)}, u32[]{:S(2)}, u32[]{:S(2)}) collective-permute-start(bf16[672,128]{1,0:T(8,128)(2,1)S(1)} %get-tuple-element.34), channel_id=1, source_target_pairs={{0,16},{8,24},{16,0},{24,8},{32,48},{40,56},{48,32},{56,40},{64,80... | collective-permute-start | bytes 516104 | tf_op jit(solution)/shard_map/ppermute | solution.py:331
  6.0 0.7 %copy-done.3 = f32[10]{0:T(128)S(1)} copy-done((f32[10]{0:T(128)S(1)}, f32[10]{0:T(128)}, u32[]{:S(2)}) %copy-start.3) | copy-done | bytes 64
  6.6 3.0 %local.1 = (f32[640,256]{1,0:T(8,128)S(1)}, bf16[128,256]{1,0:T(8,128)(2,1)S(1)}) custom-call(bf16[640,256]{1,0:T(8,128)(2,1)S(1)} %get-tuple-element.31.xt_ref, f32[16,256]{1,0:T(8,128)S(1)} %get-tuple-element.32.cum_ref, f32[10]{0:T(128)S(1)} %copy-done.3, bf16[256,128]{1,0:T(8,128)(2,1)} %k_in.3, bf16[256,128]{1,0:T(8,128)(2,1)} %q_in.1, ...), custom_call_target="tpu_custom_call" | custom-call | flops 5000000000 | bytes 50000000 | tf_op jit(solution)/shard_map/local/pallas_call | solution.py:295
  9.7 3.8 %collective-permute-done.2.r2 = bf16[672,128]{1,0:T(8,128)(2,1)S(1)} collective-permute-done((bf16[672,128]{1,0:T(8,128)(2,1)S(1)}, bf16[672,128]{1,0:T(8,128)(2,1)S(1)}, u32[]{:S(2)}, u32[]{:S(2)}) %collective-permute-start.2) | collective-permute-done | bytes 172064 | tf_op jit(solution)/shard_map/ppermute | solution.py:331
  13.7 1.7 %collective-permute-start.3 = (bf16[672,128]{1,0:T(8,128)(2,1)S(1)}, bf16[672,128]{1,0:T(8,128)(2,1)S(1)}, u32[]{:S(2)}, u32[]{:S(2)}) collective-permute-start(bf16[672,128]{1,0:T(8,128)(2,1)S(1)} %get-tuple-element.38), channel_id=1, source_target_pairs={{0,32},{8,40},{16,48},{24,56},{32,0},{40,8},{48,16},{56,24},{64,96... | collective-permute-start | bytes 516104 | tf_op jit(solution)/shard_map/ppermute | solution.py:338
  15.4 2.8 %collective-permute-done.3.refs_3_.r2 = bf16[672,128]{1,0:T(8,128)(2,1)S(1)} collective-permute-done((bf16[672,128]{1,0:T(8,128)(2,1)S(1)}, bf16[672,128]{1,0:T(8,128)(2,1)S(1)}, u32[]{:S(2)}, u32[]{:S(2)}) %collective-permute-start.3) | collective-permute-done | bytes 172064 | tf_op jit(solution)/shard_map/ppermute | solution.py:338
  18.2 4.3 %collective-permute-start.4 = (bf16[672,128]{1,0:T(8,128)(2,1)S(1)}, bf16[672,128]{1,0:T(8,128)(2,1)S(1)}, u32[]{:S(2)}, u32[]{:S(2)}) collective-permute-start(bf16[672,128]{1,0:T(8,128)(2,1)S(1)} %get-tuple-element.42), channel_id=1, source_target_pairs={{0,96},{8,104},{16,112},{24,120},{32,64},{40,72},{48,80},{56,88},{... | collective-permute-start | bytes 516104 | tf_op jit(solution)/shard_map/ppermute | solution.py:345
  22.5 2.9 %collective-permute-done.4.r3.recv_ref = bf16[672,128]{1,0:T(8,128)(2,1)S(1)} collective-permute-done((bf16[672,128]{1,0:T(8,128)(2,1)S(1)}, bf16[672,128]{1,0:T(8,128)(2,1)S(1)}, u32[]{:S(2)}, u32[]{:S(2)}) %collective-permute-start.4) | collective-permute-done | bytes 172064 | tf_op jit(solution)/shard_map/ppermute | solution.py:345
  25.5 4.6 %collective-permute-start.5 = (bf16[640,128]{1,0:T(8,128)(2,1)S(1)}, bf16[640,128]{1,0:T(8,128)(2,1)S(1)}, u32[]{:S(2)}, u32[]{:S(2)}) collective-permute-start(bf16[640,128]{1,0:T(8,128)(2,1)S(1)} %get-tuple-element.48), channel_id=1, source_target_pairs={{0,224},{8,232},{16,240},{24,248},{32,192},{40,200},{48,208},{56,2... | collective-permute-start | bytes 491528 | tf_op jit(solution)/shard_map/ppermute | solution.py:351
  30.1 0.5 near.1.near_ref
  30.6 2.3 %collective-permute-done.5.recv_ref = bf16[640,128]{1,0:T(8,128)(2,1)S(1)} collective-permute-done((bf16[640,128]{1,0:T(8,128)(2,1)S(1)}, bf16[640,128]{1,0:T(8,128)(2,1)S(1)}, u32[]{:S(2)}, u32[]{:S(2)}) %collective-permute-start.5) | collective-permute-done | bytes 163872 | tf_op jit(solution)/shard_map/ppermute | solution.py:351
  32.8 1.2 %project.1 = (bf16[128,2688]{1,0:T(8,128)(2,1)S(1)}, bf16[256,640]{1,0:T(8,128)(2,1)S(1)}, f32[256,128]{1,0:T(8,128)S(1)}) custom-call(f32[640,256]{1,0:T(8,128)S(1)} %near.1.near_ref, bf16[640,128]{1,0:T(8,128)(2,1)S(1)} %collective-permute-done.5.recv_ref, f32[16,128]{1,0:T(8,128)S(1)} %get-tuple-element.49.span_ref, ...), custom_call_target="tpu_custom_call" | custom-call | flops 1000000000 | bytes 10000000 | tf_op jit(solution)/shard_map/project/pallas_call | solution.py:295
  34.0 6.8 %collective-permute-start.6 = (bf16[128,2688]{1,0:T(8,128)(2,1)S(1)}, bf16[128,2688]{1,0:T(8,128)(2,1)S(1)}, u32[]{:S(2)}, u32[]{:S(2)}) collective-permute-start(bf16[128,2688]{1,0:T(8,128)(2,1)S(1)} %get-tuple-element.52), channel_id=1, source_target_pairs={{0,1},{1,0},{2,3},{3,2},{4,5},{5,4},{6,7},{7,6},{8,9},{9,8},{10,11... | collective-permute-start | bytes 2064392 | tf_op jit(solution)/shard_map/ppermute | solution.py:363
  40.8 0.7 %own_rows.1.mine_ref = bf16[128,2688]{1,0:T(8,128)(2,1)S(1)} custom-call(bf16[256,640]{1,0:T(8,128)(2,1)S(1)} %get-tuple-element.50.feat_ref, f32[256,128]{1,0:T(8,128)S(1)} %get-tuple-element.51.square_ref, bf16[640,2560]{1,0:T(8,128)(2,1)S(1)} %copy-done), custom_call_target="tpu_custom_call" | custom-call | flops 1000000000 | bytes 10000000 | tf_op jit(solution)/shard_map/own_rows/pallas_call | solution.py:295
  41.5 1.1 %collective-permute-done.6.recv_ref = bf16[128,2688]{1,0:T(8,128)(2,1)S(1)} collective-permute-done((bf16[128,2688]{1,0:T(8,128)(2,1)S(1)}, bf16[128,2688]{1,0:T(8,128)(2,1)S(1)}, u32[]{:S(2)}, u32[]{:S(2)}) %collective-permute-start.6) | collective-permute-done | bytes 688160 | tf_op jit(solution)/shard_map/ppermute | solution.py:363
  42.9 2.8 %collective-permute-start.7 = (bf16[32,2688]{1,0:T(8,128)(2,1)S(1)}, bf16[32,2688]{1,0:T(8,128)(2,1)S(1)}, u32[]{:S(2)}, u32[]{:S(2)}) collective-permute-start(bf16[32,2688]{1,0:T(8,128)(2,1)S(1)} %get-tuple-element.54), channel_id=1, source_target_pairs={{0,6},{1,7},{2,4},{3,5},{4,2},{5,3},{6,0},{7,1},{8,14},{9,15},{10,... | collective-permute-start | bytes 516104 | tf_op jit(solution)/shard_map/ppermute | solution.py:369
  45.7 0.3 collective-permute-start.8
  46.0 0.3 collective-permute-start.9
  46.3 6.7 %collective-permute-done.7.r1 = bf16[32,2688]{1,0:T(8,128)(2,1)S(1)} collective-permute-done((bf16[32,2688]{1,0:T(8,128)(2,1)S(1)}, bf16[32,2688]{1,0:T(8,128)(2,1)S(1)}, u32[]{:S(2)}, u32[]{:S(2)}) %collective-permute-start.7) | collective-permute-done | bytes 172064 | tf_op jit(solution)/shard_map/ppermute | solution.py:369
  53.0 1.0 %collective-permute-done.9.r3 = bf16[32,2688]{1,0:T(8,128)(2,1)S(1)} collective-permute-done((bf16[32,2688]{1,0:T(8,128)(2,1)S(1)}, bf16[32,2688]{1,0:T(8,128)(2,1)S(1)}, u32[]{:S(2)}, u32[]{:S(2)}) %collective-permute-start.9) | collective-permute-done | bytes 172064 | tf_op jit(solution)/shard_map/ppermute | solution.py:369
  54.0 0.8 %final.1 = bf16[32,2560]{1,0:T(8,128)(2,1)} custom-call(f32[32,2688]{1,0:T(8,128)S(1)} %get-tuple-element.53.own_ref, bf16[32,2688]{1,0:T(8,128)(2,1)S(1)} %collective-permute-done.7.r1, bf16[32,2688]{1,0:T(8,128)(2,1)S(1)} %collective-permute-done.8.r2, bf16[32,2688]{1,0:T(8,128)(2,1)S(1)} %collective-permute-done.9.r3), custom_call_target="tpu_custom_call" | custom-call | flops 1000000 | bytes 10000 | tf_op jit(solution)/shard_map/final/pallas_call | solution.py:295
  (18 shorter events, 0.7 us)
Async XLA Ops:
  1.4 8.3 %collective-permute-start = (bf16[672,128]{1,0:T(8,128)(2,1)S(1)}, bf16[672,128]{1,0:T(8,128)(2,1)S(1)}, u32[]{:S(2)}, u32[]{:S(2)}) collective-permute-start(bf16[672,128]{1,0:T(8,128)(2,1)S(1)} %get-tuple-element.34), channel_id=1, source_target_pairs={{0,8},{8,0},{16,24},{24,16},{32,40},{40,32},{48,56},{56,48},{64,72... | collective-permute-start | bytes 516104 | tf_op jit(solution)/shard_map/ppermute | solution.py:331
  3.5 6.2 %collective-permute-start.1 = (bf16[672,128]{1,0:T(8,128)(2,1)S(1)}, bf16[672,128]{1,0:T(8,128)(2,1)S(1)}, u32[]{:S(2)}, u32[]{:S(2)}) collective-permute-start(bf16[672,128]{1,0:T(8,128)(2,1)S(1)} %get-tuple-element.34), channel_id=1, source_target_pairs={{0,24},{8,16},{16,8},{24,0},{32,56},{40,48},{48,40},{56,32},{64,88... | collective-permute-start | bytes 516104 | tf_op jit(solution)/shard_map/ppermute | solution.py:331
  5.3 8.2 %collective-permute-start.2 = (bf16[672,128]{1,0:T(8,128)(2,1)S(1)}, bf16[672,128]{1,0:T(8,128)(2,1)S(1)}, u32[]{:S(2)}, u32[]{:S(2)}) collective-permute-start(bf16[672,128]{1,0:T(8,128)(2,1)S(1)} %get-tuple-element.34), channel_id=1, source_target_pairs={{0,16},{8,24},{16,0},{24,8},{32,48},{40,56},{48,32},{56,40},{64,80... | collective-permute-start | bytes 516104 | tf_op jit(solution)/shard_map/ppermute | solution.py:331
  6.0 0.7 %copy-start.3 = (f32[10]{0:T(128)S(1)}, f32[10]{0:T(128)}, u32[]{:S(2)}) copy-start(f32[10]{0:T(128)} %skip_ref.1) | copy-start | bytes 124
  6.6 15.9 %copy-start.4 = (f32[640]{0:T(1024)S(1)}, f32[640]{0:T(1024)}, u32[]{:S(2)}) copy-start(f32[640]{0:T(1024)} %param.18) | copy-start | bytes 7684
  6.6 23.4 %copy-start.2 = (bf16[256,10,14]{0,2,1:T(8,128)(2,1)S(1)}, bf16[256,10,14]{0,2,1:T(8,128)(2,1)}, u32[]{:S(2)}) copy-start(bf16[256,10,14]{0,2,1:T(8,128)(2,1)} %param.16) | copy-start | bytes 215044
  13.7 4.5 %collective-permute-start.3 = (bf16[672,128]{1,0:T(8,128)(2,1)S(1)}, bf16[672,128]{1,0:T(8,128)(2,1)S(1)}, u32[]{:S(2)}, u32[]{:S(2)}) collective-permute-start(bf16[672,128]{1,0:T(8,128)(2,1)S(1)} %get-tuple-element.38), channel_id=1, source_target_pairs={{0,32},{8,40},{16,48},{24,56},{32,0},{40,8},{48,16},{56,24},{64,96... | collective-permute-start | bytes 516104 | tf_op jit(solution)/shard_map/ppermute | solution.py:338
  18.2 7.2 %collective-permute-start.4 = (bf16[672,128]{1,0:T(8,128)(2,1)S(1)}, bf16[672,128]{1,0:T(8,128)(2,1)S(1)}, u32[]{:S(2)}, u32[]{:S(2)}) collective-permute-start(bf16[672,128]{1,0:T(8,128)(2,1)S(1)} %get-tuple-element.42), channel_id=1, source_target_pairs={{0,96},{8,104},{16,112},{24,120},{32,64},{40,72},{48,80},{56,88},{... | collective-permute-start | bytes 516104 | tf_op jit(solution)/shard_map/ppermute | solution.py:345
  25.5 7.4 %collective-permute-start.5 = (bf16[640,128]{1,0:T(8,128)(2,1)S(1)}, bf16[640,128]{1,0:T(8,128)(2,1)S(1)}, u32[]{:S(2)}, u32[]{:S(2)}) collective-permute-start(bf16[640,128]{1,0:T(8,128)(2,1)S(1)} %get-tuple-element.48), channel_id=1, source_target_pairs={{0,224},{8,232},{16,240},{24,248},{32,192},{40,200},{48,208},{56,2... | collective-permute-start | bytes 491528 | tf_op jit(solution)/shard_map/ppermute | solution.py:351
  30.0 2.8 %copy-start = (bf16[640,2560]{1,0:T(8,128)(2,1)S(1)}, bf16[640,2560]{1,0:T(8,128)(2,1)}, u32[]{:S(2)}) copy-start(bf16[640,2560]{1,0:T(8,128)(2,1)} %ow_ref.3) | copy-start | bytes 9830404
  30.0 2.8 %copy-start.1 = (bf16[256,640]{1,0:T(8,128)(2,1)S(1)}, bf16[256,640]{1,0:T(8,128)(2,1)}, u32[]{:S(2)}) copy-start(bf16[256,640]{1,0:T(8,128)(2,1)} %gate_ref.1) | copy-start | bytes 983044
  34.0 8.5 %collective-permute-start.6 = (bf16[128,2688]{1,0:T(8,128)(2,1)S(1)}, bf16[128,2688]{1,0:T(8,128)(2,1)S(1)}, u32[]{:S(2)}, u32[]{:S(2)}) collective-permute-start(bf16[128,2688]{1,0:T(8,128)(2,1)S(1)} %get-tuple-element.52), channel_id=1, source_target_pairs={{0,1},{1,0},{2,3},{3,2},{4,5},{5,4},{6,7},{7,6},{8,9},{9,8},{10,11... | collective-permute-start | bytes 2064392 | tf_op jit(solution)/shard_map/ppermute | solution.py:363
  42.9 10.2 %collective-permute-start.7 = (bf16[32,2688]{1,0:T(8,128)(2,1)S(1)}, bf16[32,2688]{1,0:T(8,128)(2,1)S(1)}, u32[]{:S(2)}, u32[]{:S(2)}) collective-permute-start(bf16[32,2688]{1,0:T(8,128)(2,1)S(1)} %get-tuple-element.54), channel_id=1, source_target_pairs={{0,6},{1,7},{2,4},{3,5},{4,2},{5,3},{6,0},{7,1},{8,14},{9,15},{10,... | collective-permute-start | bytes 516104 | tf_op jit(solution)/shard_map/ppermute | solution.py:369
  45.7 7.4 %collective-permute-start.8 = (bf16[32,2688]{1,0:T(8,128)(2,1)S(1)}, bf16[32,2688]{1,0:T(8,128)(2,1)S(1)}, u32[]{:S(2)}, u32[]{:S(2)}) collective-permute-start(bf16[32,2688]{1,0:T(8,128)(2,1)S(1)} %get-tuple-element.55), channel_id=1, source_target_pairs={{0,4},{1,5},{2,6},{3,7},{4,0},{5,1},{6,2},{7,3},{8,12},{9,13},{10,... | collective-permute-start | bytes 516104 | tf_op jit(solution)/shard_map/ppermute | solution.py:369
  46.0 8.0 %collective-permute-start.9 = (bf16[32,2688]{1,0:T(8,128)(2,1)S(1)}, bf16[32,2688]{1,0:T(8,128)(2,1)S(1)}, u32[]{:S(2)}, u32[]{:S(2)}) collective-permute-start(bf16[32,2688]{1,0:T(8,128)(2,1)S(1)} %get-tuple-element.56), channel_id=1, source_target_pairs={{0,2},{1,3},{2,0},{3,1},{4,6},{5,7},{6,4},{7,5},{8,10},{9,11},{10,... | collective-permute-start | bytes 516104 | tf_op jit(solution)/shard_map/ppermute | solution.py:369

commit v3 on v2

--- a/solution.py
+++ b/solution.py
@@ -40,6 +40,16 @@
     for copy in copies:
         copy.start()
     return copies
+
+
+def put_totals(pay_ref, total):
+    high, low = split_two(total)
+    pay_ref[WIDTH : WIDTH + 16, :] = high
+    pay_ref[WIDTH + 16 : WIDTH + 32, :] = low
+
+
+def totals_of(recv_ref):
+    return recv_ref[WIDTH : WIDTH + 16, :].astype(F32) + recv_ref[WIDTH + 16 : WIDTH + 32, :].astype(F32)
 
 
 def state_kernel(
@@ -62,9 +72,7 @@
     total = jnp.broadcast_to(cum[:, TOK - 1 : TOK], (16, 128))
     cum_ref[...] = cum
     tot_ref[...] = total
-    high, low = split_two(total)
-    pay_ref[WIDTH : WIDTH + 16, :] = high
-    pay_ref[WIDTH + 16 : WIDTH + 32, :] = low
+    put_totals(pay_ref, total)
     coef = step * jnp.exp(cum[:, TOK - 1 : TOK] - cum)
     copies[2].wait()
     copies[3].wait()
@@ -130,13 +138,11 @@
 def combine_kernel(bit, state_ref, tot_ref, span_ref, recv_ref, pay_ref, new_ref, ntot_ref, nspan_ref):
     upper = ((lax.axis_index("seq") >> bit) & 1) > 0
     total = tot_ref[...]
-    other = recv_ref[WIDTH : WIDTH + 16, :].astype(F32) + recv_ref[WIDTH + 16 : WIDTH + 32, :].astype(F32)
+    other = totals_of(recv_ref)
     new_total = total + other
     ntot_ref[...] = new_total
     nspan_ref[...] = span_ref[...] + jnp.where(upper, other, 0.0)
-    high, low = split_two(new_total)
-    pay_ref[WIDTH : WIDTH + 16, :] = high
-    pay_ref[WIDTH + 16 : WIDTH + 32, :] = low
+    put_totals(pay_ref, new_total)
     for_other = jnp.where(upper, jnp.exp(total), 1.0)
     for_mine = jnp.where(upper, 1.0, jnp.exp(other))
     for h in range(HEADS):
@@ -146,20 +152,15 @@
         pay_ref[rows, :] = new.astype(BF16)
 
 
-def totals_of(recv_ref):
-    return recv_ref[WIDTH : WIDTH + 16, :].astype(F32) + recv_ref[WIDTH + 16 : WIDTH + 32, :].astype(F32)
-
-
-def quad_kernel(_, r3, r2, r1, state_ref, tot_ref, pay_ref, pair_ref, new_ref, ntot_ref, span1_ref, span2_ref):
+def quad_kernel(_, r3, r2, r1, state_ref, tot_ref, pay_ref, near_ref, pair_ref, new_ref, ntot_ref, span1_ref, span2_ref):
     x = lax.axis_index("seq")
     odd, upper = (x & 1) > 0, (x & 2) > 0
+    near_ref[...] = r1[0:WIDTH, :]
     t0 = tot_ref[...]
     t1, t2, t3 = totals_of(r1), totals_of(r2), totals_of(r3)
     total = t0 + t1 + t2 + t3
     ntot_ref[...] = total
-    high, low = split_two(total)
-    pay_ref[WIDTH : WIDTH + 16, :] = high
-    pay_ref[WIDTH + 16 : WIDTH + 32, :] = low
+    put_totals(pay_ref, total)
     span1 = jnp.where(odd, t1, 0.0)
     span1_ref[...] = span1
     span2_ref[...] = span1 + jnp.where(upper, t2 + t3, 0.0)
@@ -184,7 +185,7 @@
 def last_combine_kernel(state_ref, tot_ref, span_ref, recv_ref, pay_ref, nspan_ref):
     upper = ((lax.axis_index("seq") >> 3) & 1) > 0
     total = tot_ref[...]
-    other = recv_ref[WIDTH : WIDTH + 16, :].astype(F32) + recv_ref[WIDTH + 16 : WIDTH + 32, :].astype(F32)
+    other = totals_of(recv_ref)
     nspan_ref[...] = span_ref[...] + jnp.where(upper, other, 0.0)
     for_other = jnp.where(upper, jnp.exp(total), 1.0)
     for_mine = jnp.where(upper, 1.0, jnp.exp(other))
@@ -206,33 +207,31 @@
     return jnp.where(upper, lift * weight, 0.0)
 
 
-def near_kernel(local_ref, r0, r1, r2, r3, s0, s1, s2, s3, qt_ref, cum_ref, w_ref, out_ref):
+def near_kernel(local_ref, r0, r1, r2, r3, s0, s1, s2, s3, s4, qt_ref, cum_ref, w_ref, gate_ref, near_ref, lift_ref):
     qt = qt_ref[...]
     cum = cum_ref[...]
-    for h in range(HEADS):
-        rows = slice(h * 64, (h + 1) * 64)
-        total = local_ref[rows, :]
-        for bit, (recv, span) in enumerate(((r0, s0), (r1, s1), (r2, s2), (r3, s3))):
-            total = total + far_term(recv, qt, h, far_coef(bit, cum, span, w_ref, h))
-        out_ref[rows, :] = total
-
-
-def project_kernel(
-    near_ref, recv_ref, span_ref, qt_ref, cum_ref, w_ref, gate_ref, gain_ref, ow_ref,
-    theirs_ref, feat_ref, square_ref,
-):
-    qt = qt_ref[...]
-    cum = cum_ref[...]
+    for j in range(WIDTH // 128):
+        cols = slice(j * 128, (j + 1) * 128)
+        totals, lifts = [], []
+        for h in (2 * j, 2 * j + 1):
+            total = local_ref[h * 64 : (h + 1) * 64, :]
+            for bit, (recv, span) in enumerate(((r0, s0), (r1, s1), (r2, s2), (r3, s3))):
+                total = total + far_term(recv, qt, h, far_coef(bit, cum, span, w_ref, h))
+            totals.append(total)
+            lifts.append(jnp.broadcast_to(far_coef(4, cum, s4, w_ref, h), (64, TOK)))
+        gate = gate_ref[:, cols].astype(F32)
+        gate = gate / (1.0 + jnp.exp(-gate))
+        near_ref[:, cols] = jnp.concatenate(totals, axis=0).T * gate
+        lift_ref[:, cols] = jnp.concatenate(lifts, axis=0).T * gate
+
+
+def feature_kernel(near_ref, lift_ref, recv_ref, q_ref, gain_ref, ow_ref, theirs_ref, feat_ref, square_ref):
+    query = q_ref[...]
     squares = jnp.zeros((TOK, 1), F32)
     for j in range(WIDTH // 128):
         cols = slice(j * 128, (j + 1) * 128)
-        far = jnp.concatenate(
-            [far_term(recv_ref, qt, h, far_coef(4, cum, span_ref, w_ref, h)) for h in (2 * j, 2 * j + 1)],
-            axis=0,
-        )
-        mixed = (near_ref[cols, :] + far).T
-        gate = gate_ref[:, cols].astype(F32)
-        gated = mixed * (gate / (1.0 + jnp.exp(-gate)))
+        far = lax.dot_general(query, recv_ref[cols, :], (((1,), (1,)), ((), ())), preferred_element_type=F32)
+        gated = near_ref[:, cols] + lift_ref[:, cols] * far
         squares = squares + jnp.sum(gated * gated, axis=1, keepdims=True)
         feat_ref[:, cols] = (gated * gain_ref[:, cols]).astype(BF16)
     square_ref[...] = jnp.broadcast_to(squares, (TOK, 128))
@@ -255,8 +254,8 @@
     product_rows(feat_ref, square_ref, ow_ref, mine_ref, lax.axis_index("head") & 1)
 
 
-def squares_of(ref, rows):
-    return ref[rows, DM : DM + 1].astype(F32) + ref[rows, DM + 64 : DM + 65].astype(F32)
+def squares_at(ref, rows, at):
+    return ref[rows, at : at + 1].astype(F32) + ref[rows, at + 64 : at + 65].astype(F32)
 
 
 def pair_kernel(mine_ref, recv_ref, own_ref, o1, o2, o3):
@@ -266,14 +265,14 @@
         rows = pl.ds(pl.multiple_of(jnp.bitwise_xor(y, k) * 32, 32), 32)
         total = mine_ref[rows, 0:DM].astype(F32) + recv_ref[rows, 0:DM].astype(F32)
         out_ref[:, 0:DM] = total.astype(out_ref.dtype)
-        square = jnp.broadcast_to(squares_of(mine_ref, rows) + squares_of(recv_ref, rows), (32, 128))
+        square = jnp.broadcast_to(squares_at(mine_ref, rows, DM) + squares_at(recv_ref, rows, DM), (32, 128))
         high, low = split_two(square)
         out_ref[:, DM:WIDE] = jnp.where(lane < 64, high.astype(F32), low.astype(F32)).astype(out_ref.dtype)
 
 
 def final_kernel(own_ref, r1, r2, r3, out_ref):
     every = slice(0, 32)
-    square = squares_of(own_ref, every) + squares_of(r1, every) + squares_of(r2, every) + squares_of(r3, every)
+    square = sum(squares_at(ref, every, DM) for ref in (own_ref, r1, r2, r3))
     scale = lax.rsqrt(square * (1.0 / (H * P_SIZE)) + EPSILON)
     total = own_ref[:, 0:DM].astype(F32)
     for ref in (r1, r2, r3):
@@ -329,12 +328,12 @@
         ],
     )
     r3, r2, r1 = [lax.ppermute(pay, "seq", [(d, d ^ k) for d in range(32)]) for k in (3, 2, 1)]
-    pay, pair, state, total, span1, span2 = call(
+    pay, next_state, pair, state, total, span1, span2 = call(
         quad_kernel,
-        [((PAY, N), BF16), ((WIDTH, N), BF16), ((WIDTH, N), F32)] + [((16, 128), F32)] * 3,
+        [((PAY, N), BF16), ((WIDTH, N), BF16), ((WIDTH, N), BF16), ((WIDTH, N), F32)] + [((16, 128), F32)] * 3,
         local, r3, r2, r1, state, total, flops=10**6, name="quad", free=(0,),
     )
-    recvs, spans = [r1, pair], [jnp.zeros((16, 128), F32), span1, span2]
+    recvs, spans = [next_state, pair], [jnp.zeros((16, 128), F32), span1, span2]
     recvs.append(lax.ppermute(pay, "seq", [(d, d ^ 4) for d in range(32)]))
     pay, state, total, span = call(
         lambda *refs: combine_kernel(2, *refs),
@@ -349,15 +348,16 @@
     )
     spans.append(span)
     recvs.append(lax.ppermute(pay, "seq", [(d, d ^ 28) for d in range(32)]))
-    (near,) = call(
-        near_kernel, [((WIDTH, TOK), F32)], local, *recvs[:4], *spans[:4], qt, cum, weight,
+    near, lift = call(
+        near_kernel, [((TOK, WIDTH), F32)] * 2,
+        local, *recvs[:4], *spans, qt, cum, weight, gate_values,
         flops=2 * 10**9, name="near",
     )
     theirs, feat, square = call(
-        project_kernel,
+        feature_kernel,
         [((128, WIDE), BF16), ((TOK, WIDTH), BF16), ((TOK, 128), F32)],
-        near, recvs[4], spans[4], qt, cum, weight, gate_values, norm_gain[None, :], out_weight,
-        flops=10**9, name="project",
+        near, lift, recvs[4], state_out, norm_gain[None, :], out_weight,
+        flops=10**9, name="feature",
     )
     (mine,) = call(own_rows_kernel, [((128, WIDE), BF16)], feat, square, out_weight, flops=10**9, name="own_rows")
     recv = lax.ppermute(theirs, "head", [(g, g ^ 1) for g in range(8)])

time: 55.1 us -> 54.3 us (0.985)
  waiting for transfers between devices: 20.5 us -> 19.4 us
    ppermute x3, waiting for transfers between devices: 3.8 us -> 2.86 us  [on_device(): lax.ppermute(pay, 'seq', [(d, d ^ k) for d in range(32)])]
    ppermute x1, starting transfers between devices: 1.72 us -> 2.53 us  [on_device(): recvs.append(lax.ppermute(pay, 'seq', [(d, d ^ 4) for d in range(32)]))]
where the time goes in v3:
time: 54.3 us; the launch traced here: 54.1 us
  starting transfers between devices  25.7 us (47%)
  waiting for transfers between devices  19.4 us (36%)
  Pallas kernels  8.22 us (15%)
  local copies, waits for them, and re-layouts  0.68 us (1%)
    pallas_call x10, Pallas kernels, call(): pl.pallas_call(kernel, out_shape=shapes, in_specs=specs, out_specs=[pl.Bl...  8.22 us
    ppermute x3, waiting for transfers between devices, on_device(): lax.ppermute(sends[k - 1], 'head', [(g, g ^ 2 * k) for g in range(8)])  7.7 us
    ppermute x1, starting transfers between devices, on_device(): recv = lax.ppermute(theirs, 'head', [(g, g ^ 1) for g in range(8)])  6.81 us
    ppermute x1, starting transfers between devices, on_device(): recvs.append(lax.ppermute(pay, 'seq', [(d, d ^ 28) for d in range(32)]))  4.58 us
    ppermute x1, starting transfers between devices, on_device(): recvs.append(lax.ppermute(pay, 'seq', [(d, d ^ 12) for d in range(32)]))  4.25 us
    ppermute x3, starting transfers between devices, on_device(): lax.ppermute(pay, 'seq', [(d, d ^ k) for d in range(32)])  4.06 us
    ppermute x3, starting transfers between devices, on_device(): lax.ppermute(sends[k - 1], 'head', [(g, g ^ 2 * k) for g in range(8)])  3.47 us
    ppermute x1, waiting for transfers between devices, on_device(): recvs.append(lax.ppermute(pay, 'seq', [(d, d ^ 12) for d in range(32)]))  2.89 us
  transfers between devices with their start and end apart: 10, of which 7 were waited for; matrix products, arithmetic and copies ran while one was open for 0% of the time, Pallas kernels for 8%

profile of v3, /device:TPU:1, one launch (start us, length us, event | category | flops | bytes accessed | tf_op | source)
XLA Modules:
  0.0 54.1 jit_solution(7797418781574792258)
XLA Ops:
  0.0 1.4 %state.1 = (bf16[672,128]{1,0:T(8,128)(2,1)S(1)}, f32[640,128]{1,0:T(8,128)S(1)}, bf16[640,256]{1,0:T(8,128)(2,1)S(1)}, f32[16,256]{1,0:T(8,128)S(1)}, f32[16,128]{1,0:T(8,128)S(1)}) custom-call(bf16[256,640]{1,0:T(8,128)(2,1)} %x_in.1, bf16[256,128]{1,0:T(8,128)(2,1)} %k_in.3, f32[10,256]{1,0:T(8,128)} %bitcast.6, f32[10,256]{1,0:T(8,128)} %bitcast.5), custom_call_target="tpu_custom_call" | custom-call | flops 100000000 | bytes 1000000 | tf_op jit(solution)/shard_map/state/pallas_call | solution.py:294
  1.4 3.4 %collective-permute-start = (bf16[672,128]{1,0:T(8,128)(2,1)S(1)}, bf16[672,128]{1,0:T(8,128)(2,1)S(1)}, u32[]{:S(2)}, u32[]{:S(2)}) collective-permute-start(bf16[672,128]{1,0:T(8,128)(2,1)S(1)} %get-tuple-element.37), channel_id=1, source_target_pairs={{0,24},{8,16},{16,8},{24,0},{32,56},{40,48},{48,40},{56,32},{64,88... | collective-permute-start | bytes 516104 | tf_op jit(solution)/shard_map/ppermute | solution.py:330
  4.8 0.5 collective-permute-start.1
  5.5 0.7 %copy-done.4 = f32[10]{0:T(128)S(1)} copy-done((f32[10]{0:T(128)S(1)}, f32[10]{0:T(128)}, u32[]{:S(2)}) %copy-start.4) | copy-done | bytes 64
  6.1 3.0 %local.1 = (f32[640,256]{1,0:T(8,128)S(1)}, bf16[128,256]{1,0:T(8,128)(2,1)S(1)}) custom-call(bf16[640,256]{1,0:T(8,128)(2,1)S(1)} %get-tuple-element.34.xt_ref, f32[16,256]{1,0:T(8,128)S(1)} %get-tuple-element.35.cum_ref, f32[10]{0:T(128)S(1)} %copy-done.4, bf16[256,128]{1,0:T(8,128)(2,1)} %k_in.3, bf16[256,128]{1,0:T(8,128)(2,1)} %q_ref.1, ...), custom_call_target="tpu_custom_call" | custom-call | flops 5000000000 | bytes 50000000 | tf_op jit(solution)/shard_map/local/pallas_call | solution.py:294
  9.2 2.9 %collective-permute-done.r3 = bf16[672,128]{1,0:T(8,128)(2,1)S(1)} collective-permute-done((bf16[672,128]{1,0:T(8,128)(2,1)S(1)}, bf16[672,128]{1,0:T(8,128)(2,1)S(1)}, u32[]{:S(2)}, u32[]{:S(2)}) %collective-permute-start) | collective-permute-done | bytes 172064 | tf_op jit(solution)/shard_map/ppermute | solution.py:330
  12.2 2.5 %collective-permute-start.3 = (bf16[672,128]{1,0:T(8,128)(2,1)S(1)}, bf16[672,128]{1,0:T(8,128)(2,1)S(1)}, u32[]{:S(2)}, u32[]{:S(2)}) collective-permute-start(bf16[672,128]{1,0:T(8,128)(2,1)S(1)} %get-tuple-element.42), channel_id=1, source_target_pairs={{0,32},{8,40},{16,48},{24,56},{32,0},{40,8},{48,16},{56,24},{64,96... | collective-permute-start | bytes 516104 | tf_op jit(solution)/shard_map/ppermute | solution.py:337
  14.7 2.8 %collective-permute-done.3.refs_3_.r2 = bf16[672,128]{1,0:T(8,128)(2,1)S(1)} collective-permute-done((bf16[672,128]{1,0:T(8,128)(2,1)S(1)}, bf16[672,128]{1,0:T(8,128)(2,1)S(1)}, u32[]{:S(2)}, u32[]{:S(2)}) %collective-permute-start.3) | collective-permute-done | bytes 172064 | tf_op jit(solution)/shard_map/ppermute | solution.py:337
  17.6 4.3 %collective-permute-start.4 = (bf16[672,128]{1,0:T(8,128)(2,1)S(1)}, bf16[672,128]{1,0:T(8,128)(2,1)S(1)}, u32[]{:S(2)}, u32[]{:S(2)}) collective-permute-start(bf16[672,128]{1,0:T(8,128)(2,1)S(1)} %get-tuple-element.46), channel_id=1, source_target_pairs={{0,96},{8,104},{16,112},{24,120},{32,64},{40,72},{48,80},{56,88},{... | collective-permute-start | bytes 516104 | tf_op jit(solution)/shard_map/ppermute | solution.py:344
  21.9 2.9 %collective-permute-done.4.recv_ref.r3 = bf16[672,128]{1,0:T(8,128)(2,1)S(1)} collective-permute-done((bf16[672,128]{1,0:T(8,128)(2,1)S(1)}, bf16[672,128]{1,0:T(8,128)(2,1)S(1)}, u32[]{:S(2)}, u32[]{:S(2)}) %collective-permute-start.4) | collective-permute-done | bytes 172064 | tf_op jit(solution)/shard_map/ppermute | solution.py:344
  24.8 4.6 %collective-permute-start.5 = (bf16[640,128]{1,0:T(8,128)(2,1)S(1)}, bf16[640,128]{1,0:T(8,128)(2,1)S(1)}, u32[]{:S(2)}, u32[]{:S(2)}) collective-permute-start(bf16[640,128]{1,0:T(8,128)(2,1)S(1)} %get-tuple-element.55), channel_id=1, source_target_pairs={{0,224},{8,232},{16,240},{24,248},{32,192},{40,200},{48,208},{56,2... | collective-permute-start | bytes 491528 | tf_op jit(solution)/shard_map/ppermute | solution.py:350
  29.4 0.7 %near.1 = (f32[256,640]{1,0:T(8,128)S(1)}, f32[256,640]{1,0:T(8,128)S(1)}) custom-call(f32[640,256]{1,0:T(8,128)S(1)} %get-tuple-element.36._.local_ref, bf16[640,128]{1,0:T(8,128)(2,1)S(1)} %get-tuple-element.40.r0, bf16[640,128]{1,0:T(8,128)(2,1)S(1)} %get-tuple-element.41.r1, bf16[672,128]{1,0:T(8,128)(2,1)S(1)} %collective-permute-done.3.refs_3_.r2, ...), custom_call_target="tpu_custom_call" | custom-call | flops 2000000000 | bytes 20000000 | tf_op jit(solution)/shard_map/near/pallas_call | solution.py:294
  30.1 2.1 %collective-permute-done.5.recv_ref = bf16[640,128]{1,0:T(8,128)(2,1)S(1)} collective-permute-done((bf16[640,128]{1,0:T(8,128)(2,1)S(1)}, bf16[640,128]{1,0:T(8,128)(2,1)S(1)}, u32[]{:S(2)}, u32[]{:S(2)}) %collective-permute-start.5) | collective-permute-done | bytes 163872 | tf_op jit(solution)/shard_map/ppermute | solution.py:350
  32.2 1.0 %feature.1 = (bf16[128,2688]{1,0:T(8,128)(2,1)S(1)}, bf16[256,640]{1,0:T(8,128)(2,1)S(1)}, f32[256,128]{1,0:T(8,128)S(1)}) custom-call(f32[256,640]{1,0:T(8,128)S(1)} %get-tuple-element.53.near_ref, f32[256,640]{1,0:T(8,128)S(1)} %get-tuple-element.54.lift_ref, bf16[640,128]{1,0:T(8,128)(2,1)S(1)} %collective-permute-done.5.recv_ref, ...), custom_call_target="tpu_custom_call" | custom-call | flops 1000000000 | bytes 10000000 | tf_op jit(solution)/shard_map/feature/pallas_call | solution.py:294
  33.2 6.8 %collective-permute-start.6 = (bf16[128,2688]{1,0:T(8,128)(2,1)S(1)}, bf16[128,2688]{1,0:T(8,128)(2,1)S(1)}, u32[]{:S(2)}, u32[]{:S(2)}) collective-permute-start(bf16[128,2688]{1,0:T(8,128)(2,1)S(1)} %get-tuple-element.58), channel_id=1, source_target_pairs={{0,1},{1,0},{2,3},{3,2},{4,5},{5,4},{6,7},{7,6},{8,9},{9,8},{10,11... | collective-permute-start | bytes 2064392 | tf_op jit(solution)/shard_map/ppermute | solution.py:363
  40.0 0.7 %own_rows.1.mine_ref = bf16[128,2688]{1,0:T(8,128)(2,1)S(1)} custom-call(bf16[256,640]{1,0:T(8,128)(2,1)S(1)} %get-tuple-element.56.feat_ref, f32[256,128]{1,0:T(8,128)S(1)} %get-tuple-element.57.square_ref, bf16[640,2560]{1,0:T(8,128)(2,1)S(1)} %copy-done), custom_call_target="tpu_custom_call" | custom-call | flops 1000000000 | bytes 10000000 | tf_op jit(solution)/shard_map/own_rows/pallas_call | solution.py:294
  40.7 1.1 %collective-permute-done.6.recv_ref = bf16[128,2688]{1,0:T(8,128)(2,1)S(1)} collective-permute-done((bf16[128,2688]{1,0:T(8,128)(2,1)S(1)}, bf16[128,2688]{1,0:T(8,128)(2,1)S(1)}, u32[]{:S(2)}, u32[]{:S(2)}) %collective-permute-start.6) | collective-permute-done | bytes 688160 | tf_op jit(solution)/shard_map/ppermute | solution.py:363
  41.7 0.3 pair.1
  42.1 2.8 %collective-permute-start.7 = (bf16[32,2688]{1,0:T(8,128)(2,1)S(1)}, bf16[32,2688]{1,0:T(8,128)(2,1)S(1)}, u32[]{:S(2)}, u32[]{:S(2)}) collective-permute-start(bf16[32,2688]{1,0:T(8,128)(2,1)S(1)} %get-tuple-element.60), channel_id=1, source_target_pairs={{0,6},{1,7},{2,4},{3,5},{4,2},{5,3},{6,0},{7,1},{8,14},{9,15},{10,... | collective-permute-start | bytes 516104 | tf_op jit(solution)/shard_map/ppermute | solution.py:369
  44.9 0.4 collective-permute-start.8
  45.2 0.3 collective-permute-start.9
  45.5 6.7 %collective-permute-done.7.r1 = bf16[32,2688]{1,0:T(8,128)(2,1)S(1)} collective-permute-done((bf16[32,2688]{1,0:T(8,128)(2,1)S(1)}, bf16[32,2688]{1,0:T(8,128)(2,1)S(1)}, u32[]{:S(2)}, u32[]{:S(2)}) %collective-permute-start.7) | collective-permute-done | bytes 172064 | tf_op jit(solution)/shard_map/ppermute | solution.py:369
  52.3 1.0 %collective-permute-done.9.r3 = bf16[32,2688]{1,0:T(8,128)(2,1)S(1)} collective-permute-done((bf16[32,2688]{1,0:T(8,128)(2,1)S(1)}, bf16[32,2688]{1,0:T(8,128)(2,1)S(1)}, u32[]{:S(2)}, u32[]{:S(2)}) %collective-permute-start.9) | collective-permute-done | bytes 172064 | tf_op jit(solution)/shard_map/ppermute | solution.py:369
  53.2 0.8 %final.1 = bf16[32,2560]{1,0:T(8,128)(2,1)} custom-call(f32[32,2688]{1,0:T(8,128)S(1)} %get-tuple-element.59.own_ref, bf16[32,2688]{1,0:T(8,128)(2,1)S(1)} %collective-permute-done.7.r1, bf16[32,2688]{1,0:T(8,128)(2,1)S(1)} %collective-permute-done.8.r2, bf16[32,2688]{1,0:T(8,128)(2,1)S(1)} %collective-permute-done.9.r3), custom_call_target="tpu_custom_call" | custom-call | flops 1000000 | bytes 10000 | tf_op jit(solution)/shard_map/final/pallas_call | solution.py:294
  (20 shorter events, 0.5 us)
Async XLA Ops:
  1.4 10.6 %collective-permute-start = (bf16[672,128]{1,0:T(8,128)(2,1)S(1)}, bf16[672,128]{1,0:T(8,128)(2,1)S(1)}, u32[]{:S(2)}, u32[]{:S(2)}) collective-permute-start(bf16[672,128]{1,0:T(8,128)(2,1)S(1)} %get-tuple-element.37), channel_id=1, source_target_pairs={{0,24},{8,16},{16,8},{24,0},{32,56},{40,48},{48,40},{56,32},{64,88... | collective-permute-start | bytes 516104 | tf_op jit(solution)/shard_map/ppermute | solution.py:330
  4.8 7.2 %collective-permute-start.1 = (bf16[672,128]{1,0:T(8,128)(2,1)S(1)}, bf16[672,128]{1,0:T(8,128)(2,1)S(1)}, u32[]{:S(2)}, u32[]{:S(2)}) collective-permute-start(bf16[672,128]{1,0:T(8,128)(2,1)S(1)} %get-tuple-element.37), channel_id=1, source_target_pairs={{0,16},{8,24},{16,0},{24,8},{32,48},{40,56},{48,32},{56,40},{64,80... | collective-permute-start | bytes 516104 | tf_op jit(solution)/shard_map/ppermute | solution.py:330
  5.3 6.7 %collective-permute-start.2 = (bf16[672,128]{1,0:T(8,128)(2,1)S(1)}, bf16[672,128]{1,0:T(8,128)(2,1)S(1)}, u32[]{:S(2)}, u32[]{:S(2)}) collective-permute-start(bf16[672,128]{1,0:T(8,128)(2,1)S(1)} %get-tuple-element.37), channel_id=1, source_target_pairs={{0,8},{8,0},{16,24},{24,16},{32,40},{40,32},{48,56},{56,48},{64,72... | collective-permute-start | bytes 516104 | tf_op jit(solution)/shard_map/ppermute | solution.py:330
  5.5 0.7 %copy-start.4 = (f32[10]{0:T(128)S(1)}, f32[10]{0:T(128)}, u32[]{:S(2)}) copy-start(f32[10]{0:T(128)} %skip_ref.1) | copy-start | bytes 124
  6.1 15.7 %copy-start.5 = (f32[640]{0:T(1024)S(1)}, f32[640]{0:T(1024)}, u32[]{:S(2)}) copy-start(f32[640]{0:T(1024)} %param.18) | copy-start | bytes 7684
  6.1 23.3 %copy-start.2 = (bf16[256,640]{1,0:T(8,128)(2,1)S(1)}, bf16[256,640]{1,0:T(8,128)(2,1)}, u32[]{:S(2)}) copy-start(bf16[256,640]{1,0:T(8,128)(2,1)} %gate_ref.1) | copy-start | bytes 983044
  6.1 23.3 %copy-start.3 = (bf16[256,10,14]{0,2,1:T(8,128)(2,1)S(1)}, bf16[256,10,14]{0,2,1:T(8,128)(2,1)}, u32[]{:S(2)}) copy-start(bf16[256,10,14]{0,2,1:T(8,128)(2,1)} %param.16) | copy-start | bytes 215044
  12.2 5.3 %collective-permute-start.3 = (bf16[672,128]{1,0:T(8,128)(2,1)S(1)}, bf16[672,128]{1,0:T(8,128)(2,1)S(1)}, u32[]{:S(2)}, u32[]{:S(2)}) collective-permute-start(bf16[672,128]{1,0:T(8,128)(2,1)S(1)} %get-tuple-element.42), channel_id=1, source_target_pairs={{0,32},{8,40},{16,48},{24,56},{32,0},{40,8},{48,16},{56,24},{64,96... | collective-permute-start | bytes 516104 | tf_op jit(solution)/shard_map/ppermute | solution.py:337
  17.6 7.2 %collective-permute-start.4 = (bf16[672,128]{1,0:T(8,128)(2,1)S(1)}, bf16[672,128]{1,0:T(8,128)(2,1)S(1)}, u32[]{:S(2)}, u32[]{:S(2)}) collective-permute-start(bf16[672,128]{1,0:T(8,128)(2,1)S(1)} %get-tuple-element.46), channel_id=1, source_target_pairs={{0,96},{8,104},{16,112},{24,120},{32,64},{40,72},{48,80},{56,88},{... | collective-permute-start | bytes 516104 | tf_op jit(solution)/shard_map/ppermute | solution.py:344
  24.8 7.4 %collective-permute-start.5 = (bf16[640,128]{1,0:T(8,128)(2,1)S(1)}, bf16[640,128]{1,0:T(8,128)(2,1)S(1)}, u32[]{:S(2)}, u32[]{:S(2)}) collective-permute-start(bf16[640,128]{1,0:T(8,128)(2,1)S(1)} %get-tuple-element.55), channel_id=1, source_target_pairs={{0,224},{8,232},{16,240},{24,248},{32,192},{40,200},{48,208},{56,2... | collective-permute-start | bytes 491528 | tf_op jit(solution)/shard_map/ppermute | solution.py:350
  29.4 2.8 %copy-start = (bf16[640,2560]{1,0:T(8,128)(2,1)S(1)}, bf16[640,2560]{1,0:T(8,128)(2,1)}, u32[]{:S(2)}) copy-start(bf16[640,2560]{1,0:T(8,128)(2,1)} %ow_ref.3) | copy-start | bytes 9830404
  29.4 2.8 %copy-start.1 = (bf16[256,128]{1,0:T(8,128)(2,1)S(1)}, bf16[256,128]{1,0:T(8,128)(2,1)}, u32[]{:S(2)}) copy-start(bf16[256,128]{1,0:T(8,128)(2,1)} %q_ref.1) | copy-start | bytes 196612
  33.2 8.6 %collective-permute-start.6 = (bf16[128,2688]{1,0:T(8,128)(2,1)S(1)}, bf16[128,2688]{1,0:T(8,128)(2,1)S(1)}, u32[]{:S(2)}, u32[]{:S(2)}) collective-permute-start(bf16[128,2688]{1,0:T(8,128)(2,1)S(1)} %get-tuple-element.58), channel_id=1, source_target_pairs={{0,1},{1,0},{2,3},{3,2},{4,5},{5,4},{6,7},{7,6},{8,9},{9,8},{10,11... | collective-permute-start | bytes 2064392 | tf_op jit(solution)/shard_map/ppermute | solution.py:363
  42.1 10.2 %collective-permute-start.7 = (bf16[32,2688]{1,0:T(8,128)(2,1)S(1)}, bf16[32,2688]{1,0:T(8,128)(2,1)S(1)}, u32[]{:S(2)}, u32[]{:S(2)}) collective-permute-start(bf16[32,2688]{1,0:T(8,128)(2,1)S(1)} %get-tuple-element.60), channel_id=1, source_target_pairs={{0,6},{1,7},{2,4},{3,5},{4,2},{5,3},{6,0},{7,1},{8,14},{9,15},{10,... | collective-permute-start | bytes 516104 | tf_op jit(solution)/shard_map/ppermute | solution.py:369
  44.9 7.4 %collective-permute-start.8 = (bf16[32,2688]{1,0:T(8,128)(2,1)S(1)}, bf16[32,2688]{1,0:T(8,128)(2,1)S(1)}, u32[]{:S(2)}, u32[]{:S(2)}) collective-permute-start(bf16[32,2688]{1,0:T(8,128)(2,1)S(1)} %get-tuple-element.61), channel_id=1, source_target_pairs={{0,4},{1,5},{2,6},{3,7},{4,0},{5,1},{6,2},{7,3},{8,12},{9,13},{10,... | collective-permute-start | bytes 516104 | tf_op jit(solution)/shard_map/ppermute | solution.py:369
  45.2 8.0 %collective-permute-start.9 = (bf16[32,2688]{1,0:T(8,128)(2,1)S(1)}, bf16[32,2688]{1,0:T(8,128)(2,1)S(1)}, u32[]{:S(2)}, u32[]{:S(2)}) collective-permute-start(bf16[32,2688]{1,0:T(8,128)(2,1)S(1)} %get-tuple-element.62), channel_id=1, source_target_pairs={{0,2},{1,3},{2,0},{3,1},{4,6},{5,7},{6,4},{7,5},{8,10},{9,11},{10,... | collective-permute-start | bytes 516104 | tf_op jit(solution)/shard_map/ppermute | solution.py:369

commit v4 on v3

--- a/solution.py
+++ b/solution.py
@@ -225,7 +225,7 @@
         lift_ref[:, cols] = jnp.concatenate(lifts, axis=0).T * gate
 
 
-def feature_kernel(near_ref, lift_ref, recv_ref, q_ref, gain_ref, ow_ref, theirs_ref, feat_ref, square_ref):
+def feature_kernel(near_ref, lift_ref, recv_ref, q_ref, gain_ref, ow_ref, first_ref, second_ref, feat_ref, square_ref):
     query = q_ref[...]
     squares = jnp.zeros((TOK, 1), F32)
     for j in range(WIDTH // 128):
@@ -235,34 +235,37 @@
         squares = squares + jnp.sum(gated * gated, axis=1, keepdims=True)
         feat_ref[:, cols] = (gated * gain_ref[:, cols]).astype(BF16)
     square_ref[...] = jnp.broadcast_to(squares, (TOK, 128))
-    product_rows(feat_ref, square_ref, ow_ref, theirs_ref, 1 - (lax.axis_index("head") & 1))
-
-
-def product_rows(feat_ref, square_ref, ow_ref, out_ref, side):
+    product_rows(feat_ref, square_ref, ow_ref, first_ref, second_ref, 1 - (lax.axis_index("head") & 1))
+
+
+def product_rows(feat_ref, square_ref, ow_ref, first_ref, second_ref, side):
+    y = lax.axis_index("head") >> 1
     lane = lax.broadcasted_iota(jnp.int32, (32, 128), 1)
-    starts = [pl.multiple_of((2 * y + side) * 32, 32) for y in range(4)]
+    starts = [pl.multiple_of((2 * jnp.bitwise_xor(y, k) + side) * 32, 32) for k in (3, 2, 1, 0)]
     rows = jnp.concatenate([feat_ref[pl.ds(s, 32), :] for s in starts], axis=0)
-    out_ref[:, 0:DM] = dot(rows, ow_ref[...]).astype(BF16)
-    for y, s in enumerate(starts):
+    product = dot(rows, ow_ref[...]).astype(BF16)
+    first_ref[:, 0:DM] = product[0:64]
+    second_ref[:, 0:DM] = product[64:128]
+    for i, s in enumerate(starts):
         high, low = split_two(square_ref[pl.ds(s, 32), :])
-        out_ref[y * 32 : (y + 1) * 32, DM:WIDE] = jnp.where(
+        out_ref = first_ref if i < 2 else second_ref
+        out_ref[(i % 2) * 32 : (i % 2 + 1) * 32, DM:WIDE] = jnp.where(
             lane < 64, high.astype(F32), low.astype(F32)
         ).astype(BF16)
 
 
-def own_rows_kernel(feat_ref, square_ref, ow_ref, mine_ref):
-    product_rows(feat_ref, square_ref, ow_ref, mine_ref, lax.axis_index("head") & 1)
+def own_rows_kernel(feat_ref, square_ref, ow_ref, first_ref, second_ref):
+    product_rows(feat_ref, square_ref, ow_ref, first_ref, second_ref, lax.axis_index("head") & 1)
 
 
 def squares_at(ref, rows, at):
     return ref[rows, at : at + 1].astype(F32) + ref[rows, at + 64 : at + 65].astype(F32)
 
 
-def pair_kernel(mine_ref, recv_ref, own_ref, o1, o2, o3):
-    y = lax.axis_index("head") >> 1
+def pair_kernel(mine_ref, recv_ref, *out_refs):
     lane = lax.broadcasted_iota(jnp.int32, (32, 128), 1)
-    for k, out_ref in enumerate((own_ref, o1, o2, o3)):
-        rows = pl.ds(pl.multiple_of(jnp.bitwise_xor(y, k) * 32, 32), 32)
+    for i, out_ref in enumerate(out_refs):
+        rows = slice(i * 32, (i + 1) * 32)
         total = mine_ref[rows, 0:DM].astype(F32) + recv_ref[rows, 0:DM].astype(F32)
         out_ref[:, 0:DM] = total.astype(out_ref.dtype)
         square = jnp.broadcast_to(squares_at(mine_ref, rows, DM) + squares_at(recv_ref, rows, DM), (32, 128))
@@ -353,20 +356,23 @@
         local, *recvs[:4], *spans, qt, cum, weight, gate_values,
         flops=2 * 10**9, name="near",
     )
-    theirs, feat, square = call(
+    half = ((64, WIDE), BF16)
+    *theirs, feat, square = call(
         feature_kernel,
-        [((128, WIDE), BF16), ((TOK, WIDTH), BF16), ((TOK, 128), F32)],
+        [half, half, ((TOK, WIDTH), BF16), ((TOK, 128), F32)],
         near, lift, recvs[4], state_out, norm_gain[None, :], out_weight,
         flops=10**9, name="feature",
     )
-    (mine,) = call(own_rows_kernel, [((128, WIDE), BF16)], feat, square, out_weight, flops=10**9, name="own_rows")
-    recv = lax.ppermute(theirs, "head", [(g, g ^ 1) for g in range(8)])
-    own, *sends = call(
-        pair_kernel,
-        [((32, WIDE), F32)] + [((32, WIDE), BF16)] * 3,
-        mine, recv, flops=10**6, name="pair",
-    )
-    got = [lax.ppermute(sends[k - 1], "head", [(g, g ^ (2 * k)) for g in range(8)]) for k in (3, 2, 1)]
+    mine = call(own_rows_kernel, [half, half], feat, square, out_weight, flops=10**9, name="own_rows")
+    swap = [(g, g ^ 1) for g in range(8)]
+    recv = [lax.ppermute(part, "head", swap) for part in theirs]
+    one = ((32, WIDE), BF16)
+    send3, send2 = call(pair_kernel, [one, one], mine[0], recv[0], flops=10**6, name="pair")
+    send1, own = call(pair_kernel, [one, ((32, WIDE), F32)], mine[1], recv[1], flops=10**6, name="pair")
+    got = [
+        lax.ppermute(send, "head", [(g, g ^ (2 * k)) for g in range(8)])
+        for k, send in ((3, send3), (2, send2), (1, send1))
+    ]
     (out,) = call(final_kernel, [((32, DM), BF16)], own, *got, flops=10**6, name="final")
     return out
 

time: 54.3 us -> 53.7 us (0.989)
  waiting for transfers between devices: 19.4 us -> 18.5 us
    ppermute x4 -> x5, waiting for transfers between devices: 8.79 us -> 7.93 us  [the longest x3 7.43 us: on_device(): lax.ppermute(send, 'head', [(g, g ^ 2 * k) for g in range(8)])]
    ppermute x4 -> x5, starting transfers between devices: 10.3 us -> 10.5 us  [the longest x2 6.91 us: on_device(): recv = [lax.ppermute(part, 'head', swap) for part in theirs]]
    pallas_call x10 -> x11, Pallas kernels: 8.22 us -> 8.26 us  [call(): pl.pallas_call(kernel, out_shape=shapes, in_specs=specs, out_specs=[pl.Bl...]
  transfers between devices with their start and end apart: 10 -> 11, of which waited for: 7 -> 7; matrix products, arithmetic and copies ran while one was open for 0% -> 0% of each run, Pallas kernels for 8% -> 9%
where the time goes in v4:
time: 53.7 us; the launch traced here: 53.5 us
  starting transfers between devices  25.9 us (48%)
  waiting for transfers between devices  18.5 us (34%)
  Pallas kernels  8.26 us (15%)
  local copies, waits for them, and re-layouts  0.68 us (1%)
    pallas_call x11, Pallas kernels, call(): pl.pallas_call(kernel, out_shape=shapes, in_specs=specs, out_specs=[pl.Bl...  8.26 us
    ppermute x3, waiting for transfers between devices, on_device(): lax.ppermute(send, 'head', [(g, g ^ 2 * k) for g in range(8)])  7.43 us
    ppermute x2, starting transfers between devices, on_device(): recv = [lax.ppermute(part, 'head', swap) for part in theirs]  6.91 us
    ppermute x1, starting transfers between devices, on_device(): recvs.append(lax.ppermute(pay, 'seq', [(d, d ^ 28) for d in range(32)]))  4.58 us
    ppermute x1, starting transfers between devices, on_device(): recvs.append(lax.ppermute(pay, 'seq', [(d, d ^ 12) for d in range(32)]))  4.25 us
    ppermute x3, starting transfers between devices, on_device(): lax.ppermute(pay, 'seq', [(d, d ^ k) for d in range(32)])  4.06 us
    ppermute x3, starting transfers between devices, on_device(): lax.ppermute(send, 'head', [(g, g ^ 2 * k) for g in range(8)])  3.58 us
    ppermute x1, waiting for transfers between devices, on_device(): recvs.append(lax.ppermute(pay, 'seq', [(d, d ^ 12) for d in range(32)]))  2.89 us
  transfers between devices with their start and end apart: 11, of which 7 were waited for; matrix products, arithmetic and copies ran while one was open for 0% of the time, Pallas kernels for 9%

profile of v4, /device:TPU:1, one launch (start us, length us, event | category | flops | bytes accessed | tf_op | source)
XLA Modules:
  0.0 53.5 jit_solution(8276716431062665866)
XLA Ops:
  0.0 1.4 %state.1 = (bf16[672,128]{1,0:T(8,128)(2,1)S(1)}, f32[640,128]{1,0:T(8,128)S(1)}, bf16[640,256]{1,0:T(8,128)(2,1)S(1)}, f32[16,256]{1,0:T(8,128)S(1)}, f32[16,128]{1,0:T(8,128)S(1)}) custom-call(bf16[256,640]{1,0:T(8,128)(2,1)} %x_in.1, bf16[256,128]{1,0:T(8,128)(2,1)} %k_in.3, f32[10,256]{1,0:T(8,128)} %bitcast.6, f32[10,256]{1,0:T(8,128)} %bitcast.5), custom_call_target="tpu_custom_call" | custom-call | flops 100000000 | bytes 1000000 | tf_op jit(solution)/shard_map/state/pallas_call | solution.py:297
  1.4 3.4 %collective-permute-start = (bf16[672,128]{1,0:T(8,128)(2,1)S(1)}, bf16[672,128]{1,0:T(8,128)(2,1)S(1)}, u32[]{:S(2)}, u32[]{:S(2)}) collective-permute-start(bf16[672,128]{1,0:T(8,128)(2,1)S(1)} %get-tuple-element.40), channel_id=1, source_target_pairs={{0,24},{8,16},{16,8},{24,0},{32,56},{40,48},{48,40},{56,32},{64,88... | collective-permute-start | bytes 516104 | tf_op jit(solution)/shard_map/ppermute | solution.py:333
  4.8 0.5 collective-permute-start.1
  5.5 0.7 %copy-done.4 = f32[10]{0:T(128)S(1)} copy-done((f32[10]{0:T(128)S(1)}, f32[10]{0:T(128)}, u32[]{:S(2)}) %copy-start.4) | copy-done | bytes 64
  6.1 3.0 %local.1 = (f32[640,256]{1,0:T(8,128)S(1)}, bf16[128,256]{1,0:T(8,128)(2,1)S(1)}) custom-call(bf16[640,256]{1,0:T(8,128)(2,1)S(1)} %get-tuple-element.37.xt_ref, f32[16,256]{1,0:T(8,128)S(1)} %get-tuple-element.38.cum_ref, f32[10]{0:T(128)S(1)} %copy-done.4, bf16[256,128]{1,0:T(8,128)(2,1)} %k_in.3, bf16[256,128]{1,0:T(8,128)(2,1)} %q_ref.1, ...), custom_call_target="tpu_custom_call" | custom-call | flops 5000000000 | bytes 50000000 | tf_op jit(solution)/shard_map/local/pallas_call | solution.py:297
  9.2 2.9 %collective-permute-done.r3 = bf16[672,128]{1,0:T(8,128)(2,1)S(1)} collective-permute-done((bf16[672,128]{1,0:T(8,128)(2,1)S(1)}, bf16[672,128]{1,0:T(8,128)(2,1)S(1)}, u32[]{:S(2)}, u32[]{:S(2)}) %collective-permute-start) | collective-permute-done | bytes 172064 | tf_op jit(solution)/shard_map/ppermute | solution.py:333
  12.2 2.5 %collective-permute-start.3 = (bf16[672,128]{1,0:T(8,128)(2,1)S(1)}, bf16[672,128]{1,0:T(8,128)(2,1)S(1)}, u32[]{:S(2)}, u32[]{:S(2)}) collective-permute-start(bf16[672,128]{1,0:T(8,128)(2,1)S(1)} %get-tuple-element.45), channel_id=1, source_target_pairs={{0,32},{8,40},{16,48},{24,56},{32,0},{40,8},{48,16},{56,24},{64,96... | collective-permute-start | bytes 516104 | tf_op jit(solution)/shard_map/ppermute | solution.py:340
  14.7 2.8 %collective-permute-done.3.refs_3_.r2 = bf16[672,128]{1,0:T(8,128)(2,1)S(1)} collective-permute-done((bf16[672,128]{1,0:T(8,128)(2,1)S(1)}, bf16[672,128]{1,0:T(8,128)(2,1)S(1)}, u32[]{:S(2)}, u32[]{:S(2)}) %collective-permute-start.3) | collective-permute-done | bytes 172064 | tf_op jit(solution)/shard_map/ppermute | solution.py:340
  17.6 4.3 %collective-permute-start.4 = (bf16[672,128]{1,0:T(8,128)(2,1)S(1)}, bf16[672,128]{1,0:T(8,128)(2,1)S(1)}, u32[]{:S(2)}, u32[]{:S(2)}) collective-permute-start(bf16[672,128]{1,0:T(8,128)(2,1)S(1)} %get-tuple-element.49), channel_id=1, source_target_pairs={{0,96},{8,104},{16,112},{24,120},{32,64},{40,72},{48,80},{56,88},{... | collective-permute-start | bytes 516104 | tf_op jit(solution)/shard_map/ppermute | solution.py:347
  21.9 2.9 %collective-permute-done.4.recv_ref.r3 = bf16[672,128]{1,0:T(8,128)(2,1)S(1)} collective-permute-done((bf16[672,128]{1,0:T(8,128)(2,1)S(1)}, bf16[672,128]{1,0:T(8,128)(2,1)S(1)}, u32[]{:S(2)}, u32[]{:S(2)}) %collective-permute-start.4) | collective-permute-done | bytes 172064 | tf_op jit(solution)/shard_map/ppermute | solution.py:347
  24.8 4.6 %collective-permute-start.5 = (bf16[640,128]{1,0:T(8,128)(2,1)S(1)}, bf16[640,128]{1,0:T(8,128)(2,1)S(1)}, u32[]{:S(2)}, u32[]{:S(2)}) collective-permute-start(bf16[640,128]{1,0:T(8,128)(2,1)S(1)} %get-tuple-element.58), channel_id=1, source_target_pairs={{0,224},{8,232},{16,240},{24,248},{32,192},{40,200},{48,208},{56,2... | collective-permute-start | bytes 491528 | tf_op jit(solution)/shard_map/ppermute | solution.py:353
  29.4 0.7 %near.1 = (f32[256,640]{1,0:T(8,128)S(1)}, f32[256,640]{1,0:T(8,128)S(1)}) custom-call(f32[640,256]{1,0:T(8,128)S(1)} %get-tuple-element.39._.local_ref, bf16[640,128]{1,0:T(8,128)(2,1)S(1)} %get-tuple-element.43.r0, bf16[640,128]{1,0:T(8,128)(2,1)S(1)} %get-tuple-element.44.r1, bf16[672,128]{1,0:T(8,128)(2,1)S(1)} %collective-permute-done.3.refs_3_.r2, ...), custom_call_target="tpu_custom_call" | custom-call | flops 2000000000 | bytes 20000000 | tf_op jit(solution)/shard_map/near/pallas_call | solution.py:297
  30.1 2.1 %collective-permute-done.5.recv_ref = bf16[640,128]{1,0:T(8,128)(2,1)S(1)} collective-permute-done((bf16[640,128]{1,0:T(8,128)(2,1)S(1)}, bf16[640,128]{1,0:T(8,128)(2,1)S(1)}, u32[]{:S(2)}, u32[]{:S(2)}) %collective-permute-start.5) | collective-permute-done | bytes 163872 | tf_op jit(solution)/shard_map/ppermute | solution.py:353
  32.2 1.0 %feature.1 = (bf16[64,2688]{1,0:T(8,128)(2,1)S(1)}, bf16[64,2688]{1,0:T(8,128)(2,1)S(1)}, bf16[256,640]{1,0:T(8,128)(2,1)S(1)}, f32[256,128]{1,0:T(8,128)S(1)}) custom-call(f32[256,640]{1,0:T(8,128)S(1)} %get-tuple-element.56.near_ref, f32[256,640]{1,0:T(8,128)S(1)} %get-tuple-element.57.lift_ref, bf16[640,128]{1,0:T(8,128)(2,1)S(1)} %collective-permute-done.5.recv_ref, ...), custom_call_target="tpu_custom_call" | custom-call | flops 1000000000 | bytes 10000000 | tf_op jit(solution)/shard_map/feature/pallas_call | solution.py:297
  33.2 6.8 %collective-permute-start.7 = (bf16[64,2688]{1,0:T(8,128)(2,1)S(1)}, bf16[64,2688]{1,0:T(8,128)(2,1)S(1)}, u32[]{:S(2)}, u32[]{:S(2)}) collective-permute-start(bf16[64,2688]{1,0:T(8,128)(2,1)S(1)} %get-tuple-element.65), channel_id=1, source_target_pairs={{0,1},{1,0},{2,3},{3,2},{4,5},{5,4},{6,7},{7,6},{8,9},{9,8},{10,11... | collective-permute-start | bytes 1032200 | tf_op jit(solution)/shard_map/ppermute | solution.py:368
  40.1 0.7 %own_rows.1 = (bf16[64,2688]{1,0:T(8,128)(2,1)S(1)}, bf16[64,2688]{1,0:T(8,128)(2,1)S(1)}) custom-call(bf16[256,640]{1,0:T(8,128)(2,1)S(1)} %get-tuple-element.59.feat_ref, f32[256,128]{1,0:T(8,128)S(1)} %get-tuple-element.60.square_ref, bf16[640,2560]{1,0:T(8,128)(2,1)S(1)} %copy-done), custom_call_target="tpu_custom_call" | custom-call | flops 1000000000 | bytes 10000000 | tf_op jit(solution)/shard_map/own_rows/pallas_call | solution.py:297
  40.8 0.5 collective-permute-done.7.recv_ref
  41.3 0.2 pair.3
  41.5 2.8 %collective-permute-start.8 = (bf16[32,2688]{1,0:T(8,128)(2,1)S(1)}, bf16[32,2688]{1,0:T(8,128)(2,1)S(1)}, u32[]{:S(2)}, u32[]{:S(2)}) collective-permute-start(bf16[32,2688]{1,0:T(8,128)(2,1)S(1)} %get-tuple-element.66), channel_id=1, source_target_pairs={{0,6},{1,7},{2,4},{3,5},{4,2},{5,3},{6,0},{7,1},{8,14},{9,15},{10,... | collective-permute-start | bytes 516104 | tf_op jit(solution)/shard_map/ppermute | solution.py:373
  44.3 0.4 collective-permute-start.9
  44.8 0.4 collective-permute-start.10
  45.2 6.4 %collective-permute-done.8.r1 = bf16[32,2688]{1,0:T(8,128)(2,1)S(1)} collective-permute-done((bf16[32,2688]{1,0:T(8,128)(2,1)S(1)}, bf16[32,2688]{1,0:T(8,128)(2,1)S(1)}, u32[]{:S(2)}, u32[]{:S(2)}) %collective-permute-start.8) | collective-permute-done | bytes 172064 | tf_op jit(solution)/shard_map/ppermute | solution.py:373
  51.7 1.0 %collective-permute-done.10.r3 = bf16[32,2688]{1,0:T(8,128)(2,1)S(1)} collective-permute-done((bf16[32,2688]{1,0:T(8,128)(2,1)S(1)}, bf16[32,2688]{1,0:T(8,128)(2,1)S(1)}, u32[]{:S(2)}, u32[]{:S(2)}) %collective-permute-start.10) | collective-permute-done | bytes 172064 | tf_op jit(solution)/shard_map/ppermute | solution.py:373
  52.6 0.8 %final.1 = bf16[32,2560]{1,0:T(8,128)(2,1)} custom-call(f32[32,2688]{1,0:T(8,128)S(1)} %get-tuple-element.63.own_ref, bf16[32,2688]{1,0:T(8,128)(2,1)S(1)} %collective-permute-done.8.r1, bf16[32,2688]{1,0:T(8,128)(2,1)S(1)} %collective-permute-done.9.r2, bf16[32,2688]{1,0:T(8,128)(2,1)S(1)} %collective-permute-done.10.r3), custom_call_target="tpu_custom_call" | custom-call | flops 1000000 | bytes 10000 | tf_op jit(solution)/shard_map/final/pallas_call | solution.py:297
  (23 shorter events, 0.8 us)
Async XLA Ops:
  1.4 10.6 %collective-permute-start = (bf16[672,128]{1,0:T(8,128)(2,1)S(1)}, bf16[672,128]{1,0:T(8,128)(2,1)S(1)}, u32[]{:S(2)}, u32[]{:S(2)}) collective-permute-start(bf16[672,128]{1,0:T(8,128)(2,1)S(1)} %get-tuple-element.40), channel_id=1, source_target_pairs={{0,24},{8,16},{16,8},{24,0},{32,56},{40,48},{48,40},{56,32},{64,88... | collective-permute-start | bytes 516104 | tf_op jit(solution)/shard_map/ppermute | solution.py:333
  4.8 7.2 %collective-permute-start.1 = (bf16[672,128]{1,0:T(8,128)(2,1)S(1)}, bf16[672,128]{1,0:T(8,128)(2,1)S(1)}, u32[]{:S(2)}, u32[]{:S(2)}) collective-permute-start(bf16[672,128]{1,0:T(8,128)(2,1)S(1)} %get-tuple-element.40), channel_id=1, source_target_pairs={{0,16},{8,24},{16,0},{24,8},{32,48},{40,56},{48,32},{56,40},{64,80... | collective-permute-start | bytes 516104 | tf_op jit(solution)/shard_map/ppermute | solution.py:333
  5.3 6.7 %collective-permute-start.2 = (bf16[672,128]{1,0:T(8,128)(2,1)S(1)}, bf16[672,128]{1,0:T(8,128)(2,1)S(1)}, u32[]{:S(2)}, u32[]{:S(2)}) collective-permute-start(bf16[672,128]{1,0:T(8,128)(2,1)S(1)} %get-tuple-element.40), channel_id=1, source_target_pairs={{0,8},{8,0},{16,24},{24,16},{32,40},{40,32},{48,56},{56,48},{64,72... | collective-permute-start | bytes 516104 | tf_op jit(solution)/shard_map/ppermute | solution.py:333
  5.5 0.7 %copy-start.4 = (f32[10]{0:T(128)S(1)}, f32[10]{0:T(128)}, u32[]{:S(2)}) copy-start(f32[10]{0:T(128)} %skip_ref.1) | copy-start | bytes 124
  6.1 15.7 %copy-start.5 = (f32[640]{0:T(1024)S(1)}, f32[640]{0:T(1024)}, u32[]{:S(2)}) copy-start(f32[640]{0:T(1024)} %param.18) | copy-start | bytes 7684
  6.1 23.3 %copy-start.2 = (bf16[256,640]{1,0:T(8,128)(2,1)S(1)}, bf16[256,640]{1,0:T(8,128)(2,1)}, u32[]{:S(2)}) copy-start(bf16[256,640]{1,0:T(8,128)(2,1)} %gate_ref.1) | copy-start | bytes 983044
  6.1 23.3 %copy-start.3 = (bf16[256,10,14]{0,2,1:T(8,128)(2,1)S(1)}, bf16[256,10,14]{0,2,1:T(8,128)(2,1)}, u32[]{:S(2)}) copy-start(bf16[256,10,14]{0,2,1:T(8,128)(2,1)} %param.16) | copy-start | bytes 215044
  12.2 5.3 %collective-permute-start.3 = (bf16[672,128]{1,0:T(8,128)(2,1)S(1)}, bf16[672,128]{1,0:T(8,128)(2,1)S(1)}, u32[]{:S(2)}, u32[]{:S(2)}) collective-permute-start(bf16[672,128]{1,0:T(8,128)(2,1)S(1)} %get-tuple-element.45), channel_id=1, source_target_pairs={{0,32},{8,40},{16,48},{24,56},{32,0},{40,8},{48,16},{56,24},{64,96... | collective-permute-start | bytes 516104 | tf_op jit(solution)/shard_map/ppermute | solution.py:340
  17.6 7.2 %collective-permute-start.4 = (bf16[672,128]{1,0:T(8,128)(2,1)S(1)}, bf16[672,128]{1,0:T(8,128)(2,1)S(1)}, u32[]{:S(2)}, u32[]{:S(2)}) collective-permute-start(bf16[672,128]{1,0:T(8,128)(2,1)S(1)} %get-tuple-element.49), channel_id=1, source_target_pairs={{0,96},{8,104},{16,112},{24,120},{32,64},{40,72},{48,80},{56,88},{... | collective-permute-start | bytes 516104 | tf_op jit(solution)/shard_map/ppermute | solution.py:347
  24.8 7.4 %collective-permute-start.5 = (bf16[640,128]{1,0:T(8,128)(2,1)S(1)}, bf16[640,128]{1,0:T(8,128)(2,1)S(1)}, u32[]{:S(2)}, u32[]{:S(2)}) collective-permute-start(bf16[640,128]{1,0:T(8,128)(2,1)S(1)} %get-tuple-element.58), channel_id=1, source_target_pairs={{0,224},{8,232},{16,240},{24,248},{32,192},{40,200},{48,208},{56,2... | collective-permute-start | bytes 491528 | tf_op jit(solution)/shard_map/ppermute | solution.py:353
  29.4 2.8 %copy-start = (bf16[640,2560]{1,0:T(8,128)(2,1)S(1)}, bf16[640,2560]{1,0:T(8,128)(2,1)}, u32[]{:S(2)}) copy-start(bf16[640,2560]{1,0:T(8,128)(2,1)} %ow_ref.3) | copy-start | bytes 9830404
  29.4 2.8 %copy-start.1 = (bf16[256,128]{1,0:T(8,128)(2,1)S(1)}, bf16[256,128]{1,0:T(8,128)(2,1)}, u32[]{:S(2)}) copy-start(bf16[256,128]{1,0:T(8,128)(2,1)} %q_ref.1) | copy-start | bytes 196612
  33.2 8.1 %collective-permute-start.7 = (bf16[64,2688]{1,0:T(8,128)(2,1)S(1)}, bf16[64,2688]{1,0:T(8,128)(2,1)S(1)}, u32[]{:S(2)}, u32[]{:S(2)}) collective-permute-start(bf16[64,2688]{1,0:T(8,128)(2,1)S(1)} %get-tuple-element.65), channel_id=1, source_target_pairs={{0,1},{1,0},{2,3},{3,2},{4,5},{5,4},{6,7},{7,6},{8,9},{9,8},{10,11... | collective-permute-start | bytes 1032200 | tf_op jit(solution)/shard_map/ppermute | solution.py:368
  40.0 4.6 %collective-permute-start.6 = (bf16[64,2688]{1,0:T(8,128)(2,1)S(1)}, bf16[64,2688]{1,0:T(8,128)(2,1)S(1)}, u32[]{:S(2)}, u32[]{:S(2)}) collective-permute-start(bf16[64,2688]{1,0:T(8,128)(2,1)S(1)} %get-tuple-element.62), channel_id=1, source_target_pairs={{0,1},{1,0},{2,3},{3,2},{4,5},{5,4},{6,7},{7,6},{8,9},{9,8},{10,11... | collective-permute-start | bytes 1032200 | tf_op jit(solution)/shard_map/ppermute | solution.py:368
  41.5 10.2 %collective-permute-start.8 = (bf16[32,2688]{1,0:T(8,128)(2,1)S(1)}, bf16[32,2688]{1,0:T(8,128)(2,1)S(1)}, u32[]{:S(2)}, u32[]{:S(2)}) collective-permute-start(bf16[32,2688]{1,0:T(8,128)(2,1)S(1)} %get-tuple-element.66), channel_id=1, source_target_pairs={{0,6},{1,7},{2,4},{3,5},{4,2},{5,3},{6,0},{7,1},{8,14},{9,15},{10,... | collective-permute-start | bytes 516104 | tf_op jit(solution)/shard_map/ppermute | solution.py:373
  44.3 7.4 %collective-permute-start.9 = (bf16[32,2688]{1,0:T(8,128)(2,1)S(1)}, bf16[32,2688]{1,0:T(8,128)(2,1)S(1)}, u32[]{:S(2)}, u32[]{:S(2)}) collective-permute-start(bf16[32,2688]{1,0:T(8,128)(2,1)S(1)} %get-tuple-element.67), channel_id=1, source_target_pairs={{0,4},{1,5},{2,6},{3,7},{4,0},{5,1},{6,2},{7,3},{8,12},{9,13},{10,... | collective-permute-start | bytes 516104 | tf_op jit(solution)/shard_map/ppermute | solution.py:373
  44.8 7.8 %collective-permute-start.10 = (bf16[32,2688]{1,0:T(8,128)(2,1)S(1)}, bf16[32,2688]{1,0:T(8,128)(2,1)S(1)}, u32[]{:S(2)}, u32[]{:S(2)}) collective-permute-start(bf16[32,2688]{1,0:T(8,128)(2,1)S(1)} %get-tuple-element.68), channel_id=1, source_target_pairs={{0,2},{1,3},{2,0},{3,1},{4,6},{5,7},{6,4},{7,5},{8,10},{9,11},{10,... | collective-permute-start | bytes 516104 | tf_op jit(solution)/shard_map/ppermute | solution.py:373

commit v5 on v4

--- a/solution.py
+++ b/solution.py
@@ -244,12 +244,12 @@
     starts = [pl.multiple_of((2 * jnp.bitwise_xor(y, k) + side) * 32, 32) for k in (3, 2, 1, 0)]
     rows = jnp.concatenate([feat_ref[pl.ds(s, 32), :] for s in starts], axis=0)
     product = dot(rows, ow_ref[...]).astype(BF16)
-    first_ref[:, 0:DM] = product[0:64]
-    second_ref[:, 0:DM] = product[64:128]
+    first_ref[:, 0:DM] = product[0:32]
+    second_ref[:, 0:DM] = product[32:128]
     for i, s in enumerate(starts):
         high, low = split_two(square_ref[pl.ds(s, 32), :])
-        out_ref = first_ref if i < 2 else second_ref
-        out_ref[(i % 2) * 32 : (i % 2 + 1) * 32, DM:WIDE] = jnp.where(
+        out_ref, at = (first_ref, 0) if i == 0 else (second_ref, (i - 1) * 32)
+        out_ref[at : at + 32, DM:WIDE] = jnp.where(
             lane < 64, high.astype(F32), low.astype(F32)
         ).astype(BF16)
 
@@ -356,19 +356,19 @@
         local, *recvs[:4], *spans, qt, cum, weight, gate_values,
         flops=2 * 10**9, name="near",
     )
-    half = ((64, WIDE), BF16)
+    halves = [((32, WIDE), BF16), ((96, WIDE), BF16)]
     *theirs, feat, square = call(
         feature_kernel,
-        [half, half, ((TOK, WIDTH), BF16), ((TOK, 128), F32)],
+        [*halves, ((TOK, WIDTH), BF16), ((TOK, 128), F32)],
         near, lift, recvs[4], state_out, norm_gain[None, :], out_weight,
         flops=10**9, name="feature",
     )
-    mine = call(own_rows_kernel, [half, half], feat, square, out_weight, flops=10**9, name="own_rows")
+    mine = call(own_rows_kernel, halves, feat, square, out_weight, flops=10**9, name="own_rows")
     swap = [(g, g ^ 1) for g in range(8)]
     recv = [lax.ppermute(part, "head", swap) for part in theirs]
     one = ((32, WIDE), BF16)
-    send3, send2 = call(pair_kernel, [one, one], mine[0], recv[0], flops=10**6, name="pair")
-    send1, own = call(pair_kernel, [one, ((32, WIDE), F32)], mine[1], recv[1], flops=10**6, name="pair")
+    (send3,) = call(pair_kernel, [one], mine[0], recv[0], flops=10**6, name="pair")
+    send2, send1, own = call(pair_kernel, [one, one, ((32, WIDE), F32)], mine[1], recv[1], flops=10**6, name="pair")
     got = [
         lax.ppermute(send, "head", [(g, g ^ (2 * k)) for g in range(8)])
         for k, send in ((3, send3), (2, send2), (1, send1))

time: 53.7 us -> 54.8 us (1.020)
  waiting for transfers between devices: 18.5 us -> 19.2 us
  transfers between devices with their start and end apart: 11 -> 11, of which waited for: 7 -> 8; matrix products, arithmetic and copies ran while one was open for 0% -> 0% of each run, Pallas kernels for 9% -> 9%
where the time goes in v5:
time: 54.8 us; the launch traced here: 54.7 us
  starting transfers between devices  26.4 us (48%)
  waiting for transfers between devices  19.2 us (35%)
  Pallas kernels  8.35 us (15%)
  local copies, waits for them, and re-layouts  0.68 us (1%)
    pallas_call x11, Pallas kernels, call(): pl.pallas_call(kernel, out_shape=shapes, in_specs=specs, out_specs=[pl.Bl...  8.35 us
    ppermute x3, waiting for transfers between devices, on_device(): lax.ppermute(send, 'head', [(g, g ^ 2 * k) for g in range(8)])  7.57 us
    ppermute x2, starting transfers between devices, on_device(): recv = [lax.ppermute(part, 'head', swap) for part in theirs]  6.91 us
    ppermute x1, starting transfers between devices, on_device(): recvs.append(lax.ppermute(pay, 'seq', [(d, d ^ 28) for d in range(32)]))  4.58 us
    ppermute x1, starting transfers between devices, on_device(): recvs.append(lax.ppermute(pay, 'seq', [(d, d ^ 12) for d in range(32)]))  4.25 us
    ppermute x3, starting transfers between devices, on_device(): lax.ppermute(pay, 'seq', [(d, d ^ k) for d in range(32)])  4.06 us
    ppermute x3, starting transfers between devices, on_device(): lax.ppermute(send, 'head', [(g, g ^ 2 * k) for g in range(8)])  4.04 us
    ppermute x1, waiting for transfers between devices, on_device(): recvs.append(lax.ppermute(pay, 'seq', [(d, d ^ 12) for d in range(32)]))  2.89 us
  transfers between devices with their start and end apart: 11, of which 8 were waited for; matrix products, arithmetic and copies ran while one was open for 0% of the time, Pallas kernels for 9%

profile of v5, /device:TPU:1, one launch (start us, length us, event | category | flops | bytes accessed | tf_op | source)
XLA Modules:
  0.0 54.7 jit_solution(6264614212440798268)
XLA Ops:
  0.0 1.4 %state.1 = (bf16[672,128]{1,0:T(8,128)(2,1)S(1)}, f32[640,128]{1,0:T(8,128)S(1)}, bf16[640,256]{1,0:T(8,128)(2,1)S(1)}, f32[16,256]{1,0:T(8,128)S(1)}, f32[16,128]{1,0:T(8,128)S(1)}) custom-call(bf16[256,640]{1,0:T(8,128)(2,1)} %x_in.1, bf16[256,128]{1,0:T(8,128)(2,1)} %k_in.3, f32[10,256]{1,0:T(8,128)} %bitcast.6, f32[10,256]{1,0:T(8,128)} %bitcast.5), custom_call_target="tpu_custom_call" | custom-call | flops 100000000 | bytes 1000000 | tf_op jit(solution)/shard_map/state/pallas_call | solution.py:297
  1.4 3.4 %collective-permute-start = (bf16[672,128]{1,0:T(8,128)(2,1)S(1)}, bf16[672,128]{1,0:T(8,128)(2,1)S(1)}, u32[]{:S(2)}, u32[]{:S(2)}) collective-permute-start(bf16[672,128]{1,0:T(8,128)(2,1)S(1)} %get-tuple-element.39), channel_id=1, source_target_pairs={{0,24},{8,16},{16,8},{24,0},{32,56},{40,48},{48,40},{56,32},{64,88... | collective-permute-start | bytes 516104 | tf_op jit(solution)/shard_map/ppermute | solution.py:333
  4.8 0.5 collective-permute-start.1
  5.5 0.7 %copy-done.4 = f32[10]{0:T(128)S(1)} copy-done((f32[10]{0:T(128)S(1)}, f32[10]{0:T(128)}, u32[]{:S(2)}) %copy-start.4) | copy-done | bytes 64
  6.1 3.0 %local.1 = (f32[640,256]{1,0:T(8,128)S(1)}, bf16[128,256]{1,0:T(8,128)(2,1)S(1)}) custom-call(bf16[640,256]{1,0:T(8,128)(2,1)S(1)} %get-tuple-element.36.xt_ref, f32[16,256]{1,0:T(8,128)S(1)} %get-tuple-element.37.cum_ref, f32[10]{0:T(128)S(1)} %copy-done.4, bf16[256,128]{1,0:T(8,128)(2,1)} %k_in.3, bf16[256,128]{1,0:T(8,128)(2,1)} %q_ref.1, ...), custom_call_target="tpu_custom_call" | custom-call | flops 5000000000 | bytes 50000000 | tf_op jit(solution)/shard_map/local/pallas_call | solution.py:297
  9.2 2.9 %collective-permute-done.r3 = bf16[672,128]{1,0:T(8,128)(2,1)S(1)} collective-permute-done((bf16[672,128]{1,0:T(8,128)(2,1)S(1)}, bf16[672,128]{1,0:T(8,128)(2,1)S(1)}, u32[]{:S(2)}, u32[]{:S(2)}) %collective-permute-start) | collective-permute-done | bytes 172064 | tf_op jit(solution)/shard_map/ppermute | solution.py:333
  12.2 2.5 %collective-permute-start.3 = (bf16[672,128]{1,0:T(8,128)(2,1)S(1)}, bf16[672,128]{1,0:T(8,128)(2,1)S(1)}, u32[]{:S(2)}, u32[]{:S(2)}) collective-permute-start(bf16[672,128]{1,0:T(8,128)(2,1)S(1)} %get-tuple-element.44), channel_id=1, source_target_pairs={{0,32},{8,40},{16,48},{24,56},{32,0},{40,8},{48,16},{56,24},{64,96... | collective-permute-start | bytes 516104 | tf_op jit(solution)/shard_map/ppermute | solution.py:340
  14.7 2.8 %collective-permute-done.3.refs_3_.r2 = bf16[672,128]{1,0:T(8,128)(2,1)S(1)} collective-permute-done((bf16[672,128]{1,0:T(8,128)(2,1)S(1)}, bf16[672,128]{1,0:T(8,128)(2,1)S(1)}, u32[]{:S(2)}, u32[]{:S(2)}) %collective-permute-start.3) | collective-permute-done | bytes 172064 | tf_op jit(solution)/shard_map/ppermute | solution.py:340
  17.6 4.3 %collective-permute-start.4 = (bf16[672,128]{1,0:T(8,128)(2,1)S(1)}, bf16[672,128]{1,0:T(8,128)(2,1)S(1)}, u32[]{:S(2)}, u32[]{:S(2)}) collective-permute-start(bf16[672,128]{1,0:T(8,128)(2,1)S(1)} %get-tuple-element.48), channel_id=1, source_target_pairs={{0,96},{8,104},{16,112},{24,120},{32,64},{40,72},{48,80},{56,88},{... | collective-permute-start | bytes 516104 | tf_op jit(solution)/shard_map/ppermute | solution.py:347
  21.9 2.9 %collective-permute-done.4.recv_ref.r3 = bf16[672,128]{1,0:T(8,128)(2,1)S(1)} collective-permute-done((bf16[672,128]{1,0:T(8,128)(2,1)S(1)}, bf16[672,128]{1,0:T(8,128)(2,1)S(1)}, u32[]{:S(2)}, u32[]{:S(2)}) %collective-permute-start.4) | collective-permute-done | bytes 172064 | tf_op jit(solution)/shard_map/ppermute | solution.py:347
  24.8 4.6 %collective-permute-start.5 = (bf16[640,128]{1,0:T(8,128)(2,1)S(1)}, bf16[640,128]{1,0:T(8,128)(2,1)S(1)}, u32[]{:S(2)}, u32[]{:S(2)}) collective-permute-start(bf16[640,128]{1,0:T(8,128)(2,1)S(1)} %get-tuple-element.57), channel_id=1, source_target_pairs={{0,224},{8,232},{16,240},{24,248},{32,192},{40,200},{48,208},{56,2... | collective-permute-start | bytes 491528 | tf_op jit(solution)/shard_map/ppermute | solution.py:353
  29.4 0.7 %near.1 = (f32[256,640]{1,0:T(8,128)S(1)}, f32[256,640]{1,0:T(8,128)S(1)}) custom-call(f32[640,256]{1,0:T(8,128)S(1)} %get-tuple-element.38._.local_ref, bf16[640,128]{1,0:T(8,128)(2,1)S(1)} %get-tuple-element.42.r0, bf16[640,128]{1,0:T(8,128)(2,1)S(1)} %get-tuple-element.43.r1, bf16[672,128]{1,0:T(8,128)(2,1)S(1)} %collective-permute-done.3.refs_3_.r2, ...), custom_call_target="tpu_custom_call" | custom-call | flops 2000000000 | bytes 20000000 | tf_op jit(solution)/shard_map/near/pallas_call | solution.py:297
  30.1 2.1 %collective-permute-done.5.recv_ref = bf16[640,128]{1,0:T(8,128)(2,1)S(1)} collective-permute-done((bf16[640,128]{1,0:T(8,128)(2,1)S(1)}, bf16[640,128]{1,0:T(8,128)(2,1)S(1)}, u32[]{:S(2)}, u32[]{:S(2)}) %collective-permute-start.5) | collective-permute-done | bytes 163872 | tf_op jit(solution)/shard_map/ppermute | solution.py:353
  32.2 1.0 %feature.1 = (bf16[32,2688]{1,0:T(8,128)(2,1)S(1)}, bf16[96,2688]{1,0:T(8,128)(2,1)S(1)}, bf16[256,640]{1,0:T(8,128)(2,1)S(1)}, f32[256,128]{1,0:T(8,128)S(1)}) custom-call(f32[256,640]{1,0:T(8,128)S(1)} %get-tuple-element.55.near_ref, f32[256,640]{1,0:T(8,128)S(1)} %get-tuple-element.56.lift_ref, bf16[640,128]{1,0:T(8,128)(2,1)S(1)} %collective-permute-done.5.recv_ref, ...), custom_call_target="tpu_custom_call" | custom-call | flops 1000000000 | bytes 10000000 | tf_op jit(solution)/shard_map/feature/pallas_call | solution.py:297
  33.2 6.8 %collective-permute-start.6 = (bf16[96,2688]{1,0:T(8,128)(2,1)S(1)}, bf16[96,2688]{1,0:T(8,128)(2,1)S(1)}, u32[]{:S(2)}, u32[]{:S(2)}) collective-permute-start(bf16[96,2688]{1,0:T(8,128)(2,1)S(1)} %get-tuple-element.61), channel_id=1, source_target_pairs={{0,1},{1,0},{2,3},{3,2},{4,5},{5,4},{6,7},{7,6},{8,9},{9,8},{10,11... | collective-permute-start | bytes 1548296 | tf_op jit(solution)/shard_map/ppermute | solution.py:368
  40.1 0.7 %own_rows.1 = (bf16[32,2688]{1,0:T(8,128)(2,1)S(1)}, bf16[96,2688]{1,0:T(8,128)(2,1)S(1)}) custom-call(bf16[256,640]{1,0:T(8,128)(2,1)S(1)} %get-tuple-element.58.feat_ref, f32[256,128]{1,0:T(8,128)S(1)} %get-tuple-element.59.square_ref, bf16[640,2560]{1,0:T(8,128)(2,1)S(1)} %copy-done), custom_call_target="tpu_custom_call" | custom-call | flops 1000000000 | bytes 10000000 | tf_op jit(solution)/shard_map/own_rows/pallas_call | solution.py:297
  40.8 1.0 %collective-permute-done.7.recv_ref = bf16[32,2688]{1,0:T(8,128)(2,1)S(1)} collective-permute-done((bf16[32,2688]{1,0:T(8,128)(2,1)S(1)}, bf16[32,2688]{1,0:T(8,128)(2,1)S(1)}, u32[]{:S(2)}, u32[]{:S(2)}) %collective-permute-start.7) | collective-permute-done | bytes 172064 | tf_op jit(solution)/shard_map/ppermute | solution.py:368
  42.0 2.8 %collective-permute-start.8 = (bf16[32,2688]{1,0:T(8,128)(2,1)S(1)}, bf16[32,2688]{1,0:T(8,128)(2,1)S(1)}, u32[]{:S(2)}, u32[]{:S(2)}) collective-permute-start(bf16[32,2688]{1,0:T(8,128)(2,1)S(1)} %pair.3), channel_id=1, source_target_pairs={{0,6},{1,7},{2,4},{3,5},{4,2},{5,3},{6,0},{7,1},{8,14},{9,15},{10,... | collective-permute-start | bytes 516104 | tf_op jit(solution)/shard_map/ppermute | solution.py:373
  44.7 0.2 pair.2
  45.1 1.2 %collective-permute-start.9 = (bf16[32,2688]{1,0:T(8,128)(2,1)S(1)}, bf16[32,2688]{1,0:T(8,128)(2,1)S(1)}, u32[]{:S(2)}, u32[]{:S(2)}) collective-permute-start(bf16[32,2688]{1,0:T(8,128)(2,1)S(1)} %get-tuple-element.65), channel_id=1, source_target_pairs={{0,4},{1,5},{2,6},{3,7},{4,0},{5,1},{6,2},{7,3},{8,12},{9,13},{10,... | collective-permute-start | bytes 516104 | tf_op jit(solution)/shard_map/ppermute | solution.py:373
  46.3 2.6 %collective-permute-done.8.r1 = bf16[32,2688]{1,0:T(8,128)(2,1)S(1)} collective-permute-done((bf16[32,2688]{1,0:T(8,128)(2,1)S(1)}, bf16[32,2688]{1,0:T(8,128)(2,1)S(1)}, u32[]{:S(2)}, u32[]{:S(2)}) %collective-permute-start.8) | collective-permute-done | bytes 172064 | tf_op jit(solution)/shard_map/ppermute | solution.py:373
  48.9 1.5 %collective-permute-done.10.r3 = bf16[32,2688]{1,0:T(8,128)(2,1)S(1)} collective-permute-done((bf16[32,2688]{1,0:T(8,128)(2,1)S(1)}, bf16[32,2688]{1,0:T(8,128)(2,1)S(1)}, u32[]{:S(2)}, u32[]{:S(2)}) %collective-permute-start.10) | collective-permute-done | bytes 172064 | tf_op jit(solution)/shard_map/ppermute | solution.py:373
  50.3 3.5 %collective-permute-done.9.r2 = bf16[32,2688]{1,0:T(8,128)(2,1)S(1)} collective-permute-done((bf16[32,2688]{1,0:T(8,128)(2,1)S(1)}, bf16[32,2688]{1,0:T(8,128)(2,1)S(1)}, u32[]{:S(2)}, u32[]{:S(2)}) %collective-permute-start.9) | collective-permute-done | bytes 172064 | tf_op jit(solution)/shard_map/ppermute | solution.py:373
  53.8 0.8 %final.1 = bf16[32,2560]{1,0:T(8,128)(2,1)} custom-call(f32[32,2688]{1,0:T(8,128)S(1)} %get-tuple-element.62.own_ref, bf16[32,2688]{1,0:T(8,128)(2,1)S(1)} %collective-permute-done.8.r1, bf16[32,2688]{1,0:T(8,128)(2,1)S(1)} %collective-permute-done.9.r2, bf16[32,2688]{1,0:T(8,128)(2,1)S(1)} %collective-permute-done.10.r3), custom_call_target="tpu_custom_call" | custom-call | flops 1000000 | bytes 10000 | tf_op jit(solution)/shard_map/final/pallas_call | solution.py:297
  (23 shorter events, 0.9 us)
Async XLA Ops:
  1.4 10.6 %collective-permute-start = (bf16[672,128]{1,0:T(8,128)(2,1)S(1)}, bf16[672,128]{1,0:T(8,128)(2,1)S(1)}, u32[]{:S(2)}, u32[]{:S(2)}) collective-permute-start(bf16[672,128]{1,0:T(8,128)(2,1)S(1)} %get-tuple-element.39), channel_id=1, source_target_pairs={{0,24},{8,16},{16,8},{24,0},{32,56},{40,48},{48,40},{56,32},{64,88... | collective-permute-start | bytes 516104 | tf_op jit(solution)/shard_map/ppermute | solution.py:333
  4.8 7.2 %collective-permute-start.1 = (bf16[672,128]{1,0:T(8,128)(2,1)S(1)}, bf16[672,128]{1,0:T(8,128)(2,1)S(1)}, u32[]{:S(2)}, u32[]{:S(2)}) collective-permute-start(bf16[672,128]{1,0:T(8,128)(2,1)S(1)} %get-tuple-element.39), channel_id=1, source_target_pairs={{0,16},{8,24},{16,0},{24,8},{32,48},{40,56},{48,32},{56,40},{64,80... | collective-permute-start | bytes 516104 | tf_op jit(solution)/shard_map/ppermute | solution.py:333
  5.3 6.7 %collective-permute-start.2 = (bf16[672,128]{1,0:T(8,128)(2,1)S(1)}, bf16[672,128]{1,0:T(8,128)(2,1)S(1)}, u32[]{:S(2)}, u32[]{:S(2)}) collective-permute-start(bf16[672,128]{1,0:T(8,128)(2,1)S(1)} %get-tuple-element.39), channel_id=1, source_target_pairs={{0,8},{8,0},{16,24},{24,16},{32,40},{40,32},{48,56},{56,48},{64,72... | collective-permute-start | bytes 516104 | tf_op jit(solution)/shard_map/ppermute | solution.py:333
  5.5 0.7 %copy-start.4 = (f32[10]{0:T(128)S(1)}, f32[10]{0:T(128)}, u32[]{:S(2)}) copy-start(f32[10]{0:T(128)} %skip_ref.1) | copy-start | bytes 124
  6.1 15.7 %copy-start.5 = (f32[640]{0:T(1024)S(1)}, f32[640]{0:T(1024)}, u32[]{:S(2)}) copy-start(f32[640]{0:T(1024)} %param.18) | copy-start | bytes 7684
  6.1 23.3 %copy-start.2 = (bf16[256,640]{1,0:T(8,128)(2,1)S(1)}, bf16[256,640]{1,0:T(8,128)(2,1)}, u32[]{:S(2)}) copy-start(bf16[256,640]{1,0:T(8,128)(2,1)} %gate_ref.1) | copy-start | bytes 983044
  6.1 23.3 %copy-start.3 = (bf16[256,10,14]{0,2,1:T(8,128)(2,1)S(1)}, bf16[256,10,14]{0,2,1:T(8,128)(2,1)}, u32[]{:S(2)}) copy-start(bf16[256,10,14]{0,2,1:T(8,128)(2,1)} %param.16) | copy-start | bytes 215044
  12.2 5.3 %collective-permute-start.3 = (bf16[672,128]{1,0:T(8,128)(2,1)S(1)}, bf16[672,128]{1,0:T(8,128)(2,1)S(1)}, u32[]{:S(2)}, u32[]{:S(2)}) collective-permute-start(bf16[672,128]{1,0:T(8,128)(2,1)S(1)} %get-tuple-element.44), channel_id=1, source_target_pairs={{0,32},{8,40},{16,48},{24,56},{32,0},{40,8},{48,16},{56,24},{64,96... | collective-permute-start | bytes 516104 | tf_op jit(solution)/shard_map/ppermute | solution.py:340
  17.6 7.2 %collective-permute-start.4 = (bf16[672,128]{1,0:T(8,128)(2,1)S(1)}, bf16[672,128]{1,0:T(8,128)(2,1)S(1)}, u32[]{:S(2)}, u32[]{:S(2)}) collective-permute-start(bf16[672,128]{1,0:T(8,128)(2,1)S(1)} %get-tuple-element.48), channel_id=1, source_target_pairs={{0,96},{8,104},{16,112},{24,120},{32,64},{40,72},{48,80},{56,88},{... | collective-permute-start | bytes 516104 | tf_op jit(solution)/shard_map/ppermute | solution.py:347
  24.8 7.4 %collective-permute-start.5 = (bf16[640,128]{1,0:T(8,128)(2,1)S(1)}, bf16[640,128]{1,0:T(8,128)(2,1)S(1)}, u32[]{:S(2)}, u32[]{:S(2)}) collective-permute-start(bf16[640,128]{1,0:T(8,128)(2,1)S(1)} %get-tuple-element.57), channel_id=1, source_target_pairs={{0,224},{8,232},{16,240},{24,248},{32,192},{40,200},{48,208},{56,2... | collective-permute-start | bytes 491528 | tf_op jit(solution)/shard_map/ppermute | solution.py:353
  29.4 2.8 %copy-start = (bf16[640,2560]{1,0:T(8,128)(2,1)S(1)}, bf16[640,2560]{1,0:T(8,128)(2,1)}, u32[]{:S(2)}) copy-start(bf16[640,2560]{1,0:T(8,128)(2,1)} %ow_ref.3) | copy-start | bytes 9830404
  29.4 2.8 %copy-start.1 = (bf16[256,128]{1,0:T(8,128)(2,1)S(1)}, bf16[256,128]{1,0:T(8,128)(2,1)}, u32[]{:S(2)}) copy-start(bf16[256,128]{1,0:T(8,128)(2,1)} %q_ref.1) | copy-start | bytes 196612
  33.2 11.5 %collective-permute-start.6 = (bf16[96,2688]{1,0:T(8,128)(2,1)S(1)}, bf16[96,2688]{1,0:T(8,128)(2,1)S(1)}, u32[]{:S(2)}, u32[]{:S(2)}) collective-permute-start(bf16[96,2688]{1,0:T(8,128)(2,1)S(1)} %get-tuple-element.61), channel_id=1, source_target_pairs={{0,1},{1,0},{2,3},{3,2},{4,5},{5,4},{6,7},{7,6},{8,9},{9,8},{10,11... | collective-permute-start | bytes 1548296 | tf_op jit(solution)/shard_map/ppermute | solution.py:368
  40.0 1.8 %collective-permute-start.7 = (bf16[32,2688]{1,0:T(8,128)(2,1)S(1)}, bf16[32,2688]{1,0:T(8,128)(2,1)S(1)}, u32[]{:S(2)}, u32[]{:S(2)}) collective-permute-start(bf16[32,2688]{1,0:T(8,128)(2,1)S(1)} %get-tuple-element.64), channel_id=1, source_target_pairs={{0,1},{1,0},{2,3},{3,2},{4,5},{5,4},{6,7},{7,6},{8,9},{9,8},{10,11... | collective-permute-start | bytes 516104 | tf_op jit(solution)/shard_map/ppermute | solution.py:368
  42.0 6.9 %collective-permute-start.8 = (bf16[32,2688]{1,0:T(8,128)(2,1)S(1)}, bf16[32,2688]{1,0:T(8,128)(2,1)S(1)}, u32[]{:S(2)}, u32[]{:S(2)}) collective-permute-start(bf16[32,2688]{1,0:T(8,128)(2,1)S(1)} %pair.3), channel_id=1, source_target_pairs={{0,6},{1,7},{2,4},{3,5},{4,2},{5,3},{6,0},{7,1},{8,14},{9,15},{10,... | collective-permute-start | bytes 516104 | tf_op jit(solution)/shard_map/ppermute | solution.py:373
  45.0 5.4 %collective-permute-start.10 = (bf16[32,2688]{1,0:T(8,128)(2,1)S(1)}, bf16[32,2688]{1,0:T(8,128)(2,1)S(1)}, u32[]{:S(2)}, u32[]{:S(2)}) collective-permute-start(bf16[32,2688]{1,0:T(8,128)(2,1)S(1)} %get-tuple-element.66), channel_id=1, source_target_pairs={{0,2},{1,3},{2,0},{3,1},{4,6},{5,7},{6,4},{7,5},{8,10},{9,11},{10,... | collective-permute-start | bytes 516104 | tf_op jit(solution)/shard_map/ppermute | solution.py:373
  45.1 8.8 %collective-permute-start.9 = (bf16[32,2688]{1,0:T(8,128)(2,1)S(1)}, bf16[32,2688]{1,0:T(8,128)(2,1)S(1)}, u32[]{:S(2)}, u32[]{:S(2)}) collective-permute-start(bf16[32,2688]{1,0:T(8,128)(2,1)S(1)} %get-tuple-element.65), channel_id=1, source_target_pairs={{0,4},{1,5},{2,6},{3,7},{4,0},{5,1},{6,2},{7,3},{8,12},{9,13},{10,... | collective-permute-start | bytes 516104 | tf_op jit(solution)/shard_map/ppermute | solution.py:373
